TPU v7x, 1024 devices: a whole 4x8x16 slice. The times are simulated.
1024 devices in a mesh: gx: 128 (over y_hi, z, core), gz: 8 (over x, y_lo).
Axes of the slice: x: 4, y: 8 (y_hi: 4, y_lo: 2; y = y_hi * 2 + y_lo), z: 16, core: 2. Of those that a mesh axis runs over, the one named last changes fastest.
Arguments:
- state: float32 [256, 16, 5, 12, 216], P('gx', 'gz'), as said below
- register: float32 [256, 16, 5, 12, 216], P('gx', 'gz'), may hold values from -6 to 6
- heights: float32 [12], replicated, may hold values from 0.05 to 0.3
- solid_wall_mask: int32 [256, 16, 11], P('gx', 'gz'), may hold values 0 or 1
Outputs:
- state_next: float32 [256, 16, 5, 12, 216], P('gx', 'gz')
- register_next: float32 [256, 16, 5, 12, 216], P('gx', 'gz')
Inputs may be any that keep to these rules, and one draw needn't show every extreme that they name: `state`: at every node the density lies in [0.5, 1.6], each velocity component in [-1.8, 1.8] and the pressure 0.4 (E - |m|^2 / (2 rho)) in [0.4, 2.0].
All inputs are finite; a program needn't handle non-finite values. No bound on the sum of `solid_wall_mask` on one device may be relied on, other than what follows from the above.
Results may differ from a plain program's by a relative error of at most 0.0003.
Values sent between devices are 32-bit elements; how exact they have to be, the bound alone decides.
No kernel may reach another device: no remote copies, remote signals or barrier semaphores. Data moves between devices by JAX's collectives and lax.ppermute only.
A program may use at most 64 MiB of HBM per device.

v0:
```python
import math

import jax
import jax.numpy as jnp
import numpy as np
from jax import lax
from jax.sharding import PartitionSpec as P

GAMMA = 1.4
VISCOSITY = 0.001
CONDUCT = 0.001 * 1.4 / (0.4 * 0.72)
LENGTH_X = 0.2
LENGTH_Z = 0.15
TIME_STEP = 0.004
SECTION_A = -0.4178904745
SECTION_B = 0.3792103129


def padded_2(value, sides, width):
    edges = {}
    for axis, dim in sides:
        size, length = (lax.axis_size(axis), value.shape[dim])
        up = [(i, (i + 1) % size) for i in range(size)]
        last = lax.slice_in_dim(value, length - width, length, axis=dim)
        initial = lax.slice_in_dim(value, 0, width, axis=dim)
        edges[dim] = (
            lax.ppermute(last, axis, up),
            lax.ppermute(initial, axis, [(b, a) for a, b in up]),
        )
    done = []
    for _, dim in sides:
        low, high = edges[dim]
        around = [(width, width) if d in done else (0, 0) for d in range(value.ndim)]
        value = jnp.concatenate([jnp.pad(low, around), value, jnp.pad(high, around)], axis=dim)
        done.append(dim)
    return value


def node_tables():
    root = math.sqrt(7.0)
    outer = math.sqrt(1.0 / 3.0 + 2.0 * root / 21.0)
    inner = math.sqrt(1.0 / 3.0 - 2.0 * root / 21.0)
    points = np.array([-1.0, -outer, -inner, inner, outer, 1.0])
    weights = np.array(
        [
            1.0 / 15.0,
            (14.0 - root) / 30.0,
            (14.0 + root) / 30.0,
            (14.0 + root) / 30.0,
            (14.0 - root) / 30.0,
            1.0 / 15.0,
        ]
    )
    barycen = np.array(
        [
            1.0
            / np.prod([points[source] - points[target] for target in range(6) if target != source])
            for source in range(6)
        ]
    )
    matrix = np.zeros((6, 6))
    for source in range(6):
        for target in range(6):
            if target != source:
                matrix[source, target] = (
                    barycen[target] / barycen[source] / (points[source] - points[target])
                )
        matrix[source, source] = -np.sum(matrix[source])
    return (matrix, weights)


def contract(field, table):
    flat = field.reshape((-1, field.shape[-1]))
    result = jnp.dot(
        flat, table, precision=lax.Precision.HIGHEST, preferred_element_type=jnp.float32
    )
    return result.reshape(field.shape[:-1] + (table.shape[1],))


def deriv_table(matrix, direction):
    eye_six = np.eye(6)
    if direction == 0:
        full = np.kron(matrix, np.eye(36))
    elif direction == 1:
        full = np.kron(eye_six, np.kron(matrix, eye_six))
    else:
        full = np.kron(np.eye(36), matrix)
    return jnp.asarray(full.T, jnp.float32)


def face_table(direction, side):
    nodes = np.arange(216)
    position = [nodes // 36, nodes // 6 % 6, nodes % 6][direction]
    chosen = nodes[position == side]
    table = np.zeros((216, 36))
    table[chosen, np.arange(36)] = 1.0
    return table


def apply_deriv(field, direction, matrix):
    return contract(field, deriv_table(matrix, direction))


def primitives(state):
    density = state[:, :, 0]
    velocity = state[:, :, 1:4] / density[:, :, None]
    pressure = (GAMMA - 1.0) * (state[:, :, 4] - 0.5 * jnp.sum(state[:, :, 1:4] * velocity, axis=2))
    return (density, velocity, pressure)


def phys_flux(state, direction):
    density, velocity, pressure = primitives(state)
    normal_vector = velocity[:, :, direction]
    unit = jnp.asarray(np.eye(3)[direction], jnp.float32).reshape(1, 1, 3, 1, 1)
    momentum = state[:, :, 1:4] * normal_vector[:, :, None] + pressure[:, :, None] * unit
    energy = (state[:, :, 4] + pressure) * normal_vector
    return jnp.concatenate(
        [state[:, :, direction + 1 : direction + 2], momentum, energy[:, :, None]], axis=2
    )


def rusanov(lower, upper, direction):
    rho_lo, vel_lo, pres_lo = primitives(lower)
    rho_hi, vel_hi, pres_hi = primitives(upper)
    speed = jnp.maximum(
        jnp.abs(vel_lo[:, :, direction]) + jnp.sqrt(GAMMA * pres_lo / rho_lo),
        jnp.abs(vel_hi[:, :, direction]) + jnp.sqrt(GAMMA * pres_hi / rho_hi),
    )
    return 0.5 * (phys_flux(lower, direction) + phys_flux(upper, direction)) - 0.5 * speed[
        :, :, None
    ] * (upper - lower)


def mirror(state):
    return jnp.concatenate([state[:, :, 0:1], -state[:, :, 1:4], state[:, :, 4:5]], axis=2)


def split_volume(state, direction, matrix):
    density, velocity, pressure = primitives(state)
    specific = state[:, :, 4] / density
    normal = velocity[:, :, direction]
    others = [velocity[:, :, 0], velocity[:, :, 1], velocity[:, :, 2], specific]
    fields = [density, normal, pressure, density * normal, pressure * normal]
    for other in others:
        fields = fields + [other, normal * other, density * other, density * normal * other]
    derived = apply_deriv(jnp.stack(fields, axis=0), direction, matrix)
    d_rho, d_norm, d_pres, d_mass, d_work = (
        derived[0],
        derived[1],
        derived[2],
        derived[3],
        derived[4],
    )

    def triple(member):
        base = 5 + 4 * member
        other = others[member]
        return 0.25 * (
            derived[base + 3]
            + density * derived[base + 1]
            + normal * derived[base + 2]
            + other * d_mass
            + density * normal * derived[base]
            + density * other * d_norm
            + normal * other * d_rho
        )

    parts = [0.5 * (density * d_norm + normal * d_rho + d_mass)]
    for member in range(3):
        value = triple(member)
        if member == direction:
            value = value + d_pres
        parts.append(value)
    parts.append(triple(3) + 0.5 * (pressure * d_norm + normal * d_pres + d_work))
    return jnp.stack(parts, axis=2)


def face(field, direction, side):
    return contract(field, jnp.asarray(face_table(direction, side), jnp.float32))


def embed(lower, upper, direction):
    low_table = jnp.asarray(face_table(direction, 0).T, jnp.float32)
    high_table = jnp.asarray(face_table(direction, 5).T, jnp.float32)
    return contract(lower, low_table) + contract(upper, high_table)


def lateral(xfield, zfield):
    return jnp.concatenate(
        [face(xfield, 0, 0), face(xfield, 0, 5), face(zfield, 2, 0), face(zfield, 2, 5)], axis=-1
    )


def cross(padded):
    return (
        padded[:-2, 1:-1, ..., 36:72],
        padded[2:, 1:-1, ..., 0:36],
        padded[1:-1, :-2, ..., 108:144],
        padded[1:-1, 2:, ..., 72:108],
    )


def walls(flags):
    solid = flags == 1
    edge = jnp.ones(flags.shape[:2] + (1,), dtype=bool)
    wall_low = jnp.concatenate([edge, solid], axis=2)
    wall_high = jnp.concatenate([solid, edge], axis=2)
    return (wall_low[:, :, None, :, None], wall_high[:, :, None, :, None])


def y_neighbours(bottom, top):
    below = jnp.concatenate([bottom[:, :, :, :1], top[:, :, :, :-1]], axis=3)
    above = jnp.concatenate([bottom[:, :, :, 1:], top[:, :, :, -1:]], axis=3)
    return (below, above)


def to_prim(trace):
    density, velocity, pressure = primitives(trace)
    return jnp.concatenate([velocity, (pressure / density)[:, :, None]], axis=2)


def lift(state, flags, heights, neighbours, matrix, weights):
    prim = to_prim(state)
    wall_low, wall_high = walls(flags)
    flip = jnp.asarray([-1.0, -1.0, -1.0, 1.0], jnp.float32).reshape(1, 1, 4, 1, 1)
    grads = []
    for direction in range(3):
        own_lo = face(prim, direction, 0)
        own_hi = face(prim, direction, 5)
        if direction == 0:
            out_lo, out_hi, scale = (to_prim(neighbours[0]), to_prim(neighbours[1]), 2.0 / LENGTH_X)
        elif direction == 2:
            out_lo, out_hi, scale = (to_prim(neighbours[2]), to_prim(neighbours[3]), 2.0 / LENGTH_Z)
        else:
            below, above = y_neighbours(own_lo, own_hi)
            out_lo = jnp.where(wall_low, own_lo * flip, below)
            out_hi = jnp.where(wall_high, own_hi * flip, above)
            scale = (2.0 / heights).reshape(1, 1, 1, -1, 1)
        surface = embed(
            -0.5 * (out_lo - own_lo) / weights[0], 0.5 * (out_hi - own_hi) / weights[5], direction
        )
        grads.append(scale * (apply_deriv(prim, direction, matrix) + surface))
    return (prim, grads)


def viscous(prim, grads):
    spread = grads[0][:, :, 0] + grads[1][:, :, 1] + grads[2][:, :, 2]
    fluxes = []
    for direction in range(3):
        stress = []
        for member in range(3):
            value = VISCOSITY * (grads[direction][:, :, member] + grads[member][:, :, direction])
            if member == direction:
                value = value - 2.0 / 3.0 * VISCOSITY * spread
            stress.append(value)
        energy = prim[:, :, 0] * stress[0] + prim[:, :, 1] * stress[1] + prim[:, :, 2] * stress[2]
        energy = energy + CONDUCT * grads[direction][:, :, 3]
        fluxes.append(jnp.stack(stress + [energy], axis=2))
    return fluxes


def tendency(state, flags, heights, neighbours, fluxes, visc_nbrs, matrix, weights):
    wall_low, wall_high = walls(flags)
    total = jnp.zeros_like(state)
    for direction in range(3):
        own_lo = face(state, direction, 0)
        own_hi = face(state, direction, 5)
        visc_lo = face(fluxes[direction], direction, 0)
        visc_hi = face(fluxes[direction], direction, 5)
        if direction == 1:
            below, above = y_neighbours(own_lo, own_hi)
            star_lo = rusanov(jnp.where(wall_low, mirror(own_lo), below), own_lo, 1)
            star_hi = rusanov(own_hi, jnp.where(wall_high, mirror(own_hi), above), 1)
            vbelow, vabove = y_neighbours(visc_lo, visc_hi)
            vstar_lo = jnp.where(wall_low, visc_lo, 0.5 * (vbelow + visc_lo))
            vstar_hi = jnp.where(wall_high, visc_hi, 0.5 * (vabove + visc_hi))
            scale = (2.0 / heights).reshape(1, 1, 1, -1, 1)
        else:
            slot = 0 if direction == 0 else 2
            star_lo = rusanov(neighbours[slot], own_lo, direction)
            star_hi = rusanov(own_hi, neighbours[slot + 1], direction)
            vstar_lo = 0.5 * (visc_nbrs[slot] + visc_lo)
            vstar_hi = 0.5 * (visc_nbrs[slot + 1] + visc_hi)
            scale = 2.0 / LENGTH_X if direction == 0 else 2.0 / LENGTH_Z
        inv_surface = embed(
            -(star_lo - phys_flux(own_lo, direction)) / weights[0],
            (star_hi - phys_flux(own_hi, direction)) / weights[5],
            direction,
        )
        visc_surface = embed(
            -(vstar_lo - visc_lo) / weights[0], (vstar_hi - visc_hi) / weights[5], direction
        )
        visc_all = apply_deriv(fluxes[direction], direction, matrix) + visc_surface
        visc_all = jnp.concatenate([jnp.zeros_like(visc_all[:, :, :1]), visc_all], axis=2)
        total = total + scale * (visc_all - split_volume(state, direction, matrix) - inv_surface)
    return total


def shards(state, register, heights, solid_wall_mask):
    matrix, weights = node_tables()
    padded = padded_2(lateral(state, state), (("gx", 0), ("gz", 1)), 1)
    neighbours = cross(padded)
    prim, grads = lift(state, solid_wall_mask, heights, neighbours, matrix, weights)
    fluxes = viscous(prim, grads)
    visc_pad = padded_2(lateral(fluxes[0], fluxes[2]), (("gx", 0), ("gz", 1)), 1)
    visc_nbrs = cross(visc_pad)
    rhs = tendency(state, solid_wall_mask, heights, neighbours, fluxes, visc_nbrs, matrix, weights)
    register_next = SECTION_A * register + TIME_STEP * rhs
    return (state + SECTION_B * register_next, register_next)


def solution(mesh):
    in_specs = (
        P("gx", "gz", None, None, None),
        P("gx", "gz", None, None, None),
        P(),
        P("gx", "gz", None),
    )
    out_specs = (P("gx", "gz", None, None, None), P("gx", "gz", None, None, None))
    return jax.shard_map(shards, mesh=mesh, in_specs=in_specs, out_specs=out_specs, check_vma=False)
```

profile of v0, /device:TPU:14, one launch (start us, length us, event | category | flops | bytes accessed | tf_op | source)
XLA Modules:
  0.0 212.0 jit_solution(16593155693130331720)
XLA Ops:
  0.7 1.4 convolution_bitcast_fusion.2
  2.1 1.4 convolution_bitcast_fusion.3
  3.5 1.4 convolution_bitcast_fusion.5
  6.4 1.9 collective-permute-start
  8.3 20.5 %collective-permute-start.1 = (f32[1,2,5,12,144]{4,3,1,0,2:T(8,128)}, f32[1,2,5,12,144]{4,3,1,0,2:T(8,128)S(1)}, u32[]{:S(2)}, u32[]{:S(2)}) collective-permute-start(f32[1,2,5,12,144]{4,3,1,0,2:T(8,128)} %get-tuple-element.153), channel_id=1, source_target_pairs={{8,0},{16,8},{24,16},{32,24},{40,32},{48,40},{56,48},{64,56},{72,6... | collective-permute-start | bytes 207368 | tf_op jit(solution)/shard_map/ppermute | solution.py:28
  29.5 3.2 %collective-permute-start.2 = (f32[2,1,5,12,144]{4,3,1,0,2:T(8,128)}, f32[2,1,5,12,144]{4,3,1,0,2:T(8,128)}, u32[]{:S(2)}, u32[]{:S(2)}) collective-permute-start(f32[2,1,5,12,144]{4,3,1,0,2:T(8,128)} %get-tuple-element.152), channel_id=1, source_target_pairs={{0,1},{1,2},{2,3},{3,4},{4,5},{5,6},{6,7},{7,0},{8,9},{9,10},{10,1... | collective-permute-start | bytes 207368 | tf_op jit(solution)/shard_map/ppermute | solution.py:27
  32.7 2.7 %collective-permute-start.3 = (f32[2,1,5,12,144]{4,3,1,0,2:T(8,128)}, f32[2,1,5,12,144]{4,3,1,0,2:T(8,128)}, u32[]{:S(2)}, u32[]{:S(2)}) collective-permute-start(f32[2,1,5,12,144]{4,3,1,0,2:T(8,128)} %get-tuple-element.151), channel_id=1, source_target_pairs={{1,0},{2,1},{3,2},{4,3},{5,4},{6,5},{7,6},{0,7},{9,8},{10,9},{11,1... | collective-permute-start | bytes 207368 | tf_op jit(solution)/shard_map/ppermute | solution.py:28
  38.9 2.4 %reshape.1151 = f32[1008,216]{1,0:T(8,128)} reshape(f32[21,2,2,12,216]{4,3,2,1,0:T(8,128)} %copy-done.3) | data formatting | bytes 1741824 | tf_op jit(solution)/shard_map/reshape | solution.py:73
  41.3 2.3 %fusion.375 = f32[1008,216]{0,1:T(8,128)S(1)} fusion(f32[1008,216]{1,0:T(8,128)} %reshape.1151, f32[216,216]{1,0:T(8,128)} %constant.134.clone), kind=kOutput, calls=%fused_computation.790 | convolution fusion | flops 564350976 | bytes 1928448 | tf_op jit(solution)/shard_map/dot_general | solution.py:74
  43.7 1.9 fusion.363
  47.4 2.3 %fusion.376 = f32[1008,216]{0,1:T(8,128)S(1)} fusion(f32[1008,216]{1,0:T(8,128)} %reshape.1152, f32[216,216]{1,0:T(8,128)} %constant.137.clone), kind=kOutput, calls=%fused_computation.791 | convolution fusion | flops 564350976 | bytes 1928448 | tf_op jit(solution)/shard_map/dot_general | solution.py:74
  49.8 1.8 fusion.365
  53.4 2.3 %fusion.374 = f32[1008,216]{0,1:T(8,128)S(1)} fusion(f32[1008,216]{1,0:T(8,128)} %reshape.1150, f32[216,216]{1,0:T(8,128)} %constant.129.clone), kind=kOutput, calls=%fused_computation.789 | convolution fusion | flops 564350976 | bytes 1928448 | tf_op jit(solution)/shard_map/dot_general | solution.py:74
  55.8 1.7 fusion.367
  106.2 1.6 copy.451
  108.6 1.6 copy.452
  110.1 1.4 squeeze.167
  111.6 1.6 copy.455
  113.1 1.4 squeeze.168
  114.6 1.6 copy.458
  116.2 1.4 squeeze.169
  118.3 1.4 squeeze.170
  126.3 1.6 copy.339
  128.8 1.6 copy.341
  130.3 1.4 squeeze.137
  131.8 1.6 copy.342
  133.4 1.4 squeeze.138
  134.8 1.6 copy.345
  136.4 1.4 squeeze.139
  137.8 1.6 copy.348
  139.4 1.4 squeeze.140
  140.8 1.6 copy.352
  142.4 1.4 squeeze.141
  143.8 1.6 copy.353
  145.4 1.4 squeeze.142
  146.8 1.6 copy.356
  148.4 1.4 squeeze.143
  149.8 1.6 copy.359
  151.4 1.4 squeeze.144
  152.8 1.6 copy.363
  154.4 1.4 squeeze.145
  156.5 1.4 squeeze.146
  171.9 1.6 select_maximum_fusion
  182.3 1.9 collective-permute-start.4
  184.2 7.9 %collective-permute-start.5 = (f32[1,2,4,12,144]{4,3,1,0,2:T(8,128)S(1)}, f32[1,2,4,12,144]{4,3,1,0,2:T(8,128)S(1)}, u32[]{:S(2)}, u32[]{:S(2)}) collective-permute-start(f32[1,2,4,12,144]{4,3,1,0,2:T(8,128)S(1)} %get-tuple-element.170), channel_id=1, source_target_pairs={{8,0},{16,8},{24,16},{32,24},{40,32},{48,40},{56,48},{64,56},{72,6... | collective-permute-start | bytes 165896 | tf_op jit(solution)/shard_map/ppermute | solution.py:28
  192.1 5.3 %collective-permute-start.6 = (f32[2,1,4,12,144]{4,3,1,0,2:T(8,128)S(1)}, f32[2,1,4,12,144]{4,3,1,0,2:T(8,128)S(1)}, u32[]{:S(2)}, u32[]{:S(2)}) collective-permute-start(f32[2,1,4,12,144]{4,3,1,0,2:T(8,128)S(1)} %get-tuple-element.164), channel_id=1, source_target_pairs={{0,1},{1,2},{2,3},{3,4},{4,5},{5,6},{6,7},{7,0},{8,9},{9,10},{10,1... | collective-permute-start | bytes 165896 | tf_op jit(solution)/shard_map/ppermute | solution.py:27
  197.4 2.2 %collective-permute-start.7 = (f32[2,1,4,12,144]{4,3,1,0,2:T(8,128)S(1)}, f32[2,1,4,12,144]{4,3,1,0,2:T(8,128)S(1)}, u32[]{:S(2)}, u32[]{:S(2)}) collective-permute-start(f32[2,1,4,12,144]{4,3,1,0,2:T(8,128)S(1)} %get-tuple-element.163), channel_id=1, source_target_pairs={{1,0},{2,1},{3,2},{4,3},{5,4},{6,5},{7,6},{0,7},{9,8},{10,9},{11,1... | collective-permute-start | bytes 165896 | tf_op jit(solution)/shard_map/ppermute | solution.py:28
  202.3 4.0 %collective-permute-done.7 = f32[2,1,4,12,144]{4,3,1,0,2:T(8,128)S(1)} collective-permute-done((f32[2,1,4,12,144]{4,3,1,0,2:T(8,128)S(1)}, f32[2,1,4,12,144]{4,3,1,0,2:T(8,128)S(1)}, u32[]{:S(2)}, u32[]{:S(2)}) %collective-permute-start.7) | collective-permute-done | bytes 55328 | tf_op jit(solution)/shard_map/ppermute | solution.py:28
  (435 shorter events, 96.4 us)
Async XLA Ops:
  0.6 4.2 %copy-start.19 = (f32[216,36,1,1,1]{0,1,3,2,4:T(8,128)S(1)}, f32[216,36,1,1,1]{0,1,3,2,4:T(8,128)}, u32[]{:S(2)}) copy-start(f32[216,36,1,1,1]{0,1,3,2,4:T(8,128)} %constant.164) | copy-start | bytes 93316
  0.6 4.2 %copy-start = (f32[2,2,5,12,216]{4,1,3,2,0:T(2,128)S(1)}, f32[2,2,5,12,216]{4,1,3,2,0:T(2,128)}, u32[]{:S(2)}) copy-start(f32[2,2,5,12,216]{4,1,3,2,0:T(2,128)} %param.76) | copy-start | bytes 622084
  6.4 165.4 %collective-permute-start = (f32[1,2,5,12,144]{4,3,1,0,2:T(8,128)}, f32[1,2,5,12,144]{4,3,1,0,2:T(8,128)S(1)}, u32[]{:S(2)}, u32[]{:S(2)}) collective-permute-start(f32[1,2,5,12,144]{4,3,1,0,2:T(8,128)} %get-tuple-element.154), channel_id=1, source_target_pairs={{0,8},{8,16},{16,24},{24,32},{32,40},{40,48},{48,56},{56,64},{64,7... | collective-permute-start | bytes 207368 | tf_op jit(solution)/shard_map/ppermute | solution.py:27
  8.3 163.5 %collective-permute-start.1 = (f32[1,2,5,12,144]{4,3,1,0,2:T(8,128)}, f32[1,2,5,12,144]{4,3,1,0,2:T(8,128)S(1)}, u32[]{:S(2)}, u32[]{:S(2)}) collective-permute-start(f32[1,2,5,12,144]{4,3,1,0,2:T(8,128)} %get-tuple-element.153), channel_id=1, source_target_pairs={{8,0},{16,8},{24,16},{32,24},{40,32},{48,40},{56,48},{64,56},{72,6... | collective-permute-start | bytes 207368 | tf_op jit(solution)/shard_map/ppermute | solution.py:28
  29.5 142.3 %collective-permute-start.2 = (f32[2,1,5,12,144]{4,3,1,0,2:T(8,128)}, f32[2,1,5,12,144]{4,3,1,0,2:T(8,128)}, u32[]{:S(2)}, u32[]{:S(2)}) collective-permute-start(f32[2,1,5,12,144]{4,3,1,0,2:T(8,128)} %get-tuple-element.152), channel_id=1, source_target_pairs={{0,1},{1,2},{2,3},{3,4},{4,5},{5,6},{6,7},{7,0},{8,9},{9,10},{10,1... | collective-permute-start | bytes 207368 | tf_op jit(solution)/shard_map/ppermute | solution.py:27
  32.7 139.2 %collective-permute-start.3 = (f32[2,1,5,12,144]{4,3,1,0,2:T(8,128)}, f32[2,1,5,12,144]{4,3,1,0,2:T(8,128)}, u32[]{:S(2)}, u32[]{:S(2)}) collective-permute-start(f32[2,1,5,12,144]{4,3,1,0,2:T(8,128)} %get-tuple-element.151), channel_id=1, source_target_pairs={{1,0},{2,1},{3,2},{4,3},{5,4},{6,5},{7,6},{0,7},{9,8},{10,9},{11,1... | collective-permute-start | bytes 207368 | tf_op jit(solution)/shard_map/ppermute | solution.py:28
  49.7 2.6 %copy-start.2 = (f32[21,2,2,12,216]{4,3,2,1,0:T(8,128)S(1)}, f32[21,2,2,12,216]{4,3,2,1,0:T(8,128)}, u32[]{:S(2)}) copy-start(f32[21,2,2,12,216]{4,3,2,1,0:T(8,128)} %copy-done.1) | copy-start | bytes 2612740
  55.8 1.9 copy-start.16
  55.8 2.0 copy-start.10
  55.8 2.1 copy-start.9
  57.6 6.8 %copy-start.15 = (f32[48,216]{0,1:T(8,128)S(1)}, f32[48,216]{0,1:T(8,128)}, u32[]{:S(2)}) copy-start(f32[48,216]{0,1:T(8,128)} %get-tuple-element.80) | copy-start | bytes 124420
  57.8 12.2 %copy-start.14 = (f32[48,216]{0,1:T(8,128)S(1)}, f32[48,216]{0,1:T(8,128)}, u32[]{:S(2)}) copy-start(f32[48,216]{0,1:T(8,128)} %get-tuple-element.76) | copy-start | bytes 124420
  64.4 13.1 %copy-start.8 = (f32[48,216]{0,1:T(8,128)S(1)}, f32[48,216]{0,1:T(8,128)}, u32[]{:S(2)}) copy-start(f32[48,216]{0,1:T(8,128)} %get-tuple-element.107) | copy-start | bytes 124420
  65.1 12.5 %copy-start.7 = (f32[48,216]{0,1:T(8,128)S(1)}, f32[48,216]{0,1:T(8,128)}, u32[]{:S(2)}) copy-start(f32[48,216]{0,1:T(8,128)} %get-tuple-element.108) | copy-start | bytes 124420
  80.9 16.1 %copy-start.13 = (f32[48,216]{0,1:T(8,128)S(1)}, f32[48,216]{0,1:T(8,128)}, u32[]{:S(2)}) copy-start(f32[48,216]{0,1:T(8,128)} %get-tuple-element.93) | copy-start | bytes 124420
  97.1 20.5 %copy-start.12 = (f32[48,216]{0,1:T(8,128)S(1)}, f32[48,216]{0,1:T(8,128)}, u32[]{:S(2)}) copy-start(f32[48,216]{0,1:T(8,128)} %get-tuple-element.68) | copy-start | bytes 124420
  126.3 29.5 %copy-start.11 = (f32[48,216]{0,1:T(8,128)S(1)}, f32[48,216]{0,1:T(8,128)}, u32[]{:S(2)}) copy-start(f32[48,216]{0,1:T(8,128)} %get-tuple-element.113) | copy-start | bytes 124420
  160.1 3.4 %copy-start.31 = (f32[2,2,1,12,216]{4,3,1,0,2:T(8,128)S(1)}, f32[2,2,1,12,216]{4,3,1,0,2:T(8,128)}, u32[]{:S(2)}) copy-start(f32[2,2,1,12,216]{4,3,1,0,2:T(8,128)} %squeeze.174) | copy-start | bytes 124420
  160.1 3.4 %copy-start.32 = (f32[2,2,1,12,216]{4,3,1,0,2:T(8,128)S(1)}, f32[2,2,1,12,216]{4,3,1,0,2:T(8,128)}, u32[]{:S(2)}) copy-start(f32[2,2,1,12,216]{4,3,1,0,2:T(8,128)} %squeeze.175) | copy-start | bytes 124420
  160.1 3.5 %copy-start.33 = (f32[2,2,1,12,216]{4,3,1,0,2:T(8,128)S(1)}, f32[2,2,1,12,216]{4,3,1,0,2:T(8,128)}, u32[]{:S(2)}) copy-start(f32[2,2,1,12,216]{4,3,1,0,2:T(8,128)} %squeeze.176) | copy-start | bytes 124420
  160.1 3.5 %copy-start.34 = (f32[2,2,1,12,216]{4,3,1,0,2:T(8,128)S(1)}, f32[2,2,1,12,216]{4,3,1,0,2:T(8,128)}, u32[]{:S(2)}) copy-start(f32[2,2,1,12,216]{4,3,1,0,2:T(8,128)} %squeeze.177) | copy-start | bytes 124420
  161.2 2.4 %copy-start.35 = (f32[2,2,1,12,216]{4,3,1,0,2:T(8,128)S(1)}, f32[2,2,1,12,216]{4,3,1,0,2:T(8,128)}, u32[]{:S(2)}) copy-start(f32[2,2,1,12,216]{4,3,1,0,2:T(8,128)} %squeeze.178) | copy-start | bytes 124420
  161.2 2.4 %copy-start.36 = (f32[2,2,1,12,216]{4,3,1,0,2:T(8,128)S(1)}, f32[2,2,1,12,216]{4,3,1,0,2:T(8,128)}, u32[]{:S(2)}) copy-start(f32[2,2,1,12,216]{4,3,1,0,2:T(8,128)} %squeeze.179) | copy-start | bytes 124420
  161.2 2.4 %copy-start.37 = (f32[2,2,1,12,216]{4,3,1,0,2:T(8,128)S(1)}, f32[2,2,1,12,216]{4,3,1,0,2:T(8,128)}, u32[]{:S(2)}) copy-start(f32[2,2,1,12,216]{4,3,1,0,2:T(8,128)} %squeeze.180) | copy-start | bytes 124420
  161.2 2.4 %copy-start.38 = (f32[2,2,1,12,216]{4,3,1,0,2:T(8,128)S(1)}, f32[2,2,1,12,216]{4,3,1,0,2:T(8,128)}, u32[]{:S(2)}) copy-start(f32[2,2,1,12,216]{4,3,1,0,2:T(8,128)} %squeeze.181) | copy-start | bytes 124420
  162.3 1.5 copy-start.39
  162.3 1.5 copy-start.40
  162.3 1.5 copy-start.41
  162.3 1.5 copy-start.42
  162.3 1.6 copy-start.55
  162.3 1.6 copy-start.56
  162.3 1.6 copy-start.57
  162.3 1.6 copy-start.58
  162.4 1.6 copy-start.59
  165.8 1.5 copy-start.5
  166.2 1.5 copy-start.75
  166.2 1.5 copy-start.6
  169.9 1.5 copy-start.21
  175.0 1.8 copy-start.23
  175.2 2.0 copy-start.65
  175.2 2.4 %copy-start.22 = (f32[36,216,1,1,1]{1,0,4,3,2:T(8,128)S(1)}, f32[36,216,1,1,1]{1,0,4,3,2:T(8,128)}, u32[]{:S(2)}) copy-start(f32[36,216,1,1,1]{1,0,4,3,2:T(8,128)} %constant.168) | copy-start | bytes 93316
  176.0 1.9 copy-start.25
  176.4 1.9 copy-start.26
  182.2 18.3 %copy-start.73 = (f32[3]{0:T(128)S(1)}, f32[3]{0:T(128)}, u32[]{:S(2)}) copy-start(f32[3]{0:T(128)} %constant.138.clone) | copy-start | bytes 40
  182.3 20.0 %collective-permute-start.4 = (f32[1,2,4,12,144]{4,3,1,0,2:T(8,128)S(1)}, f32[1,2,4,12,144]{4,3,1,0,2:T(8,128)S(1)}, u32[]{:S(2)}, u32[]{:S(2)}) collective-permute-start(f32[1,2,4,12,144]{4,3,1,0,2:T(8,128)S(1)} %get-tuple-element.171), channel_id=1, source_target_pairs={{0,8},{8,16},{16,24},{24,32},{32,40},{40,48},{48,56},{56,64},{64,7... | collective-permute-start | bytes 165896 | tf_op jit(solution)/shard_map/ppermute | solution.py:27
  184.2 18.1 %collective-permute-start.5 = (f32[1,2,4,12,144]{4,3,1,0,2:T(8,128)S(1)}, f32[1,2,4,12,144]{4,3,1,0,2:T(8,128)S(1)}, u32[]{:S(2)}, u32[]{:S(2)}) collective-permute-start(f32[1,2,4,12,144]{4,3,1,0,2:T(8,128)S(1)} %get-tuple-element.170), channel_id=1, source_target_pairs={{8,0},{16,8},{24,16},{32,24},{40,32},{48,40},{56,48},{64,56},{72,6... | collective-permute-start | bytes 165896 | tf_op jit(solution)/shard_map/ppermute | solution.py:28
  192.1 10.2 %collective-permute-start.6 = (f32[2,1,4,12,144]{4,3,1,0,2:T(8,128)S(1)}, f32[2,1,4,12,144]{4,3,1,0,2:T(8,128)S(1)}, u32[]{:S(2)}, u32[]{:S(2)}) collective-permute-start(f32[2,1,4,12,144]{4,3,1,0,2:T(8,128)S(1)} %get-tuple-element.164), channel_id=1, source_target_pairs={{0,1},{1,2},{2,3},{3,4},{4,5},{5,6},{6,7},{7,0},{8,9},{9,10},{10,1... | collective-permute-start | bytes 165896 | tf_op jit(solution)/shard_map/ppermute | solution.py:27
  197.4 9.0 %collective-permute-start.7 = (f32[2,1,4,12,144]{4,3,1,0,2:T(8,128)S(1)}, f32[2,1,4,12,144]{4,3,1,0,2:T(8,128)S(1)}, u32[]{:S(2)}, u32[]{:S(2)}) collective-permute-start(f32[2,1,4,12,144]{4,3,1,0,2:T(8,128)S(1)} %get-tuple-element.163), channel_id=1, source_target_pairs={{1,0},{2,1},{3,2},{4,3},{5,4},{6,5},{7,6},{0,7},{9,8},{10,9},{11,1... | collective-permute-start | bytes 165896 | tf_op jit(solution)/shard_map/ppermute | solution.py:28
  (36 other events, 34.5 us)
where the time goes:
time: 215 us; the launch traced here: 212 us
  local copies, waits for them, and re-layouts  123 us (57%)
  starting transfers between devices  45.4 us (21%)
  matrix products  26.4 us (12%)
  other arithmetic  10 us (5%)
  waiting for transfers between devices  4.02 us (2%)
  between operations  3.32 us (2%)
    ppermute x4, starting transfers between devices, padded_2(): lax.ppermute(initial, axis, [(b, a) for a, b in up])  33.2 us
    dot_general x45, matrix products, contract(): jnp.dot(flat, table, precision=lax.Precision.HIGHEST, preferred_element_t...  26.4 us
    slice x15, local copies, waits for them, and re-layouts, triple(): derived[base + 3] + density * derived[base + 1] + normal * derived[base + 2]  18.7 us
    slice x12, local copies, waits for them, and re-layouts, triple(): derived[base + 1]  13.2 us
    slice x12, local copies, waits for them, and re-layouts, triple(): derived[base + 2]  12.6 us
    slice x12, local copies, waits for them, and re-layouts, triple(): derived[base]  12.6 us
    ppermute x4, starting transfers between devices, padded_2(): lax.ppermute(last, axis, up)  12.3 us
    squeeze x12, local copies, waits for them, and re-layouts, triple(): derived[base + 1]  10.8 us
  transfers between devices with their start and end apart: 8, of which 1 were waited for; matrix products, arithmetic and copies ran while one was open for 63% of the time, Pallas kernels for 0%

commit v1 on v0

v1 whole, which is shorter than its diff:
```python
import functools
import math

import jax
import jax.numpy as jnp
import numpy as np
from jax import lax
from jax.experimental import pallas as pl
from jax.experimental.pallas import tpu as pltpu
from jax.sharding import PartitionSpec as P

GAMMA = 1.4
VISCOSITY = 0.001
CONDUCT = 0.001 * 1.4 / (0.4 * 0.72)
SCALE_X = 2.0 / 0.2
SCALE_Z = 2.0 / 0.15
TIME_STEP = 0.004
SECTION_A = -0.4178904745
SECTION_B = 0.3792103129
HALF_W = 7.5

ROWS, NODES = (48, 216)
F32, BF16 = (jnp.float32, jnp.bfloat16)


def node_matrix():
    root = math.sqrt(7.0)
    outer = math.sqrt(1.0 / 3.0 + 2.0 * root / 21.0)
    inner = math.sqrt(1.0 / 3.0 - 2.0 * root / 21.0)
    points = np.array([-1.0, -outer, -inner, inner, outer, 1.0])
    barycen = np.array(
        [1.0 / np.prod([points[i] - points[j] for j in range(6) if j != i]) for i in range(6)]
    )
    matrix = np.zeros((6, 6))
    for i in range(6):
        for j in range(6):
            if j != i:
                matrix[i, j] = barycen[j] / barycen[i] / (points[i] - points[j])
        matrix[i, i] = -np.sum(matrix[i])
    return matrix


STRIDE = (36, 6, 1)


def coefficients():
    matrix = node_matrix()
    nodes = np.arange(NODES)
    place = (nodes // 36, nodes // 6 % 6, nodes % 6)
    rows = [matrix[place[d], j] for d in range(3) for j in range(6)]
    return np.stack(rows).astype(np.float32)


def tables():
    nodes = np.arange(NODES)
    low_face = nodes[nodes % 6 == 0]
    unpack = np.zeros((2, 3, 128, NODES), np.float32)
    corner_unpack = np.zeros((2, 3, 128, NODES), np.float32)
    for j in range(3):
        slot = 36 * j + np.arange(36)
        unpack[0, j, slot, low_face] = 1.0
        unpack[1, j, slot, low_face + 5] = 1.0
        for iy in range(6):
            slot = 108 + 6 * j + iy
            for ix in (0, 5):
                base = 36 * ix + 6 * iy
                corner_unpack[0, j, slot, base] = 1.0
                corner_unpack[1, j, slot, base + 5] = 1.0
    return dict(uz=unpack.astype(jnp.bfloat16), cu=corner_unpack.astype(jnp.bfloat16))


def one_hot(source, depth):
    rows = lax.broadcasted_iota(jnp.int32, (depth, source.shape[1]), 0)
    return jnp.where(rows == source, 1.0, 0.0).astype(BF16)


def x_pack_table(side, j):
    lane = lax.broadcasted_iota(jnp.int32, (1, 128), 1) - 36 * j
    inside = jnp.logical_and(lane >= 0, lane < 36)
    return one_hot(jnp.where(inside, lane + (180 if side == 0 else 0), -1), NODES)


def x_unpack_table(side, j):
    lane = lax.broadcasted_iota(jnp.int32, (1, NODES), 1) - (0 if side == 0 else 180)
    inside = jnp.logical_and(lane >= 0, lane < 36)
    return one_hot(jnp.where(inside, lane + 36 * j, -1), 128)


def z_pack_table(side, j):
    lane = lax.broadcasted_iota(jnp.int32, (1, 128), 1) - 36 * j
    inside = jnp.logical_and(lane >= 0, lane < 36)
    return one_hot(jnp.where(inside, 6 * lane + (5 if side == 0 else 0), -1), NODES)


def corner_pack_table(side, j):
    lane = lax.broadcasted_iota(jnp.int32, (1, 128), 1) - (108 + 6 * j)
    inside = jnp.logical_and(lane >= 0, lane < 6)
    source = jnp.where(inside, 6 * lane + (5 if side == 0 else 0), -1000)
    return one_hot(source, NODES) + one_hot(source + 180, NODES)


def pick_table(side):
    row = lax.broadcasted_iota(jnp.int32, (24, ROWS), 0)
    column = lax.broadcasted_iota(jnp.int32, (24, ROWS), 1)
    return jnp.where(column == 2 * row + (1 - side), 1.0, 0.0).astype(BF16)


def swap_table(lanes, d):
    lane = lax.broadcasted_iota(jnp.int32, (1, NODES), 1)
    step = 5 * STRIDE[d]
    return one_hot(
        jnp.where(lanes.lo[d], lane + step, jnp.where(lanes.hi[d], lane - step, -1)), NODES
    )


def deriv_table(lanes, coef_ref, d):
    lane = lax.broadcasted_iota(jnp.int32, (1, NODES), 1)
    base = lane - STRIDE[d] * lanes.place[d]
    rows = lax.broadcasted_iota(jnp.int32, (NODES, NODES), 0) - base
    table = jnp.zeros((NODES, NODES), F32)
    for j in range(6):
        line = coef_ref[6 * d + j : 6 * d + j + 1, :]
        table = jnp.where(rows == STRIDE[d] * j, line, table)
    return table


def halves(value):
    high = value.astype(BF16)
    return (high, (value - high.astype(F32)).astype(BF16))


def dot(a, b):
    return jnp.dot(a, b, preferred_element_type=F32)


def derive(pair, dh, dl):
    return dot(pair[0], dh) + (dot(pair[1], dh) + dot(pair[0], dl))


def move(pair, table):
    return dot(pair[0], table) + dot(pair[1], table)


def stack(fields):
    return jnp.concatenate(fields, axis=0)


def rows_of(value, count, size=ROWS):
    return [value[i * size : (i + 1) * size] for i in range(count)]


class Lanes:
    def __init__(self):
        lane = lax.broadcasted_iota(jnp.int32, (1, NODES), 1)
        row = lax.broadcasted_iota(jnp.int32, (ROWS, 1), 0)
        self.a, self.c = (row // 24, row % 2)
        self.k = (row % 24) // 2
        place = (lane // 36, lane // 6 % 6, lane % 6)
        self.place = place
        self.lo = [p == 0 for p in place]
        self.hi = [p == 5 for p in place]
        self.sig = [
            jnp.where(p == 0, 1.0, 0.0) + jnp.where(p == 5, -1.0, 0.0) for p in place
        ]
        self.face = [jnp.logical_or(lo, hi) for lo, hi in zip(self.lo, self.hi)]
        self.ghost_x = jnp.logical_or(
            jnp.logical_and(self.a == 0, self.lo[0]), jnp.logical_and(self.a == 1, self.hi[0])
        )
        self.ghost_z = jnp.logical_or(
            jnp.logical_and(self.c == 0, self.lo[2]), jnp.logical_and(self.c == 1, self.hi[2])
        )


def read_rows(ref, field):
    return stack([ref[a, field].reshape(24, NODES) for a in range(2)])


def write_rows(ref, field, value):
    for a in range(2):
        ref[a, field] = value[24 * a : 24 * a + 24].reshape(12, 2, NODES)


def load_prims(state_ref):
    rho = state_ref[0]
    inv = 1.0 / rho
    mom = [state_ref[1], state_ref[2], state_ref[3]]
    vel = [m * inv for m in mom]
    energy = state_ref[4]
    pres = (GAMMA - 1.0) * (
        energy - 0.5 * (mom[0] * vel[0] + mom[1] * vel[1] + mom[2] * vel[2])
    )
    return (rho, mom, energy, vel, pres, pres * inv, inv)


def walls_of(mask_ref, lanes):
    spread = jnp.zeros((ROWS, 11), jnp.int32)
    for a in range(2):
        for c in range(2):
            here = jnp.logical_and(lanes.a == a, lanes.c == c)
            spread = jnp.where(here, mask_ref[a, c : c + 1, :], spread)
    column = lax.broadcasted_iota(jnp.int32, (ROWS, 11), 1)
    solid = jnp.where(spread == 1, 1.0, 0.0)
    low = jnp.sum(jnp.where(column == lanes.k - 1, solid, 0.0), axis=1, keepdims=True)
    high = jnp.sum(jnp.where(column == lanes.k, solid, 0.0), axis=1, keepdims=True)
    return (
        jnp.logical_or(low > 0.5, lanes.k == 0),
        jnp.logical_or(high > 0.5, lanes.k == 11),
    )


def scale_y(h_ref, lanes):
    column = lax.broadcasted_iota(jnp.int32, (ROWS, 12), 1)
    own = jnp.where(column == lanes.k, h_ref[0:1, :], 0.0)
    return 2.0 / jnp.sum(own, axis=1, keepdims=True)


def shift(value, by):
    return pltpu.roll(value, by % value.shape[0], 0)


def inner_x(swapped, own, lanes):
    other = stack([swapped[24:48], swapped[0:24]])
    return jnp.where(jnp.logical_and(lanes.face[0], jnp.logical_not(lanes.ghost_x)), other, own)


def inner_z(swapped, own, lanes):
    other = jnp.where(lanes.lo[2], shift(swapped, 1), shift(swapped, -1))
    return jnp.where(jnp.logical_and(lanes.face[2], jnp.logical_not(lanes.ghost_z)), other, own)


def inner_y(swapped, own, lanes, wall_lo, wall_hi, sign):
    other = jnp.where(lanes.lo[1], shift(swapped, 2), shift(swapped, -2))
    solid = jnp.logical_or(
        jnp.logical_and(wall_lo, lanes.lo[1]), jnp.logical_and(wall_hi, lanes.hi[1])
    )
    return jnp.where(lanes.face[1], jnp.where(solid, sign * own, other), own)


def stress(grads):
    gx, gy, gz = grads
    third = (2.0 / 3.0) * VISCOSITY * (gx[0] + gy[1] + gz[2])
    return [
        2.0 * VISCOSITY * gx[0] - third,
        2.0 * VISCOSITY * gy[1] - third,
        2.0 * VISCOSITY * gz[2] - third,
        VISCOSITY * (gx[1] + gy[0]),
        VISCOSITY * (gx[2] + gz[0]),
        VISCOSITY * (gy[2] + gz[1]),
        CONDUCT * gx[3],
        CONDUCT * gy[3],
        CONDUCT * gz[3],
    ]


def add_lift(tg, delta, direction):
    tg = list(tg)
    bulk = (2.0 / 3.0) * VISCOSITY * delta[direction]
    for d in range(3):
        tg[d] = tg[d] - bulk
    tg[direction] = tg[direction] + 2.0 * VISCOSITY * delta[direction]
    for other in range(3):
        if other != direction:
            slot = {1: 3, 2: 4, 3: 5}[direction + other]
            tg[slot] = tg[slot] + VISCOSITY * delta[other]
    tg[6 + direction] = tg[6 + direction] + CONDUCT * delta[3]
    return tg


def flux_of(tg, vel, direction):
    t = [
        (tg[0], tg[3], tg[4]),
        (tg[3], tg[1], tg[5]),
        (tg[4], tg[5], tg[2]),
    ][direction]
    work = vel[0] * t[0] + vel[1] * t[1] + vel[2] * t[2] + tg[6 + direction]
    return [t[0], t[1], t[2], work]


def ghost_lift(flux, vel, delta, direction, lift_direction):
    zero = jnp.zeros_like(delta[0])
    tg = add_lift([zero] * 9, delta, lift_direction)
    change = flux_of(tg, vel, direction)
    return [f + d for f, d in zip(flux, change)]


def pack_faces(fields, table_of, side):
    total = None
    for j in range(3):
        part = halves(stack([fields[3 * s + j] for s in range(3)]))
        value = move(part, table_of(side, j))
        total = value if total is None else total + value
    return total


def euler(rho, vel, pres, direction):
    normal = vel[direction]
    mass = rho * normal
    square = vel[0] * vel[0] + vel[1] * vel[1] + vel[2] * vel[2]
    energy = pres * (1.0 / (GAMMA - 1.0)) + 0.5 * rho * square
    flux = [mass] + [mass * v for v in vel] + [(energy + pres) * normal]
    flux[1 + direction] = flux[1 + direction] + pres
    state = [rho, rho * vel[0], rho * vel[1], rho * vel[2], energy]
    return (flux, state)


def face_terms(own, out, direction, sig, scale):
    rho, vel, temp = own
    rho_out, vel_out, temp_out = out
    flux, state = euler(rho, vel, rho * temp, direction)
    flux_out, state_out = euler(rho_out, vel_out, rho_out * temp_out, direction)
    speed = jnp.maximum(
        jnp.abs(vel[direction]) + jnp.sqrt(GAMMA * temp),
        jnp.abs(vel_out[direction]) + jnp.sqrt(GAMMA * temp_out),
    )
    speed = speed * jnp.abs(sig)
    return [
        (HALF_W * scale) * (sig * (fo - fi) + speed * (so - si))
        for fi, fo, si, so in zip(flux, flux_out, state, state_out)
    ]


def parity_of(axis):
    return lax.rem(lax.axis_index(axis), 2) == 0


def first_kernel(state_hbm, mask_hbm, h_hbm, coef_hbm, st_ref, aux_ref, dh_ref, dl_ref, sw_ref, tg_ref,
                 even_ref, odd_ref, state_buf, mask_buf, h_buf, coef_buf, sems):
    copies = [
        pltpu.make_async_copy(src, dst, sems.at[i])
        for i, (src, dst) in enumerate(
            ((coef_hbm, coef_buf), (state_hbm, state_buf), (mask_hbm, mask_buf), (h_hbm, h_buf))
        )
    ]
    for copy in copies:
        copy.start()
    lanes = Lanes()
    for d in range(3):
        sw_ref[d] = swap_table(lanes, d)
    copies[0].wait()
    for d in range(3):
        high, low = halves(deriv_table(lanes, coef_buf, d))
        dh_ref[d] = high
        dl_ref[d] = low
    for copy in copies[1:]:
        copy.wait()
    for i in range(5):
        st_ref[i] = read_rows(state_buf, i)
    rho, _, _, vel, _, temp, _ = load_prims(st_ref)
    wall_lo, wall_hi = walls_of(mask_buf, lanes)
    sy = scale_y(h_buf, lanes)
    slot = lax.broadcasted_iota(jnp.int32, (ROWS, 128), 1)
    aux_ref[...] = jnp.where(
        slot == 0,
        jnp.where(wall_lo, 1.0, 0.0),
        jnp.where(slot == 1, jnp.where(wall_hi, 1.0, 0.0), sy),
    )
    own = vel + [temp]
    pair = halves(stack(own))
    scales = (SCALE_X, sy, SCALE_Z)
    grads = []
    for d in range(3):
        slope = rows_of(derive(pair, dh_ref[d], dl_ref[d]), 4)
        swapped = rows_of(move(pair, sw_ref[d]), 4)
        grad = []
        for i in range(4):
            if d == 0:
                out = inner_x(swapped[i], own[i], lanes)
            elif d == 2:
                out = inner_z(swapped[i], own[i], lanes)
            else:
                sign = 1.0 if i == 3 else -1.0
                out = inner_y(swapped[i], own[i], lanes, wall_lo, wall_hi, sign)
            grad.append(scales[d] * (slope[i] + (HALF_W * lanes.sig[d]) * (own[i] - out)))
        grads.append(grad)
    tg = stress(grads)
    for i in range(9):
        tg_ref[i] = tg[i]
    fields = [rho] + own + flux_of(tg, vel, 0)
    up = pack_faces([f[24:48] for f in fields], x_pack_table, 0)
    down = pack_faces([f[0:24] for f in fields], x_pack_table, 1)
    even = parity_of("gx")
    even_ref[...] = jnp.where(even, up, down)
    odd_ref[...] = jnp.where(even, down, up)


def aux_of(aux_ref):
    return (aux_ref[:, 0:1] > 0.5, aux_ref[:, 1:2] > 0.5, aux_ref[:, 2:3])


def volume_kernel(state_ref, aux_ref, dh_ref, dl_ref, sw_ref, out_ref, ux_ref, pz_ref, cp_ref):
    lanes = Lanes()
    rho, mom, energy, vel, pres, temp, inv = load_prims(state_ref)
    wall_lo, wall_hi, sy = aux_of(aux_ref)
    scales = (SCALE_X, sy, SCALE_Z)
    spec = energy * inv
    common = halves(stack([rho] + vel + [pres, spec] + mom + [energy]))
    swap_pair = halves(stack([rho] + vel + [temp]))
    others = vel + [spec]
    dens = mom + [energy]
    own = [rho] + vel + [temp]
    total = [None] * 5
    for d in range(3):
        normal = vel[d]
        mine = [pres * normal] + [normal * o for o in others] + [normal * m for m in dens]
        base = rows_of(derive(common, dh_ref[d], dl_ref[d]), 10)
        rest = rows_of(derive(halves(stack(mine)), dh_ref[d], dl_ref[d]), 9)
        d_rho, d_pres, d_work = (base[0], base[4], rest[0])
        d_others = base[1:4] + [base[5]]
        d_dens = base[6:10]
        d_norm, d_mass = (base[1 + d], base[6 + d])
        mass = mom[d]
        parts = [0.5 * (rho * d_norm + normal * d_rho + d_mass)]
        for m in range(4):
            value = 0.25 * (
                rest[5 + m]
                + rho * rest[1 + m]
                + normal * d_dens[m]
                + others[m] * (d_mass + rho * d_norm + normal * d_rho)
                + mass * d_others[m]
            )
            if m == d:
                value = value + d_pres
            if m == 3:
                value = value + 0.5 * (pres * d_norm + normal * d_pres + d_work)
            parts.append(value)
        swapped = rows_of(move(swap_pair, sw_ref[d]), 5)
        outs = []
        for i in range(5):
            if d == 0:
                outs.append(inner_x(swapped[i], own[i], lanes))
            elif d == 2:
                outs.append(inner_z(swapped[i], own[i], lanes))
            else:
                sign = -1.0 if i in (1, 2, 3) else 1.0
                outs.append(inner_y(swapped[i], own[i], lanes, wall_lo, wall_hi, sign))
        faces = face_terms(
            (rho, vel, temp), (outs[0], outs[1:4], outs[4]), d, lanes.sig[d], scales[d]
        )
        for i in range(5):
            value = faces[i] - scales[d] * parts[i]
            total[i] = value if d == 0 else total[i] + value
    for i in range(5):
        out_ref[i] = total[i]
    for side in range(2):
        for j in range(3):
            ux_ref[side, j] = x_unpack_table(side, j)
            pz_ref[side, j] = z_pack_table(side, j)
            cp_ref[side, j] = corner_pack_table(side, j)


def sides_of(even_ref, odd_ref, axis):
    even = parity_of(axis)
    return (
        jnp.where(even, odd_ref[...], even_ref[...]),
        jnp.where(even, even_ref[...], odd_ref[...]),
    )


def unpack_faces(lower, upper, table_ref, spread):
    first, second = (halves(lower), halves(upper))
    fields = [None] * 9
    for j in range(3):
        low = rows_of(move(first, table_ref[0, j]), 3, 24)
        high = rows_of(move(second, table_ref[1, j]), 3, 24)
        for s in range(3):
            fields[3 * s + j] = spread(low[s], high[s])
    return fields


def second_kernel(state_ref, tg_ref, even_ref, odd_ref, ux_ref, pz_ref, cp_ref,
                  tgo_ref, gx_ref, even_out, odd_out):
    lanes = Lanes()
    rho, _, _, vel, _, temp, _ = load_prims(state_ref)
    own = vel + [temp]
    lower, upper = sides_of(even_ref, odd_ref, "gx")
    ghost = unpack_faces(lower, upper, ux_ref, lambda lo, hi: stack([lo, hi]))
    weight = (SCALE_X * HALF_W) * lanes.sig[0] * jnp.where(lanes.ghost_x, 1.0, 0.0)
    delta = [weight * (o - g) for o, g in zip(own, ghost[1:5])]
    tg = add_lift([tg_ref[i] for i in range(9)], delta, 0)
    for i in range(9):
        tgo_ref[i] = tg[i]
    flux = ghost_lift(ghost[5:9], ghost[1:4], delta, 0, 0)
    for i, field in enumerate(ghost[:5] + flux):
        gx_ref[i] = field
    fields = [rho] + own + flux_of(tg, vel, 2)
    corner = [jnp.where(lanes.ghost_x, g, 0.0) for g in ghost[1:5]]
    messages = []
    for side in (0, 1):
        total = None
        for j in range(3):
            picked = [fields[3 * s + j] for s in range(3)]
            part = move(halves(stack(picked)), pz_ref[side, j])
            total = part if total is None else total + part
        edges = move(halves(stack([corner[0], corner[3]])), cp_ref[side, 0])
        first = edges[0:48]
        for j in (1, 2):
            first = first + move(halves(corner[j]), cp_ref[side, j])
        total = total + stack([first, edges[48:96], jnp.zeros((ROWS, 128), F32)])
        pick = pick_table(side)
        kept = []
        for s in range(3):
            high, low = halves(total[48 * s : 48 * s + 48])
            kept.append(dot(pick, high) + dot(pick, low))
        messages.append(stack(kept))
    even = parity_of("gz")
    even_out[...] = jnp.where(even, messages[0], messages[1])
    odd_out[...] = jnp.where(even, messages[1], messages[0])


def last_kernel(state_ref, reg_ref, vol_ref, tg_ref, gx_ref, aux_ref, even_ref, odd_ref,
                dh_ref, dl_ref, sw_ref, uz_ref, cu_ref, ri_ref, state_out, reg_out):
    lanes = Lanes()
    rho, mom, energy, vel, _, temp, _ = load_prims(state_ref)
    wall_lo, wall_hi, sy = aux_of(aux_ref)
    scales = (SCALE_X, sy, SCALE_Z)
    own = vel + [temp]
    lower, upper = sides_of(even_ref, odd_ref, "gz")

    def widen(value, side):
        put = ri_ref[side]
        parts = []
        for s in range(3):
            high, low = halves(value[24 * s : 24 * s + 24, :])
            parts.append(dot(put, high) + dot(put, low))
        return stack(parts)

    first, second = (halves(widen(lower, 0)), halves(widen(upper, 1)))
    ghost_z = [None] * 9
    corner = [None] * 4
    for j in range(3):
        value = rows_of(move(first, uz_ref[0, j]) + move(second, uz_ref[1, j]), 3)
        edge = rows_of(move(first, cu_ref[0, j]) + move(second, cu_ref[1, j]), 3)
        for s in range(3):
            ghost_z[3 * s + j] = value[s]
        corner[j] = edge[0]
        if j == 0:
            corner[3] = edge[1]
    keep_x = jnp.where(lanes.ghost_x, 1.0, 0.0)
    keep_z = jnp.where(lanes.ghost_z, 1.0, 0.0)
    ghost_x = [gx_ref[i] for i in range(9)]
    weight = (SCALE_Z * HALF_W) * lanes.sig[2] * keep_z
    delta = [weight * (o - g) for o, g in zip(own, ghost_z[1:5])]
    tg = add_lift([tg_ref[i] for i in range(9)], delta, 2)
    flux_z = ghost_lift(ghost_z[5:9], ghost_z[1:4], delta, 2, 2)
    edge_delta = [(weight * keep_x) * (g - c) for g, c in zip(ghost_x[1:5], corner)]
    flux_x = ghost_lift(ghost_x[5:9], ghost_x[1:4], edge_delta, 0, 2)
    total = [vol_ref[i] for i in range(5)]
    for d, ghost, keep in ((0, ghost_x, lanes.ghost_x), (2, ghost_z, lanes.ghost_z)):
        out = [jnp.where(keep, g, o) for g, o in zip(ghost[:5], [rho] + own)]
        faces = face_terms(
            (rho, vel, temp), (out[0], out[1:4], out[4]), d, lanes.sig[d], scales[d]
        )
        total = [t + f for t, f in zip(total, faces)]
    for d in range(3):
        flux = flux_of(tg, vel, d)
        pair = halves(stack(flux))
        slope = rows_of(derive(pair, dh_ref[d], dl_ref[d]), 4)
        swapped = rows_of(move(pair, sw_ref[d]), 4)
        for i in range(4):
            if d == 0:
                out = jnp.where(lanes.ghost_x, flux_x[i], inner_x(swapped[i], flux[i], lanes))
            elif d == 2:
                out = jnp.where(lanes.ghost_z, flux_z[i], inner_z(swapped[i], flux[i], lanes))
            else:
                out = inner_y(swapped[i], flux[i], lanes, wall_lo, wall_hi, 1.0)
            total[i + 1] = total[i + 1] + scales[d] * (
                slope[i] + (HALF_W * lanes.sig[d]) * (flux[i] - out)
            )
    for i, field in enumerate([rho] + mom + [energy]):
        reg = SECTION_A * read_rows(reg_ref, i) + TIME_STEP * total[i]
        write_rows(reg_out, i, reg)
        write_rows(state_out, i, field + SECTION_B * reg)


def row_table():
    put = np.zeros((2, ROWS, 24), np.float32)
    for i in range(24):
        put[0, 2 * i, i] = 1.0
        put[1, 2 * i + 1, i] = 1.0
    return put.astype(jnp.bfloat16)


def field_shape(count):
    return jax.ShapeDtypeStruct((count, ROWS, NODES), F32)


LIMIT = 20 * 1024 * 1024
FACE = jax.ShapeDtypeStruct((72, 128), F32)


def call(kernel, outs, name, flops, **more):
    return pl.pallas_call(
        kernel,
        out_shape=outs,
        name=name,
        compiler_params=pltpu.CompilerParams(vmem_limit_bytes=LIMIT),
        cost_estimate=pl.CostEstimate(flops=flops, bytes_accessed=2_000_000, transcendentals=0),
        **more,
    )


def swap_pairs(axis):
    size = lax.axis_size(axis)
    even = [(i, i ^ 1) for i in range(size)]
    odd = [(i, (i + 1) % size if i % 2 else (i - 1) % size) for i in range(size)]
    return (even, odd)


def shards(state, register, heights, solid_wall_mask):
    t = {key: jnp.asarray(value) for key, value in tables().items()}
    put = jnp.asarray(row_table())
    coef = jnp.asarray(coefficients())
    h = heights.reshape(1, 12)

    def rows(array):
        return jnp.transpose(array, (0, 2, 3, 1, 4))

    def unrows(array):
        return jnp.transpose(array, (0, 3, 1, 2, 4))

    reg = rows(register)
    whole = jax.ShapeDtypeStruct((2, 5, 12, 2, NODES), F32)
    table = jax.ShapeDtypeStruct((3, NODES, NODES), BF16)
    aux_shape = jax.ShapeDtypeStruct((ROWS, 128), F32)
    hbm = pl.BlockSpec(memory_space=pltpu.HBM)
    st, aux, dh, dl, sw, tg, even_x, odd_x = call(
        first_kernel,
        (field_shape(5), aux_shape, table, table, table, field_shape(9), FACE, FACE),
        "first",
        10**8,
        in_specs=[hbm] * 4,
        scratch_shapes=[
            pltpu.VMEM((2, 5, 12, 2, NODES), F32),
            pltpu.VMEM((2, 2, 11), jnp.int32),
            pltpu.VMEM((1, 12), F32),
            pltpu.VMEM((18, NODES), F32),
            pltpu.SemaphoreType.DMA((4,)),
        ],
    )(*[pltpu.with_memory_space_constraint(v, pltpu.HBM) for v in (rows(state), solid_wall_mask, h, coef)])
    even, odd = swap_pairs("gx")
    even_x = lax.ppermute(even_x, "gx", even)
    odd_x = lax.ppermute(odd_x, "gx", odd)
    pack = jax.ShapeDtypeStruct((2, 3, NODES, 128), BF16)
    unpack = jax.ShapeDtypeStruct((2, 3, 128, NODES), BF16)
    vol, ux, pz, cp = call(
        volume_kernel, (field_shape(5), unpack, pack, pack), "volume", 10**9
    )(st, aux, dh, dl, sw)
    tg, gx, even_z, odd_z = call(
        second_kernel, (field_shape(9), field_shape(9), FACE, FACE), "second", 10**8
    )(st, tg, even_x, odd_x, ux, pz, cp)
    even, odd = swap_pairs("gz")
    even_z = lax.ppermute(even_z, "gz", even)
    odd_z = lax.ppermute(odd_z, "gz", odd)
    state_next, reg_next = call(last_kernel, (whole, whole), "last", 10**8)(
        st, reg, vol, tg, gx, aux, even_z, odd_z, dh, dl, sw, t["uz"], t["cu"], put,
    )
    return (unrows(state_next), unrows(reg_next))


def solution(mesh):
    spec = P("gx", "gz", None, None, None)
    return jax.shard_map(
        shards,
        mesh=mesh,
        in_specs=(spec, spec, P(), P("gx", "gz", None)),
        out_specs=(spec, spec),
        check_vma=False,
    )
```

time: 215 us -> 43.8 us (0.20); the launches traced: 212 us -> 43.5 us
  local copies, waits for them, and re-layouts: 123 us -> 0.03 us
  matrix products: 26.4 us -> 0 us
  starting transfers between devices: 45.4 us -> 28.8 us
  other arithmetic: 10 us -> 0 us
  Pallas kernels: 0 us -> 8.52 us
  between operations: 3.32 us -> 0.74 us
    slice x83 -> x0, local copies, waits for them, and re-layouts: 66.2 us -> none  [the longest x15 18.7 us: triple(): derived[base + 3] + density * derived[base + 1] + normal * derived[base + 2]]
    squeeze x63 -> x0, local copies, waits for them, and re-layouts: 44.4 us -> none  [the longest x12 10.8 us: triple(): derived[base + 1]]
    dot_general x45 -> x0, matrix products: 26.4 us -> none  [contract(): jnp.dot(flat, table, precision=lax.Precision.HIGHEST, preferred_element_t...]
    ppermute x8 -> x4, starting transfers between devices: 45.4 us -> 28.8 us  [the longest x1 21.1 us: shards(): odd_x = lax.ppermute(odd_x, 'gx', odd)]
    pallas_call x0 -> x4, Pallas kernels: none -> 8.52 us  [the longest x1 2.45 us: shards(): call(volume_kernel, (field_shape(5), unpack, pack, pack), 'volume', 10 ** 9)]
    unnamed x178 -> x8, local copies, waits for them, and re-layouts: 7.37 us -> 0.03 us
    reshape x3 -> x0, local copies, waits for them, and re-layouts: 4.59 us -> none  [contract(): flat = field.reshape((-1, field.shape[-1]))]
    unnamed x34 -> x0, other arithmetic: 3.99 us -> none
  transfers between devices with their start and end apart: 8 -> 4, of which waited for: 1 -> 2; matrix products, arithmetic and copies ran while one was open for 63% -> 0% of each run, Pallas kernels for 0% -> 6%
where the time goes in v1:
time: 43.8 us; the launch traced here: 43.5 us
  starting transfers between devices  28.8 us (66%)
  Pallas kernels  8.52 us (19%)
  waiting for transfers between devices  5.44 us (12%)
  between operations  0.74 us (2%)
    ppermute x1, starting transfers between devices, shards(): odd_x = lax.ppermute(odd_x, 'gx', odd)  21.1 us
    ppermute x1, waiting for transfers between devices, shards(): odd_z = lax.ppermute(odd_z, 'gz', odd)  5.36 us
    ppermute x1, starting transfers between devices, shards(): even_z = lax.ppermute(even_z, 'gz', even)  3.24 us
    ppermute x1, starting transfers between devices, shards(): odd_z = lax.ppermute(odd_z, 'gz', odd)  2.52 us
    pallas_call x1, Pallas kernels, shards(): call(volume_kernel, (field_shape(5), unpack, pack, pack), 'volume', 10 ** 9)  2.45 us
    pallas_call x1, Pallas kernels, shards(): call(last_kernel, (whole, whole), 'last', 10 ** 8)  2.44 us
    pallas_call x1, Pallas kernels, shards(): call(first_kernel, (field_shape(5), aux_shape, table, table, table, field...  2.15 us
    ppermute x1, starting transfers between devices, shards(): even_x = lax.ppermute(even_x, 'gx', even)  1.92 us
  transfers between devices with their start and end apart: 4, of which 2 were waited for; matrix products, arithmetic and copies ran while one was open for 0% of the time, Pallas kernels for 6%

profile of v1, /device:TPU:14, one launch (start us, length us, event | category | flops | bytes accessed | tf_op | source)
XLA Modules:
  0.0 43.5 jit_solution(2914219424340158530)
XLA Ops:
  0.6 2.1 %first.1 = (f32[5,48,216]{2,1,0:T(8,128)S(1)}, f32[48,128]{1,0:T(8,128)S(1)}, bf16[3,216,216]{2,1,0:T(8,128)(2,1)S(1)}, bf16[3,216,216]{2,1,0:T(8,128)(2,1)S(1)}...) custom-call(f32[2,5,12,2,216]{4,3,2,1,0:T(2,128)} %bitcast.6, ...), custom_call_target="tpu_custom_call" | custom-call | flops 100000000 | bytes 2000000 | tf_op jit(solution)/shard_map/first/pallas_call | solution.py:626
  2.8 1.9 %collective-permute-start = (f32[72,128]{1,0:T(8,128)S(1)}, f32[72,128]{1,0:T(8,128)S(1)}, u32[]{:S(2)}, u32[]{:S(2)}) collective-permute-start(f32[72,128]{1,0:T(8,128)S(1)} %get-tuple-element.27), channel_id=1, source_target_pairs={{0,8},{8,0},{16,24},{24,16},{32,40},{40,32},{48,56},{56,48},{64,72... | collective-permute-start | bytes 110600 | tf_op jit(solution)/shard_map/ppermute | solution.py:641
  4.7 21.1 %collective-permute-start.1 = (f32[72,128]{1,0:T(8,128)S(1)}, f32[72,128]{1,0:T(8,128)S(1)}, u32[]{:S(2)}, u32[]{:S(2)}) collective-permute-start(f32[72,128]{1,0:T(8,128)S(1)} %get-tuple-element.28), channel_id=1, source_target_pairs={{0,1016},{8,16},{16,8},{24,32},{32,24},{40,48},{48,40},{56,64},{64... | collective-permute-start | bytes 110600 | tf_op jit(solution)/shard_map/ppermute | solution.py:642
  25.8 2.5 %volume.1 = (f32[5,48,216]{2,1,0:T(8,128)S(1)}, bf16[2,3,128,216]{3,2,1,0:T(8,128)(2,1)S(1)}, bf16[2,3,216,128]{3,2,1,0:T(8,128)(2,1)S(1)}, bf16[2,3,216,128]{3,2,1,0:T(8,128)(2,1)S(1)}) custom-call(f32[5,48,216]{2,1,0:T(8,128)S(1)} %get-tuple-element.20.state_ref, f32[48,128]{1,0:T(8,128)S(1)} %get-tuple-element.21.aux_ref, ...), custom_call_target="tpu_custom_call" | custom-call | flops 1000000000 | bytes 2000000 | tf_op jit(solution)/shard_map/volume/pallas_call | solution.py:645
  28.3 0.0 collective-permute-done.even_ref
  28.3 0.0 collective-permute-done.1.odd_ref
  28.3 0.0 copy-start
  28.3 0.0 copy-start.1
  28.3 0.0 copy-start.2
  28.4 0.0 copy-start.3
  28.4 1.5 %second.1 = (f32[9,48,216]{2,1,0:T(8,128)S(1)}, f32[9,48,216]{2,1,0:T(8,128)S(1)}, f32[72,128]{1,0:T(8,128)S(1)}, f32[72,128]{1,0:T(8,128)S(1)}) custom-call(f32[5,48,216]{2,1,0:T(8,128)S(1)} %get-tuple-element.20.state_ref, f32[9,48,216]{2,1,0:T(8,128)S(1)} %get-tuple-element.26.tg_ref, f32[72,128]{1,0:T(8,128)S(1)} %collective-permute-done.even_ref, ...), custom_call_target="tpu_custom_call" | custom-call | flops 100000000 | bytes 2000000 | tf_op jit(solution)/shard_map/second/pallas_call | solution.py:648
  29.8 3.2 %collective-permute-start.2 = (f32[72,128]{1,0:T(8,128)S(1)}, f32[72,128]{1,0:T(8,128)S(1)}, u32[]{:S(2)}, u32[]{:S(2)}) collective-permute-start(f32[72,128]{1,0:T(8,128)S(1)} %get-tuple-element.34), channel_id=1, source_target_pairs={{0,1},{1,0},{2,3},{3,2},{4,5},{5,4},{6,7},{7,6},{8,9},{9,8},{10,11... | collective-permute-start | bytes 110600 | tf_op jit(solution)/shard_map/ppermute | solution.py:652
  33.1 2.5 %collective-permute-start.3 = (f32[72,128]{1,0:T(8,128)S(1)}, f32[72,128]{1,0:T(8,128)S(1)}, u32[]{:S(2)}, u32[]{:S(2)}) collective-permute-start(f32[72,128]{1,0:T(8,128)S(1)} %get-tuple-element.35), channel_id=1, source_target_pairs={{0,7},{1,2},{2,1},{3,4},{4,3},{5,6},{6,5},{7,0},{8,15},{9,10},{10,... | collective-permute-start | bytes 110600 | tf_op jit(solution)/shard_map/ppermute | solution.py:653
  35.6 0.1 collective-permute-done.2.even_ref
  35.7 5.4 %collective-permute-done.3.odd_ref = f32[72,128]{1,0:T(8,128)S(1)} collective-permute-done((f32[72,128]{1,0:T(8,128)S(1)}, f32[72,128]{1,0:T(8,128)S(1)}, u32[]{:S(2)}, u32[]{:S(2)}) %collective-permute-start.3) | collective-permute-done | bytes 36896 | tf_op jit(solution)/shard_map/ppermute | solution.py:653
  41.1 0.0 copy-done
  41.1 0.0 copy-done.1
  41.1 0.0 copy-done.2
  41.1 0.0 copy-done.3
  41.1 2.4 %last.1 = (f32[2,5,12,2,216]{4,3,2,1,0:T(2,128)}, f32[2,5,12,2,216]{4,3,2,1,0:T(2,128)}) custom-call(f32[5,48,216]{2,1,0:T(8,128)S(1)} %get-tuple-element.20.state_ref, f32[2,5,12,2,216]{4,3,2,1,0:T(2,128)S(1)} %bitcast.5, f32[5,48,216]{2,1,0:T(8,128)S(1)} %get-tuple-element.25.vol_ref, f32[9,48,216]{2,1,0:T(8,128)S(1)} %get-tuple-element.32.tg_ref, ...), custom_call_target="tpu_custom_call" | custom-call | flops 100000000 | bytes 2000000 | tf_op jit(solution)/shard_map/last/pallas_call | solution.py:654
Async XLA Ops:
  2.8 25.5 %collective-permute-start = (f32[72,128]{1,0:T(8,128)S(1)}, f32[72,128]{1,0:T(8,128)S(1)}, u32[]{:S(2)}, u32[]{:S(2)}) collective-permute-start(f32[72,128]{1,0:T(8,128)S(1)} %get-tuple-element.27), channel_id=1, source_target_pairs={{0,8},{8,0},{16,24},{24,16},{32,40},{40,32},{48,56},{56,48},{64,72... | collective-permute-start | bytes 110600 | tf_op jit(solution)/shard_map/ppermute | solution.py:641
  4.7 23.6 %collective-permute-start.1 = (f32[72,128]{1,0:T(8,128)S(1)}, f32[72,128]{1,0:T(8,128)S(1)}, u32[]{:S(2)}, u32[]{:S(2)}) collective-permute-start(f32[72,128]{1,0:T(8,128)S(1)} %get-tuple-element.28), channel_id=1, source_target_pairs={{0,1016},{8,16},{16,8},{24,32},{32,24},{40,48},{48,40},{56,64},{64... | collective-permute-start | bytes 110600 | tf_op jit(solution)/shard_map/ppermute | solution.py:642
  28.3 12.7 %copy-start = (bf16[2,3,128,216]{3,2,1,0:T(8,128)(2,1)S(1)}, bf16[2,3,128,216]{3,2,1,0:T(8,128)(2,1)}, u32[]{:S(2)}) copy-start(bf16[2,3,128,216]{3,2,1,0:T(8,128)(2,1)} %constant.9.clone.cu_ref) | copy-start | bytes 995332
  28.3 12.7 %copy-start.1 = (bf16[2,3,128,216]{3,2,1,0:T(8,128)(2,1)S(1)}, bf16[2,3,128,216]{3,2,1,0:T(8,128)(2,1)}, u32[]{:S(2)}) copy-start(bf16[2,3,128,216]{3,2,1,0:T(8,128)(2,1)} %constant.8.clone.uz_ref) | copy-start | bytes 995332
  28.3 12.7 %copy-start.2 = (f32[2,2,5,12,216]{4,1,3,2,0:T(2,128)S(1)}, f32[2,2,5,12,216]{4,1,3,2,0:T(2,128)}, u32[]{:S(2)}) copy-start(f32[2,2,5,12,216]{4,1,3,2,0:T(2,128)} %param.9) | copy-start | bytes 622084
  28.4 12.7 %copy-start.3 = (bf16[2,48,24]{2,1,0:T(8,128)(2,1)S(1)}, bf16[2,48,24]{2,1,0:T(8,128)(2,1)}, u32[]{:S(2)}) copy-start(bf16[2,48,24]{2,1,0:T(8,128)(2,1)} %constant.10.clone.ri_ref) | copy-start | bytes 13828
  29.8 5.9 %collective-permute-start.2 = (f32[72,128]{1,0:T(8,128)S(1)}, f32[72,128]{1,0:T(8,128)S(1)}, u32[]{:S(2)}, u32[]{:S(2)}) collective-permute-start(f32[72,128]{1,0:T(8,128)S(1)} %get-tuple-element.34), channel_id=1, source_target_pairs={{0,1},{1,0},{2,3},{3,2},{4,5},{5,4},{6,7},{7,6},{8,9},{9,8},{10,11... | collective-permute-start | bytes 110600 | tf_op jit(solution)/shard_map/ppermute | solution.py:652
  33.1 8.0 %collective-permute-start.3 = (f32[72,128]{1,0:T(8,128)S(1)}, f32[72,128]{1,0:T(8,128)S(1)}, u32[]{:S(2)}, u32[]{:S(2)}) collective-permute-start(f32[72,128]{1,0:T(8,128)S(1)} %get-tuple-element.35), channel_id=1, source_target_pairs={{0,7},{1,2},{2,1},{3,4},{4,3},{5,6},{6,5},{7,0},{8,15},{9,10},{10,... | collective-permute-start | bytes 110600 | tf_op jit(solution)/shard_map/ppermute | solution.py:653

commit v2 on v1

--- a/solution.py
+++ b/solution.py
@@ -1,4 +1,3 @@
-import functools
 import math
 
 import jax
@@ -8,6 +7,7 @@
 from jax.experimental import pallas as pl
 from jax.experimental.pallas import tpu as pltpu
 from jax.sharding import PartitionSpec as P
+
 
 GAMMA = 1.4
 VISCOSITY = 0.001
@@ -19,6 +19,7 @@
 SECTION_B = 0.3792103129
 HALF_W = 7.5
 
+
 ROWS, NODES = (48, 216)
 F32, BF16 = (jnp.float32, jnp.bfloat16)
 
@@ -51,65 +52,45 @@
     return np.stack(rows).astype(np.float32)
 
 
-def tables():
-    nodes = np.arange(NODES)
-    low_face = nodes[nodes % 6 == 0]
-    unpack = np.zeros((2, 3, 128, NODES), np.float32)
-    corner_unpack = np.zeros((2, 3, 128, NODES), np.float32)
-    for j in range(3):
-        slot = 36 * j + np.arange(36)
-        unpack[0, j, slot, low_face] = 1.0
-        unpack[1, j, slot, low_face + 5] = 1.0
-        for iy in range(6):
-            slot = 108 + 6 * j + iy
-            for ix in (0, 5):
-                base = 36 * ix + 6 * iy
-                corner_unpack[0, j, slot, base] = 1.0
-                corner_unpack[1, j, slot, base + 5] = 1.0
-    return dict(uz=unpack.astype(jnp.bfloat16), cu=corner_unpack.astype(jnp.bfloat16))
-
-
-def one_hot(source, depth):
-    rows = lax.broadcasted_iota(jnp.int32, (depth, source.shape[1]), 0)
-    return jnp.where(rows == source, 1.0, 0.0).astype(BF16)
-
-
-def x_pack_table(side, j):
-    lane = lax.broadcasted_iota(jnp.int32, (1, 128), 1) - 36 * j
-    inside = jnp.logical_and(lane >= 0, lane < 36)
-    return one_hot(jnp.where(inside, lane + (180 if side == 0 else 0), -1), NODES)
-
-
-def x_unpack_table(side, j):
-    lane = lax.broadcasted_iota(jnp.int32, (1, NODES), 1) - (0 if side == 0 else 180)
-    inside = jnp.logical_and(lane >= 0, lane < 36)
-    return one_hot(jnp.where(inside, lane + 36 * j, -1), 128)
-
-
-def z_pack_table(side, j):
-    lane = lax.broadcasted_iota(jnp.int32, (1, 128), 1) - 36 * j
-    inside = jnp.logical_and(lane >= 0, lane < 36)
-    return one_hot(jnp.where(inside, 6 * lane + (5 if side == 0 else 0), -1), NODES)
-
-
-def corner_pack_table(side, j):
-    lane = lax.broadcasted_iota(jnp.int32, (1, 128), 1) - (108 + 6 * j)
-    inside = jnp.logical_and(lane >= 0, lane < 6)
-    source = jnp.where(inside, 6 * lane + (5 if side == 0 else 0), -1000)
-    return one_hot(source, NODES) + one_hot(source + 180, NODES)
-
-
-def pick_table(side):
-    row = lax.broadcasted_iota(jnp.int32, (24, ROWS), 0)
-    column = lax.broadcasted_iota(jnp.int32, (24, ROWS), 1)
-    return jnp.where(column == 2 * row + (1 - side), 1.0, 0.0).astype(BF16)
+def hot(sources, depth):
+    rows = lax.broadcasted_iota(jnp.int32, (depth, sources[0].shape[1]), 0)
+    found = rows == sources[0]
+    for source in sources[1:]:
+        found = jnp.logical_or(found, rows == source)
+    return jnp.where(found, 1.0, 0.0).astype(BF16)
+
+
+def slot_lane(first, width):
+    lane = lax.broadcasted_iota(jnp.int32, (1, 128), 1) - first
+    return jnp.where(jnp.logical_and(lane >= 0, lane < width), lane, -1000)
+
+
+def pack_table(d, j):
+    node = slot_lane(36 * j, 36) * (1 if d == 0 else 6)
+    return hot([node, node + 5 * STRIDE[d]], NODES)
+
+
+def unpack_table(lanes, d, j):
+    node = lax.broadcasted_iota(jnp.int32, (1, NODES), 1)
+    face = (node % 36) if d == 0 else node // 6
+    return hot([jnp.where(lanes.face[d], 36 * j + face, -1)], 128)
+
+
+def edge_pack_table(j):
+    node = 6 * slot_lane(108 + 6 * j, 6)
+    return hot([node, node + 5, node + 180, node + 185], NODES)
+
+
+def edge_unpack_table(lanes, j):
+    edge = jnp.logical_and(lanes.face[0], lanes.face[2])
+    return hot([jnp.where(edge, 108 + 6 * j + lanes.place[1], -1)], 128)
 
 
 def swap_table(lanes, d):
     lane = lax.broadcasted_iota(jnp.int32, (1, NODES), 1)
     step = 5 * STRIDE[d]
-    return one_hot(
-        jnp.where(lanes.lo[d], lane + step, jnp.where(lanes.hi[d], lane - step, -1)), NODES
+    return hot(
+        [jnp.where(lanes.lo[d], lane + step, jnp.where(lanes.hi[d], lane - step, -1))], NODES
     )
 
 
@@ -283,13 +264,20 @@
     return [f + d for f, d in zip(flux, change)]
 
 
-def pack_faces(fields, table_of, side):
+def pack_faces(fields, table_of):
     total = None
     for j in range(3):
-        part = halves(stack([fields[3 * s + j] for s in range(3)]))
-        value = move(part, table_of(side, j))
+        value = move(halves(stack([fields[3 * s + j] for s in range(3)])), table_of(j))
         total = value if total is None else total + value
     return total
+
+
+def edge_rows(fields, table_of):
+    edges = move(halves(stack([fields[0], fields[3]])), table_of(0))
+    first = edges[0:48]
+    for j in (1, 2):
+        first = first + move(halves(fields[j]), table_of(j))
+    return stack([first, edges[48:96]])
 
 
 def euler(rho, vel, pres, direction):
@@ -319,12 +307,36 @@
     ]
 
 
+def period_of(size):
+    return 32 if size % 32 == 0 else size
+
+
+def sends_late():
+    period = period_of(lax.axis_size("gx"))
+    return lax.rem(lax.axis_index("gx"), period) == period - 1
+
+
+def is_device(gx, gz):
+    return jnp.logical_and(lax.axis_index("gx") == gx, lax.axis_index("gz") == gz)
+
+
+def hears_late():
+    first = lax.rem(lax.axis_index("gx"), period_of(lax.axis_size("gx"))) == 0
+    return jnp.logical_or(first, is_device(1, 0))
+
+
+def ends_late():
+    period = period_of(lax.axis_size("gx"))
+    pair = lax.rem(lax.axis_index("gx"), period) >= period - 2
+    return jnp.logical_or(pair, is_device(0, 0))
+
+
 def parity_of(axis):
     return lax.rem(lax.axis_index(axis), 2) == 0
 
 
 def first_kernel(state_hbm, mask_hbm, h_hbm, coef_hbm, st_ref, aux_ref, dh_ref, dl_ref, sw_ref, tg_ref,
-                 even_ref, odd_ref, state_buf, mask_buf, h_buf, coef_buf, sems):
+                 even_ref, odd_ref, turn_1, turn_2, turn_3, edge_ref, upper_ref, state_buf, mask_buf, h_buf, coef_buf, face_buf, sems):
     copies = [
         pltpu.make_async_copy(src, dst, sems.at[i])
         for i, (src, dst) in enumerate(
@@ -355,6 +367,9 @@
         jnp.where(slot == 1, jnp.where(wall_hi, 1.0, 0.0), sy),
     )
     own = vel + [temp]
+    keep = jnp.logical_and(lanes.ghost_x, lanes.ghost_z)
+    edges = edge_rows([jnp.where(keep, f, 0.0) for f in own], edge_pack_table)
+    edge_ref[...] = stack([edges[24:48], edges[72:96]])
     pair = halves(stack(own))
     scales = (SCALE_X, sy, SCALE_Z)
     grads = []
@@ -376,18 +391,27 @@
     for i in range(9):
         tg_ref[i] = tg[i]
     fields = [rho] + own + flux_of(tg, vel, 0)
-    up = pack_faces([f[24:48] for f in fields], x_pack_table, 0)
-    down = pack_faces([f[0:24] for f in fields], x_pack_table, 1)
-    even = parity_of("gx")
+    fields = [jnp.where(lanes.hi[0], f[24:48], 0.0) for f in fields]
+    upper_ref[...] = pack_faces(fields, lambda j: pack_table(0, j))
+    fields = [rho] + own + flux_of(tg, vel, 2)
+    fields = [jnp.where(lanes.ghost_z, f, 0.0) for f in fields]
+    face_buf[...] = pack_faces(fields, lambda j: pack_table(2, j))
+    down = face_buf[pl.ds(0, 72, stride=2), :]
+    up = face_buf[pl.ds(1, 72, stride=2), :]
+    even = parity_of("gz")
     even_ref[...] = jnp.where(even, up, down)
     odd_ref[...] = jnp.where(even, down, up)
+    for ref, turn in zip((turn_1, turn_2, turn_3), turns_of(lax.axis_size("gz"))):
+        ref[...] = jnp.where(among(lax.axis_index("gz"), turn), up, down)
 
 
 def aux_of(aux_ref):
     return (aux_ref[:, 0:1] > 0.5, aux_ref[:, 1:2] > 0.5, aux_ref[:, 2:3])
 
 
-def volume_kernel(state_ref, aux_ref, dh_ref, dl_ref, sw_ref, out_ref, ux_ref, pz_ref, cp_ref):
+def volume(reg_hbm, state_ref, aux_ref, dh_ref, dl_ref, sw_ref, out_ref, reg_buf, sem):
+    copy = pltpu.make_async_copy(reg_hbm, reg_buf, sem)
+    copy.start()
     lanes = Lanes()
     rho, mom, energy, vel, pres, temp, inv = load_prims(state_ref)
     wall_lo, wall_hi, sy = aux_of(aux_ref)
@@ -439,112 +463,139 @@
         for i in range(5):
             value = faces[i] - scales[d] * parts[i]
             total[i] = value if d == 0 else total[i] + value
+    copy.wait()
     for i in range(5):
-        out_ref[i] = total[i]
-    for side in range(2):
-        for j in range(3):
-            ux_ref[side, j] = x_unpack_table(side, j)
-            pz_ref[side, j] = z_pack_table(side, j)
-            cp_ref[side, j] = corner_pack_table(side, j)
-
-
-def sides_of(even_ref, odd_ref, axis):
+        out_ref[i] = SECTION_A * read_rows(reg_buf, i) + TIME_STEP * total[i]
+
+
+def starts_late():
+    return jnp.logical_or(sends_late(), is_device(0, 0))
+
+
+def volume_kernel(reg_hbm, state_ref, aux_ref, dh_ref, dl_ref, sw_ref,
+                  out_ref, uz_ref, px_ref, ep_ref, ux_ref, eu_ref, reg_buf, sem):
+    lanes = Lanes()
+    for j in range(3):
+        uz_ref[j] = unpack_table(lanes, 2, j)
+        px_ref[j] = pack_table(0, j)
+        ep_ref[j] = edge_pack_table(j)
+        ux_ref[j] = unpack_table(lanes, 0, j)
+        eu_ref[j] = edge_unpack_table(lanes, j)
+
+    @pl.when(jnp.logical_not(starts_late()))
+    def _():
+        volume(reg_hbm, state_ref, aux_ref, dh_ref, dl_ref, sw_ref, out_ref, reg_buf, sem)
+
+
+def sides_of(from_even, from_odd, axis):
     even = parity_of(axis)
-    return (
-        jnp.where(even, odd_ref[...], even_ref[...]),
-        jnp.where(even, even_ref[...], odd_ref[...]),
-    )
-
-
-def unpack_faces(lower, upper, table_ref, spread):
-    first, second = (halves(lower), halves(upper))
+    return (jnp.where(even, from_odd, from_even), jnp.where(even, from_even, from_odd))
+
+
+def unpack_faces(pair, table_ref, keep):
     fields = [None] * 9
     for j in range(3):
-        low = rows_of(move(first, table_ref[0, j]), 3, 24)
-        high = rows_of(move(second, table_ref[1, j]), 3, 24)
-        for s in range(3):
-            fields[3 * s + j] = spread(low[s], high[s])
+        for s, value in enumerate(rows_of(move(pair, table_ref[j]), 3)):
+            fields[3 * s + j] = jnp.where(keep, value, 0.0)
     return fields
 
 
-def second_kernel(state_ref, tg_ref, even_ref, odd_ref, ux_ref, pz_ref, cp_ref,
-                  tgo_ref, gx_ref, even_out, odd_out):
-    lanes = Lanes()
+def complete_z(lanes, state_ref, tg_ref, lower, upper, uz_ref, px_ref, ep_ref, face_buf):
     rho, _, _, vel, _, temp, _ = load_prims(state_ref)
     own = vel + [temp]
-    lower, upper = sides_of(even_ref, odd_ref, "gx")
-    ghost = unpack_faces(lower, upper, ux_ref, lambda lo, hi: stack([lo, hi]))
-    weight = (SCALE_X * HALF_W) * lanes.sig[0] * jnp.where(lanes.ghost_x, 1.0, 0.0)
+    face_buf[pl.ds(0, 72, stride=2), :] = lower
+    face_buf[pl.ds(1, 72, stride=2), :] = upper
+    ghost = unpack_faces(halves(face_buf[...]), uz_ref, lanes.ghost_z)
+    weight = jnp.where(lanes.ghost_z, (SCALE_Z * HALF_W) * lanes.sig[2], 0.0)
     delta = [weight * (o - g) for o, g in zip(own, ghost[1:5])]
-    tg = add_lift([tg_ref[i] for i in range(9)], delta, 0)
-    for i in range(9):
-        tgo_ref[i] = tg[i]
-    flux = ghost_lift(ghost[5:9], ghost[1:4], delta, 0, 0)
-    for i, field in enumerate(ghost[:5] + flux):
-        gx_ref[i] = field
-    fields = [rho] + own + flux_of(tg, vel, 2)
-    corner = [jnp.where(lanes.ghost_x, g, 0.0) for g in ghost[1:5]]
-    messages = []
-    for side in (0, 1):
-        total = None
-        for j in range(3):
-            picked = [fields[3 * s + j] for s in range(3)]
-            part = move(halves(stack(picked)), pz_ref[side, j])
-            total = part if total is None else total + part
-        edges = move(halves(stack([corner[0], corner[3]])), cp_ref[side, 0])
-        first = edges[0:48]
-        for j in (1, 2):
-            first = first + move(halves(corner[j]), cp_ref[side, j])
-        total = total + stack([first, edges[48:96], jnp.zeros((ROWS, 128), F32)])
-        pick = pick_table(side)
-        kept = []
-        for s in range(3):
-            high, low = halves(total[48 * s : 48 * s + 48])
-            kept.append(dot(pick, high) + dot(pick, low))
-        messages.append(stack(kept))
-    even = parity_of("gz")
-    even_out[...] = jnp.where(even, messages[0], messages[1])
-    odd_out[...] = jnp.where(even, messages[1], messages[0])
-
-
-def last_kernel(state_ref, reg_ref, vol_ref, tg_ref, gx_ref, aux_ref, even_ref, odd_ref,
-                dh_ref, dl_ref, sw_ref, uz_ref, cu_ref, ri_ref, state_out, reg_out):
+    tg = add_lift([tg_ref[i] for i in range(9)], delta, 2)
+    flux = ghost_lift(ghost[5:9], ghost[1:4], delta, 2, 2)
+    fields = [rho] + own + flux_of(tg, vel, 0)
+    fields = [jnp.where(lanes.ghost_x, f, 0.0) for f in fields]
+    total = pack_faces(fields, lambda j: px_ref[j])
+    edges = edge_rows([jnp.where(lanes.ghost_x, g, 0.0) for g in ghost[1:5]], lambda j: ep_ref[j])
+    total = total + stack([edges, jnp.zeros((ROWS, 128), F32)])
+    down = stack([total[48 * s : 48 * s + 24] for s in range(3)])
+    up = stack([total[48 * s + 24 : 48 * s + 48] for s in range(3)])
+    return (own, tg, ghost[:5] + flux, up, down)
+
+
+def second_kernel(state_ref, tg_ref, turn_1, turn_2, turn_3, uz_ref, px_ref, ep_ref,
+                  tgo_ref, gz_ref, even_out, odd_out, face_buf):
+    @pl.when(jnp.logical_not(sends_late()))
+    def _():
+        lower, upper = (jnp.zeros((72, 128), F32), jnp.zeros((72, 128), F32))
+        for ref, turn in zip((turn_1, turn_2, turn_3), turns_of(lax.axis_size("gz"))):
+            above = among(lax.axis_index("gz"), turn)
+            upper = upper + jnp.where(above, ref[...], 0.0)
+            lower = lower + jnp.where(above, 0.0, ref[...])
+        _, tg, ghost, up, down = complete_z(Lanes(), state_ref, tg_ref, lower, upper, uz_ref, px_ref, ep_ref, face_buf)
+        for i in range(9):
+            tgo_ref[i] = tg[i]
+            gz_ref[i] = ghost[i]
+        even = parity_of("gx")
+        even_out[...] = jnp.where(even, up, down)
+        odd_out[...] = jnp.where(even, down, up)
+
+
+def third_kernel(state_ref, tg_first_ref, tg_ref, gz_ref, mine_ref, even_ref, odd_ref,
+                 uz_ref, px_ref, ep_ref, tgo_ref, gzo_ref, even_out, face_buf):
+    late = sends_late()
+
+    @pl.when(late)
+    def _():
+        lanes = Lanes()
+        lower, upper = sides_of(even_ref[...], odd_ref[...], "gz")
+        _, tg, ghost, up, down = complete_z(
+            lanes, state_ref, tg_first_ref, lower, upper, uz_ref, px_ref, ep_ref, face_buf
+        )
+        for i in range(9):
+            tgo_ref[i] = tg[i]
+            gzo_ref[i] = ghost[i]
+        even_out[...] = jnp.where(parity_of("gx"), up, down)
+
+    @pl.when(jnp.logical_not(late))
+    def _():
+        tgo_ref[...] = tg_ref[...]
+        gzo_ref[...] = gz_ref[...]
+        even_out[...] = mine_ref[...]
+
+
+def finish(from_even, vol_ref, state_ref, tg_ref, gz_ref, aux_ref, odd_ref, up_ref,
+           below_ref, above_ref, dh_ref, dl_ref, sw_ref, ux_ref, eu_ref,
+           state_hbm, reg_hbm, state_out, reg_out, sems):
     lanes = Lanes()
     rho, mom, energy, vel, _, temp, _ = load_prims(state_ref)
     wall_lo, wall_hi, sy = aux_of(aux_ref)
     scales = (SCALE_X, sy, SCALE_Z)
     own = vel + [temp]
-    lower, upper = sides_of(even_ref, odd_ref, "gz")
-
-    def widen(value, side):
-        put = ri_ref[side]
-        parts = []
-        for s in range(3):
-            high, low = halves(value[24 * s : 24 * s + 24, :])
-            parts.append(dot(put, high) + dot(put, low))
-        return stack(parts)
-
-    first, second = (halves(widen(lower, 0)), halves(widen(upper, 1)))
-    ghost_z = [None] * 9
-    corner = [None] * 4
-    for j in range(3):
-        value = rows_of(move(first, uz_ref[0, j]) + move(second, uz_ref[1, j]), 3)
-        edge = rows_of(move(first, cu_ref[0, j]) + move(second, cu_ref[1, j]), 3)
-        for s in range(3):
-            ghost_z[3 * s + j] = value[s]
-        corner[j] = edge[0]
-        if j == 0:
-            corner[3] = edge[1]
-    keep_x = jnp.where(lanes.ghost_x, 1.0, 0.0)
-    keep_z = jnp.where(lanes.ghost_z, 1.0, 0.0)
-    ghost_x = [gx_ref[i] for i in range(9)]
-    weight = (SCALE_Z * HALF_W) * lanes.sig[2] * keep_z
-    delta = [weight * (o - g) for o, g in zip(own, ghost_z[1:5])]
-    tg = add_lift([tg_ref[i] for i in range(9)], delta, 2)
-    flux_z = ghost_lift(ghost_z[5:9], ghost_z[1:4], delta, 2, 2)
-    edge_delta = [(weight * keep_x) * (g - c) for g, c in zip(ghost_x[1:5], corner)]
-    flux_x = ghost_lift(ghost_x[5:9], ghost_x[1:4], edge_delta, 0, 2)
-    total = [vol_ref[i] for i in range(5)]
+    lower, upper = sides_of(from_even, odd_ref[...], "gx")
+    lower = lower + up_ref[...]
+    late = hears_late()
+    row = lax.broadcasted_iota(jnp.int32, (48, 128), 0)
+    slot = lax.broadcasted_iota(jnp.int32, (48, 128), 1)
+    direct = jnp.where(row % 2 == 0, shift(below_ref[...], -1), shift(above_ref[...], 1))
+    edge_slot = jnp.where(late, slot, 0) >= 108
+    lower = stack([jnp.where(edge_slot, direct, lower[0:48]), lower[48:72]])
+    pair = halves(
+        stack([side[24 * s : 24 * s + 24] for s in range(3) for side in (lower, upper)])
+    )
+    ghost_x = unpack_faces(pair, ux_ref, lanes.ghost_x)
+    edge = [rows_of(move(pair, eu_ref[j]), 3) for j in range(3)]
+    edge = [edge[0][0], edge[1][0], edge[2][0], edge[0][1]]
+    ghost_z = [gz_ref[i] for i in range(9)]
+    weight = jnp.where(lanes.ghost_x, (SCALE_X * HALF_W) * lanes.sig[0], 0.0)
+    delta = [weight * (o - g) for o, g in zip(own, ghost_x[1:5])]
+    tg = add_lift([tg_ref[i] for i in range(9)], delta, 0)
+    flux_x = ghost_lift(ghost_x[5:9], ghost_x[1:4], delta, 0, 0)
+    weight = jnp.where(lanes.ghost_z, weight, 0.0)
+    edge_delta = [weight * (g - e) for g, e in zip(ghost_z[1:5], edge)]
+    flux_z = ghost_lift(ghost_z[5:9], ghost_z[1:4], edge_delta, 2, 0)
+    weight = jnp.where(lanes.ghost_z, (SCALE_Z * HALF_W) * lanes.sig[2], 0.0)
+    weight = jnp.where(jnp.logical_and(lanes.ghost_x, jnp.where(late, lanes.a, 1) == 0), weight, 0.0)
+    edge_delta = [weight * (g - e) for g, e in zip(ghost_x[1:5], edge)]
+    flux_x = ghost_lift(flux_x, ghost_x[1:4], edge_delta, 0, 2)
+    total = [0.0] * 5
     for d, ghost, keep in ((0, ghost_x, lanes.ghost_x), (2, ghost_z, lanes.ghost_z)):
         out = [jnp.where(keep, g, o) for g, o in zip(ghost[:5], [rho] + own)]
         faces = face_terms(
@@ -567,17 +618,43 @@
                 slope[i] + (HALF_W * lanes.sig[d]) * (flux[i] - out)
             )
     for i, field in enumerate([rho] + mom + [energy]):
-        reg = SECTION_A * read_rows(reg_ref, i) + TIME_STEP * total[i]
+        reg = vol_ref[i] + TIME_STEP * total[i]
         write_rows(reg_out, i, reg)
         write_rows(state_out, i, field + SECTION_B * reg)
-
-
-def row_table():
-    put = np.zeros((2, ROWS, 24), np.float32)
-    for i in range(24):
-        put[0, 2 * i, i] = 1.0
-        put[1, 2 * i + 1, i] = 1.0
-    return put.astype(jnp.bfloat16)
+    copies = [
+        pltpu.make_async_copy(reg_out, reg_hbm, sems.at[0]),
+        pltpu.make_async_copy(state_out, state_hbm, sems.at[1]),
+    ]
+    for copy in copies:
+        copy.start()
+    for copy in copies:
+        copy.wait()
+
+
+def last_a_kernel(even_ref, vol_ref, *refs):
+    @pl.when(jnp.logical_not(ends_late()))
+    def _():
+        finish(even_ref[...], vol_ref, *refs)
+
+
+def last_b_kernel(state_in, reg_in, register_hbm, even_a_ref, even_b_ref, vol_ref, state_ref, tg_ref, gz_ref,
+                  aux_ref, odd_ref, up_ref, below_ref, above_ref, dh_ref, dl_ref, sw_ref, *refs):
+    vol_buf, reg_buf, sem = refs[-3:]
+
+    @pl.when(ends_late())
+    def _():
+        @pl.when(starts_late())
+        def _():
+            volume(register_hbm, state_ref, aux_ref, dh_ref, dl_ref, sw_ref, vol_buf, reg_buf, sem)
+
+        @pl.when(jnp.logical_not(starts_late()))
+        def _():
+            vol_buf[...] = vol_ref[...]
+
+        finish(
+            even_a_ref[...] + even_b_ref[...], vol_buf, state_ref, tg_ref, gz_ref, aux_ref, odd_ref,
+            up_ref, below_ref, above_ref, dh_ref, dl_ref, sw_ref, *refs[:-3],
+        )
 
 
 def field_shape(count):
@@ -588,27 +665,43 @@
 FACE = jax.ShapeDtypeStruct((72, 128), F32)
 
 
-def call(kernel, outs, name, flops, **more):
+def call(kernel, outs, flops, **more):
     return pl.pallas_call(
         kernel,
         out_shape=outs,
-        name=name,
         compiler_params=pltpu.CompilerParams(vmem_limit_bytes=LIMIT),
         cost_estimate=pl.CostEstimate(flops=flops, bytes_accessed=2_000_000, transcendentals=0),
         **more,
     )
 
 
-def swap_pairs(axis):
-    size = lax.axis_size(axis)
-    even = [(i, i ^ 1) for i in range(size)]
-    odd = [(i, (i + 1) % size if i % 2 else (i - 1) % size) for i in range(size)]
-    return (even, odd)
+def send(value, partner):
+    nx, nz = (lax.axis_size("gx"), lax.axis_size("gz"))
+    pairs = []
+    for i in range(nx):
+        for j in range(nz):
+            to = partner(i, j)
+            if to is not None:
+                pairs.append((i * nz + j, (to[0] % nx) * nz + to[1] % nz))
+    return lax.ppermute(value, ("gx", "gz"), pairs)
+
+
+def odd_partner(i):
+    return i + 1 if i % 2 else i - 1
+
+
+def turns_of(size):
+    return {8: ((1, 3, 6), (2, 4, 7), (0, 5)), 4: ((1,), (3,), (0, 2))}[size]
+
+
+def among(position, members):
+    found = position == members[0]
+    for member in members[1:]:
+        found = jnp.logical_or(found, position == member)
+    return found
 
 
 def shards(state, register, heights, solid_wall_mask):
-    t = {key: jnp.asarray(value) for key, value in tables().items()}
-    put = jnp.asarray(row_table())
     coef = jnp.asarray(coefficients())
     h = heights.reshape(1, 12)
 
@@ -618,15 +711,15 @@
     def unrows(array):
         return jnp.transpose(array, (0, 3, 1, 2, 4))
 
-    reg = rows(register)
+    reg = pltpu.with_memory_space_constraint(rows(register), pltpu.HBM)
     whole = jax.ShapeDtypeStruct((2, 5, 12, 2, NODES), F32)
     table = jax.ShapeDtypeStruct((3, NODES, NODES), BF16)
     aux_shape = jax.ShapeDtypeStruct((ROWS, 128), F32)
     hbm = pl.BlockSpec(memory_space=pltpu.HBM)
-    st, aux, dh, dl, sw, tg, even_x, odd_x = call(
+    edge_shape = jax.ShapeDtypeStruct((48, 128), F32)
+    st, aux, dh, dl, sw, tg_first, even_z, odd_z, *turns_z, edge, up_x = call(
         first_kernel,
-        (field_shape(5), aux_shape, table, table, table, field_shape(9), FACE, FACE),
-        "first",
+        (field_shape(5), aux_shape, table, table, table, field_shape(9), *[FACE] * 5, edge_shape, FACE),
         10**8,
         in_specs=[hbm] * 4,
         scratch_shapes=[
@@ -634,31 +727,69 @@
             pltpu.VMEM((2, 2, 11), jnp.int32),
             pltpu.VMEM((1, 12), F32),
             pltpu.VMEM((18, NODES), F32),
+            pltpu.VMEM((144, 128), F32),
             pltpu.SemaphoreType.DMA((4,)),
         ],
     )(*[pltpu.with_memory_space_constraint(v, pltpu.HBM) for v in (rows(state), solid_wall_mask, h, coef)])
-    even, odd = swap_pairs("gx")
-    even_x = lax.ppermute(even_x, "gx", even)
-    odd_x = lax.ppermute(odd_x, "gx", odd)
-    pack = jax.ShapeDtypeStruct((2, 3, NODES, 128), BF16)
-    unpack = jax.ShapeDtypeStruct((2, 3, 128, NODES), BF16)
-    vol, ux, pz, cp = call(
-        volume_kernel, (field_shape(5), unpack, pack, pack), "volume", 10**9
-    )(st, aux, dh, dl, sw)
-    tg, gx, even_z, odd_z = call(
-        second_kernel, (field_shape(9), field_shape(9), FACE, FACE), "second", 10**8
-    )(st, tg, even_x, odd_x, ux, pz, cp)
-    even, odd = swap_pairs("gz")
-    even_z = lax.ppermute(even_z, "gz", even)
-    odd_z = lax.ppermute(odd_z, "gz", odd)
-    state_next, reg_next = call(last_kernel, (whole, whole), "last", 10**8)(
-        st, reg, vol, tg, gx, aux, even_z, odd_z, dh, dl, sw, t["uz"], t["cu"], put,
-    )
+    period = period_of(lax.axis_size("gx"))
+    late = lambda i: i % period == period - 1
+    ok = lambda flag, to: to if flag else None
+    origin = lambda i, j: i == 0 and j == 0
+    beside = lambda i, j: i == 1 and j == 0
+    last_z = lax.axis_size("gz") - 1
+    below = send(edge, lambda i, j: ok(late(i) or (i == 0 and j == last_z), (i + 1, j + 1)))
+    above = send(edge, lambda i, j: ok(late(i) or (i == 0 and j == 1), (i + 1, j - 1)))
+    up_x = send(up_x, lambda i, j: ok(late(i) or origin(i, j), (i + 1, j)))
+    za = []
+    for n, turn in enumerate(turns_of(last_z + 1)):
+        to = {j: (j + 1) % (last_z + 1) for j in turn}
+        to.update({v: k for k, v in to.items()})
+        za.append(send(turns_z[n], lambda i, j: ok(j in to and not late(i), (i, to.get(j)))))
+    pack = jax.ShapeDtypeStruct((3, NODES, 128), BF16)
+    unpack = jax.ShapeDtypeStruct((3, 128, NODES), BF16)
+    vmem = pl.BlockSpec(memory_space=pltpu.VMEM)
+    block = pltpu.VMEM((2, 5, 12, 2, NODES), F32)
+    vol, uz, px, ep, ux, eu = call(
+        volume_kernel,
+        (field_shape(5), unpack, pack, pack, unpack, unpack),
+        10**6,
+        in_specs=[hbm] + [vmem] * 5,
+        scratch_shapes=[block, pltpu.SemaphoreType.DMA],
+    )(reg, st, aux, dh, dl, sw)
+    face_buf = [pltpu.VMEM((144, 128), F32)]
+    tg, gz, even_x, odd_x = call(
+        second_kernel, (field_shape(9), field_shape(9), FACE, FACE), 10**8, scratch_shapes=face_buf
+    )(st, tg_first, *za, uz, px, ep)
+    early = lambda i: not (late(i) or late(i ^ 1))
+    apart = lambda i, j: i < 2 and j == 0
+    xa_even = send(even_x, lambda i, j: ok(early(i) and not apart(i, j), (i ^ 1, j)))
+    x_odd = send(odd_x, lambda i, j: ok(not late(i), (odd_partner(i), j)))
+    zb_even = send(even_z, lambda i, j: ok(late(i), (i, j ^ 1)))
+    zb_odd = send(odd_z, lambda i, j: ok(late(i), (i, odd_partner(j))))
+    tg, gz, even_x = call(
+        third_kernel, (field_shape(9), field_shape(9), FACE), 10**8, scratch_shapes=face_buf
+    )(st, tg_first, tg, gz, even_x, zb_even, zb_odd, uz, px, ep)
+    rest = (vol, st, tg, gz, aux, x_odd, up_x, below, above, dh, dl, sw, ux, eu)
+    buffers = [block, block, pltpu.SemaphoreType.DMA((2,))]
+    outs = call(
+        last_a_kernel, (whole, whole), 10**8, in_specs=[vmem] * 15, out_specs=[hbm, hbm], scratch_shapes=buffers
+    )(xa_even, *rest)
+    xb_even = send(even_x, lambda i, j: ok(not early(i) or beside(i, j), (i ^ 1, j)))
+    state_next, reg_next = call(
+        last_b_kernel,
+        (whole, whole),
+        10**8,
+        in_specs=[hbm] * 3 + [vmem] * 16,
+        out_specs=[hbm, hbm],
+        scratch_shapes=buffers + [pltpu.VMEM((5, ROWS, NODES), F32), block, pltpu.SemaphoreType.DMA],
+        input_output_aliases={0: 0, 1: 1},
+    )(*outs, reg, xa_even, xb_even, *rest)
     return (unrows(state_next), unrows(reg_next))
 
 
 def solution(mesh):
     spec = P("gx", "gz", None, None, None)
+
     return jax.shard_map(
         shards,
         mesh=mesh,

time: 43.8 us -> 52.4 us (1.20)
  waiting for transfers between devices: 5.44 us -> 11.3 us
  starting transfers between devices: 28.8 us -> 31.2 us
    ppermute x4 -> x11, waiting for transfers between devices: 5.44 us -> 11.3 us  [send(): return lax.ppermute(value, ('gx', 'gz'), pairs)]
    ppermute x4 -> x11, starting transfers between devices: 28.8 us -> 31.2 us  [send(): return lax.ppermute(value, ('gx', 'gz'), pairs)]
    pallas_call x3 -> x5, Pallas kernels: 6.37 us -> 6.28 us  [the longest x1 3.14 us: shards(): call(volume_kernel, (field_shape(5), unpack, pack, pack, unpack, unpack),...]
  transfers between devices with their start and end apart: 4 -> 11, of which waited for: 2 -> 1; matrix products, arithmetic and copies ran while one was open for 0% -> 0% of each run, Pallas kernels for 6% -> 12%
where the time goes in v2:
time: 52.4 us; the launch traced here: 52.1 us
  starting transfers between devices  31.2 us (60%)
  waiting for transfers between devices  11.3 us (22%)
  Pallas kernels  8.8 us (17%)
  between operations  0.81 us (2%)
    ppermute x11, starting transfers between devices, send(): return lax.ppermute(value, ('gx', 'gz'), pairs)  31.2 us
    ppermute x11, waiting for transfers between devices, send(): return lax.ppermute(value, ('gx', 'gz'), pairs)  11.3 us
    pallas_call x1, Pallas kernels, shards(): call(volume_kernel, (field_shape(5), unpack, pack, pack, unpack, unpack),...  3.14 us
    pallas_call x1, Pallas kernels, shards(): call(first_kernel, (field_shape(5), aux_shape, table, table, table, field...  2.51 us
    pallas_call x1, Pallas kernels, shards(): call(last_a_kernel, (whole, whole), 10 ** 8, in_specs=[vmem] * 15, out_sp...  2.26 us
  transfers between devices with their start and end apart: 11, of which 1 were waited for; matrix products, arithmetic and copies ran while one was open for 0% of the time, Pallas kernels for 12%

profile of v2, /device:TPU:14, one launch (start us, length us, event | category | flops | bytes accessed | tf_op | source)
XLA Modules:
  0.0 52.1 jit_solution(15037685503664324519)
XLA Ops:
  0.6 2.5 %shard_map.68 = (f32[5,48,216]{2,1,0:T(8,128)S(1)}, f32[48,128]{1,0:T(8,128)S(1)}, bf16[3,216,216]{2,1,0:T(8,128)(2,1)S(1)}, bf16[3,216,216]{2,1,0:T(8,128)(2,1)...) custom-call(f32[2,5,12,2,216]{4,3,2,1,0:T(2,128)} %bitcast.9, ...), custom_call_target="tpu_custom_call" | custom-call | flops 100000000 | bytes 2000000 | tf_op jit(solution)/shard_map/pallas_call | solution.py:720
  3.2 2.4 %collective-permute-start = (f32[72,128]{1,0:T(8,128)S(1)}, f32[72,128]{1,0:T(8,128)S(1)}, u32[]{:S(2)}, u32[]{:S(2)}) collective-permute-start(f32[72,128]{1,0:T(8,128)S(1)} %get-tuple-element.34), channel_id=1, source_target_pairs={{1,2},{2,1},{3,4},{4,3},{6,7},{7,6},{9,10},{10,9},{11,12},{12,11},... | collective-permute-start | bytes 110600 | tf_op jit(solution)/shard_map/ppermute | solution.py:686
  5.5 13.2 %collective-permute-start.1 = (f32[72,128]{1,0:T(8,128)S(1)}, f32[72,128]{1,0:T(8,128)S(1)}, u32[]{:S(2)}, u32[]{:S(2)}) collective-permute-start(f32[72,128]{1,0:T(8,128)S(1)} %get-tuple-element.35), channel_id=1, source_target_pairs={{0,7},{2,3},{3,2},{4,5},{5,4},{7,0},{8,15},{10,11},{11,10},{12,13}... | collective-permute-start | bytes 110600 | tf_op jit(solution)/shard_map/ppermute | solution.py:686
  18.7 0.7 %collective-permute-start.2 = (f32[72,128]{1,0:T(8,128)S(1)}, f32[72,128]{1,0:T(8,128)S(1)}, u32[]{:S(2)}, u32[]{:S(2)}) collective-permute-start(f32[72,128]{1,0:T(8,128)S(1)} %get-tuple-element.36), channel_id=1, source_target_pairs={{0,1},{1,0},{5,6},{6,5},{8,9},{9,8},{13,14},{14,13},{16,17},{17,16... | collective-permute-start | bytes 110600 | tf_op jit(solution)/shard_map/ppermute | solution.py:686
  19.4 0.7 %collective-permute-start.4 = (f32[72,128]{1,0:T(8,128)S(1)}, f32[72,128]{1,0:T(8,128)S(1)}, u32[]{:S(2)}, u32[]{:S(2)}) collective-permute-start(f32[72,128]{1,0:T(8,128)S(1)} %get-tuple-element.48), channel_id=1, source_target_pairs={{248,249},{249,248},{250,251},{251,250},{252,253},{253,252},{254,2... | collective-permute-start | bytes 110600 | tf_op jit(solution)/shard_map/ppermute | solution.py:686
  20.1 0.7 %collective-permute-start.5 = (f32[72,128]{1,0:T(8,128)S(1)}, f32[72,128]{1,0:T(8,128)S(1)}, u32[]{:S(2)}, u32[]{:S(2)}) collective-permute-start(f32[72,128]{1,0:T(8,128)S(1)} %get-tuple-element.49), channel_id=1, source_target_pairs={{248,255},{249,250},{250,249},{251,252},{252,251},{253,254},{254,2... | collective-permute-start | bytes 110600 | tf_op jit(solution)/shard_map/ppermute | solution.py:686
  20.7 0.0 collective-permute-done.turn_1
  20.7 1.9 %collective-permute-start.8 = (f32[48,128]{1,0:T(8,128)S(1)}, f32[48,128]{1,0:T(8,128)S(1)}, u32[]{:S(2)}, u32[]{:S(2)}) collective-permute-start(f32[48,128]{1,0:T(8,128)S(1)} %get-tuple-element.54), channel_id=1, source_target_pairs={{7,8},{248,257},{249,258},{250,259},{251,260},{252,261},{253,262},... | collective-permute-start | bytes 73736 | tf_op jit(solution)/shard_map/ppermute | solution.py:686
  22.7 3.1 %shard_map.69 = (f32[5,48,216]{2,1,0:T(8,128)S(1)}, bf16[3,128,216]{2,1,0:T(8,128)(2,1)S(1)}, bf16[3,216,128]{2,1,0:T(8,128)(2,1)S(1)}, bf16[3,216,128]{2,1,0:T(...) custom-call(f32[2,5,12,2,216]{4,3,2,1,0:T(2,128)} %bitcast.5, ...), custom_call_target="tpu_custom_call" | custom-call | flops 1000000 | bytes 2000000 | tf_op jit(solution)/shard_map/pallas_call | solution.py:752
  25.8 0.0 collective-permute-done.1.turn_2
  25.8 1.3 %collective-permute-start.7 = (f32[72,128]{1,0:T(8,128)S(1)}, f32[72,128]{1,0:T(8,128)S(1)}, u32[]{:S(2)}, u32[]{:S(2)}) collective-permute-start(f32[72,128]{1,0:T(8,128)S(1)} %get-tuple-element.53), channel_id=1, source_target_pairs={{0,8},{248,256},{249,257},{250,258},{251,259},{252,260},{253,261},... | collective-permute-start | bytes 110600 | tf_op jit(solution)/shard_map/ppermute | solution.py:686
  27.1 0.0 collective-permute-done.2.turn_3
  27.2 0.7 %shard_map.70 = (f32[9,48,216]{2,1,0:T(8,128)S(1)}, f32[9,48,216]{2,1,0:T(8,128)S(1)}, f32[72,128]{1,0:T(8,128)S(1)}, f32[72,128]{1,0:T(8,128)S(1)}) custom-call(f32[5,48,216]{2,1,0:T(8,128)S(1)} %get-tuple-element.32.state_ref.refs_0_, f32[9,48,216]{2,1,0:T(8,128)S(1)} %get-tuple-element.33.tg_ref.tg_first_ref, f32[72,128]{1,0:T(8,128)S(1)} %collective-permute-done.turn_1, ...), custom_call_target="tpu_custom_call" | custom-call | flops 100000000 | bytes 2000000 | tf_op jit(solution)/shard_map/pallas_call | solution.py:760
  27.9 1.9 %collective-permute-start.3 = (f32[72,128]{1,0:T(8,128)S(1)}, f32[72,128]{1,0:T(8,128)S(1)}, u32[]{:S(2)}, u32[]{:S(2)}) collective-permute-start(f32[72,128]{1,0:T(8,128)S(1)} %get-tuple-element.44.mine_ref), channel_id=1, source_target_pairs={{1,9},{2,10},{3,11},{4,12},{5,13},{6,14},{7,15},{9,1},{10,2},{11,3... | collective-permute-start | bytes 110600 | tf_op jit(solution)/shard_map/ppermute | solution.py:686
  29.8 0.0 collective-permute-done.4.even_ref
  29.8 6.5 %collective-permute-start.6 = (f32[72,128]{1,0:T(8,128)S(1)}, f32[72,128]{1,0:T(8,128)S(1)}, u32[]{:S(2)}, u32[]{:S(2)}) collective-permute-start(f32[72,128]{1,0:T(8,128)S(1)} %get-tuple-element.52), channel_id=1, source_target_pairs={{0,1016},{1,1017},{2,1018},{3,1019},{4,1020},{5,1021},{6,1022},{7,... | collective-permute-start | bytes 110600 | tf_op jit(solution)/shard_map/ppermute | solution.py:686
  36.4 0.0 collective-permute-done.5.odd_ref
  36.4 0.1 shard_map.71
  36.5 0.7 %collective-permute-start.10 = (f32[72,128]{1,0:T(8,128)S(1)}, f32[72,128]{1,0:T(8,128)S(1)}, u32[]{:S(2)}, u32[]{:S(2)}) collective-permute-start(f32[72,128]{1,0:T(8,128)S(1)} %get-tuple-element.59), channel_id=1, source_target_pairs={{8,0},{240,248},{241,249},{242,250},{243,251},{244,252},{245,253},... | collective-permute-start | bytes 110600 | tf_op jit(solution)/shard_map/ppermute | solution.py:686
  37.1 0.0 collective-permute-done.8.refs_6_.below_ref
  37.1 1.3 %collective-permute-start.9 = (f32[48,128]{1,0:T(8,128)S(1)}, f32[48,128]{1,0:T(8,128)S(1)}, u32[]{:S(2)}, u32[]{:S(2)}) collective-permute-start(f32[48,128]{1,0:T(8,128)S(1)} %get-tuple-element.54), channel_id=1, source_target_pairs={{1,8},{248,263},{249,256},{250,257},{251,258},{252,259},{253,260},... | collective-permute-start | bytes 73736 | tf_op jit(solution)/shard_map/ppermute | solution.py:686
  38.4 11.3 %collective-permute-done.9.refs_7_.above_ref = f32[48,128]{1,0:T(8,128)S(1)} collective-permute-done((f32[48,128]{1,0:T(8,128)S(1)}, f32[48,128]{1,0:T(8,128)S(1)}, u32[]{:S(2)}, u32[]{:S(2)}) %collective-permute-start.9) | collective-permute-done | bytes 24608 | tf_op jit(solution)/shard_map/ppermute | solution.py:686
  49.7 0.0 collective-permute-done.7.refs_5_.up_ref
  49.7 0.0 collective-permute-done.3.even_ref.even_a_ref
  49.7 0.0 collective-permute-done.6.refs_4_.odd_ref
  49.8 2.3 %shard_map.72 = (f32[2,5,12,2,216]{4,3,2,1,0:T(2,128)}, f32[2,5,12,2,216]{4,3,2,1,0:T(2,128)}) custom-call(f32[72,128]{1,0:T(8,128)S(1)} %collective-permute-done.3.even_ref.even_a_ref, f32[5,48,216]{2,1,0:T(8,128)S(1)} %get-tuple-element.45.vol_ref, f32[5,48,216]{2,1,0:T(8,128)S(1)} %get-tuple-element.32.state_ref.refs_0_, ...), custom_call_target="tpu_custom_call" | custom-call | flops 100000000 | bytes 2000000 | tf_op jit(solution)/shard_map/pallas_call | solution.py:774
  52.0 0.0 collective-permute-done.10.even_b_ref
  52.0 0.1 shard_map.73
Async XLA Ops:
  3.2 17.6 %collective-permute-start = (f32[72,128]{1,0:T(8,128)S(1)}, f32[72,128]{1,0:T(8,128)S(1)}, u32[]{:S(2)}, u32[]{:S(2)}) collective-permute-start(f32[72,128]{1,0:T(8,128)S(1)} %get-tuple-element.34), channel_id=1, source_target_pairs={{1,2},{2,1},{3,4},{4,3},{6,7},{7,6},{9,10},{10,9},{11,12},{12,11},... | collective-permute-start | bytes 110600 | tf_op jit(solution)/shard_map/ppermute | solution.py:686
  5.5 20.3 %collective-permute-start.1 = (f32[72,128]{1,0:T(8,128)S(1)}, f32[72,128]{1,0:T(8,128)S(1)}, u32[]{:S(2)}, u32[]{:S(2)}) collective-permute-start(f32[72,128]{1,0:T(8,128)S(1)} %get-tuple-element.35), channel_id=1, source_target_pairs={{0,7},{2,3},{3,2},{4,5},{5,4},{7,0},{8,15},{10,11},{11,10},{12,13}... | collective-permute-start | bytes 110600 | tf_op jit(solution)/shard_map/ppermute | solution.py:686
  18.7 8.4 %collective-permute-start.2 = (f32[72,128]{1,0:T(8,128)S(1)}, f32[72,128]{1,0:T(8,128)S(1)}, u32[]{:S(2)}, u32[]{:S(2)}) collective-permute-start(f32[72,128]{1,0:T(8,128)S(1)} %get-tuple-element.36), channel_id=1, source_target_pairs={{0,1},{1,0},{5,6},{6,5},{8,9},{9,8},{13,14},{14,13},{16,17},{17,16... | collective-permute-start | bytes 110600 | tf_op jit(solution)/shard_map/ppermute | solution.py:686
  19.4 10.4 %collective-permute-start.4 = (f32[72,128]{1,0:T(8,128)S(1)}, f32[72,128]{1,0:T(8,128)S(1)}, u32[]{:S(2)}, u32[]{:S(2)}) collective-permute-start(f32[72,128]{1,0:T(8,128)S(1)} %get-tuple-element.48), channel_id=1, source_target_pairs={{248,249},{249,248},{250,251},{251,250},{252,253},{253,252},{254,2... | collective-permute-start | bytes 110600 | tf_op jit(solution)/shard_map/ppermute | solution.py:686
  20.1 16.3 %collective-permute-start.5 = (f32[72,128]{1,0:T(8,128)S(1)}, f32[72,128]{1,0:T(8,128)S(1)}, u32[]{:S(2)}, u32[]{:S(2)}) collective-permute-start(f32[72,128]{1,0:T(8,128)S(1)} %get-tuple-element.49), channel_id=1, source_target_pairs={{248,255},{249,250},{250,249},{251,252},{252,251},{253,254},{254,2... | collective-permute-start | bytes 110600 | tf_op jit(solution)/shard_map/ppermute | solution.py:686
  20.7 16.4 %collective-permute-start.8 = (f32[48,128]{1,0:T(8,128)S(1)}, f32[48,128]{1,0:T(8,128)S(1)}, u32[]{:S(2)}, u32[]{:S(2)}) collective-permute-start(f32[48,128]{1,0:T(8,128)S(1)} %get-tuple-element.54), channel_id=1, source_target_pairs={{7,8},{248,257},{249,258},{250,259},{251,260},{252,261},{253,262},... | collective-permute-start | bytes 73736 | tf_op jit(solution)/shard_map/ppermute | solution.py:686
  25.8 23.9 %collective-permute-start.7 = (f32[72,128]{1,0:T(8,128)S(1)}, f32[72,128]{1,0:T(8,128)S(1)}, u32[]{:S(2)}, u32[]{:S(2)}) collective-permute-start(f32[72,128]{1,0:T(8,128)S(1)} %get-tuple-element.53), channel_id=1, source_target_pairs={{0,8},{248,256},{249,257},{250,258},{251,259},{252,260},{253,261},... | collective-permute-start | bytes 110600 | tf_op jit(solution)/shard_map/ppermute | solution.py:686
  27.9 21.9 %collective-permute-start.3 = (f32[72,128]{1,0:T(8,128)S(1)}, f32[72,128]{1,0:T(8,128)S(1)}, u32[]{:S(2)}, u32[]{:S(2)}) collective-permute-start(f32[72,128]{1,0:T(8,128)S(1)} %get-tuple-element.44.mine_ref), channel_id=1, source_target_pairs={{1,9},{2,10},{3,11},{4,12},{5,13},{6,14},{7,15},{9,1},{10,2},{11,3... | collective-permute-start | bytes 110600 | tf_op jit(solution)/shard_map/ppermute | solution.py:686
  29.8 19.9 %collective-permute-start.6 = (f32[72,128]{1,0:T(8,128)S(1)}, f32[72,128]{1,0:T(8,128)S(1)}, u32[]{:S(2)}, u32[]{:S(2)}) collective-permute-start(f32[72,128]{1,0:T(8,128)S(1)} %get-tuple-element.52), channel_id=1, source_target_pairs={{0,1016},{1,1017},{2,1018},{3,1019},{4,1020},{5,1021},{6,1022},{7,... | collective-permute-start | bytes 110600 | tf_op jit(solution)/shard_map/ppermute | solution.py:686
  36.5 15.6 %collective-permute-start.10 = (f32[72,128]{1,0:T(8,128)S(1)}, f32[72,128]{1,0:T(8,128)S(1)}, u32[]{:S(2)}, u32[]{:S(2)}) collective-permute-start(f32[72,128]{1,0:T(8,128)S(1)} %get-tuple-element.59), channel_id=1, source_target_pairs={{8,0},{240,248},{241,249},{242,250},{243,251},{244,252},{245,253},... | collective-permute-start | bytes 110600 | tf_op jit(solution)/shard_map/ppermute | solution.py:686
  37.1 12.6 %collective-permute-start.9 = (f32[48,128]{1,0:T(8,128)S(1)}, f32[48,128]{1,0:T(8,128)S(1)}, u32[]{:S(2)}, u32[]{:S(2)}) collective-permute-start(f32[48,128]{1,0:T(8,128)S(1)} %get-tuple-element.54), channel_id=1, source_target_pairs={{1,8},{248,263},{249,256},{250,257},{251,258},{252,259},{253,260},... | collective-permute-start | bytes 73736 | tf_op jit(solution)/shard_map/ppermute | solution.py:686

commit v3 on v2

--- a/solution.py
+++ b/solution.py
@@ -1,3 +1,4 @@
+import functools
 import math
 
 import jax
@@ -44,14 +45,6 @@
 STRIDE = (36, 6, 1)
 
 
-def coefficients():
-    matrix = node_matrix()
-    nodes = np.arange(NODES)
-    place = (nodes // 36, nodes // 6 % 6, nodes % 6)
-    rows = [matrix[place[d], j] for d in range(3) for j in range(6)]
-    return np.stack(rows).astype(np.float32)
-
-
 def hot(sources, depth):
     rows = lax.broadcasted_iota(jnp.int32, (depth, sources[0].shape[1]), 0)
     found = rows == sources[0]
@@ -94,13 +87,15 @@
     )
 
 
-def deriv_table(lanes, coef_ref, d):
+def deriv_table(lanes, matrix, d):
     lane = lax.broadcasted_iota(jnp.int32, (1, NODES), 1)
     base = lane - STRIDE[d] * lanes.place[d]
     rows = lax.broadcasted_iota(jnp.int32, (NODES, NODES), 0) - base
     table = jnp.zeros((NODES, NODES), F32)
     for j in range(6):
-        line = coef_ref[6 * d + j : 6 * d + j + 1, :]
+        line = jnp.zeros((1, NODES), F32)
+        for i in range(6):
+            line = jnp.where(lanes.place[d] == i, float(np.float32(matrix[i, j])), line)
         table = jnp.where(rows == STRIDE[d] * j, line, table)
     return table
 
@@ -156,11 +151,6 @@
     return stack([ref[a, field].reshape(24, NODES) for a in range(2)])
 
 
-def write_rows(ref, field, value):
-    for a in range(2):
-        ref[a, field] = value[24 * a : 24 * a + 24].reshape(12, 2, NODES)
-
-
 def load_prims(state_ref):
     rho = state_ref[0]
     inv = 1.0 / rho
@@ -328,19 +318,21 @@
 def ends_late():
     period = period_of(lax.axis_size("gx"))
     pair = lax.rem(lax.axis_index("gx"), period) >= period - 2
-    return jnp.logical_or(pair, is_device(0, 0))
+    last = lax.axis_size("gz") - 1
+    near = [is_device(0, 0)] + [is_device(i, j) for i in (0, 1) for j in (1, last)]
+    return functools.reduce(jnp.logical_or, near, pair)
 
 
 def parity_of(axis):
     return lax.rem(lax.axis_index(axis), 2) == 0
 
 
-def first_kernel(state_hbm, mask_hbm, h_hbm, coef_hbm, st_ref, aux_ref, dh_ref, dl_ref, sw_ref, tg_ref,
-                 even_ref, odd_ref, turn_1, turn_2, turn_3, edge_ref, upper_ref, state_buf, mask_buf, h_buf, coef_buf, face_buf, sems):
+def first_kernel(state_hbm, mask_hbm, h_hbm, st_ref, aux_ref, dh_ref, dl_ref, sw_ref, tg_ref,
+                 even_ref, odd_ref, turn_1, turn_2, turn_3, edge_ref, upper_ref, state_buf, mask_buf, h_buf, face_buf, sems):
     copies = [
         pltpu.make_async_copy(src, dst, sems.at[i])
         for i, (src, dst) in enumerate(
-            ((coef_hbm, coef_buf), (state_hbm, state_buf), (mask_hbm, mask_buf), (h_hbm, h_buf))
+            ((state_hbm, state_buf), (mask_hbm, mask_buf), (h_hbm, h_buf))
         )
     ]
     for copy in copies:
@@ -348,12 +340,12 @@
     lanes = Lanes()
     for d in range(3):
         sw_ref[d] = swap_table(lanes, d)
-    copies[0].wait()
+    matrix = node_matrix()
     for d in range(3):
-        high, low = halves(deriv_table(lanes, coef_buf, d))
+        high, low = halves(deriv_table(lanes, matrix, d))
         dh_ref[d] = high
         dl_ref[d] = low
-    for copy in copies[1:]:
+    for copy in copies:
         copy.wait()
     for i in range(5):
         st_ref[i] = read_rows(state_buf, i)
@@ -602,11 +594,11 @@
             (rho, vel, temp), (out[0], out[1:4], out[4]), d, lanes.sig[d], scales[d]
         )
         total = [t + f for t, f in zip(total, faces)]
+    pairs = []
     for d in range(3):
         flux = flux_of(tg, vel, d)
-        pair = halves(stack(flux))
-        slope = rows_of(derive(pair, dh_ref[d], dl_ref[d]), 4)
-        swapped = rows_of(move(pair, sw_ref[d]), 4)
+        pairs.append([halves(f) for f in flux])
+        swapped = rows_of(move([stack(list(v)) for v in zip(*pairs[d])], sw_ref[d]), 4)
         for i in range(4):
             if d == 0:
                 out = jnp.where(lanes.ghost_x, flux_x[i], inner_x(swapped[i], flux[i], lanes))
@@ -614,19 +606,28 @@
                 out = jnp.where(lanes.ghost_z, flux_z[i], inner_z(swapped[i], flux[i], lanes))
             else:
                 out = inner_y(swapped[i], flux[i], lanes, wall_lo, wall_hi, 1.0)
-            total[i + 1] = total[i + 1] + scales[d] * (
-                slope[i] + (HALF_W * lanes.sig[d]) * (flux[i] - out)
-            )
-    for i, field in enumerate([rho] + mom + [energy]):
-        reg = vol_ref[i] + TIME_STEP * total[i]
-        write_rows(reg_out, i, reg)
-        write_rows(state_out, i, field + SECTION_B * reg)
-    copies = [
-        pltpu.make_async_copy(reg_out, reg_hbm, sems.at[0]),
-        pltpu.make_async_copy(state_out, state_hbm, sems.at[1]),
-    ]
-    for copy in copies:
-        copy.start()
+            total[i + 1] = total[i + 1] + (scales[d] * HALF_W * lanes.sig[d]) * (flux[i] - out)
+    fields = [rho] + mom + [energy]
+    copies = []
+    for a in range(2):
+        part = slice(24 * a, 24 * a + 24)
+        mine = [t[part] for t in total]
+        for d in range(3):
+            pair = [stack([f[part] for f in v]) for v in zip(*pairs[d])]
+            slope = rows_of(derive(pair, dh_ref[d], dl_ref[d]), 4, 24)
+            scale = sy[part] if d == 1 else scales[d]
+            for i in range(4):
+                mine[i + 1] = mine[i + 1] + scale * slope[i]
+        for i in range(5):
+            reg = vol_ref[i][part] + TIME_STEP * mine[i]
+            reg_out[a, i] = reg.reshape(12, 2, NODES)
+            state_out[a, i] = (fields[i][part] + SECTION_B * reg).reshape(12, 2, NODES)
+        copies += [
+            pltpu.make_async_copy(reg_out.at[a], reg_hbm.at[a], sems.at[2 * a]),
+            pltpu.make_async_copy(state_out.at[a], state_hbm.at[a], sems.at[2 * a + 1]),
+        ]
+        for copy in copies[2 * a :]:
+            copy.start()
     for copy in copies:
         copy.wait()
 
@@ -702,7 +703,6 @@
 
 
 def shards(state, register, heights, solid_wall_mask):
-    coef = jnp.asarray(coefficients())
     h = heights.reshape(1, 12)
 
     def rows(array):
@@ -721,21 +721,19 @@
         first_kernel,
         (field_shape(5), aux_shape, table, table, table, field_shape(9), *[FACE] * 5, edge_shape, FACE),
         10**8,
-        in_specs=[hbm] * 4,
+        in_specs=[hbm] * 3,
         scratch_shapes=[
             pltpu.VMEM((2, 5, 12, 2, NODES), F32),
             pltpu.VMEM((2, 2, 11), jnp.int32),
             pltpu.VMEM((1, 12), F32),
-            pltpu.VMEM((18, NODES), F32),
             pltpu.VMEM((144, 128), F32),
-            pltpu.SemaphoreType.DMA((4,)),
+            pltpu.SemaphoreType.DMA((3,)),
         ],
-    )(*[pltpu.with_memory_space_constraint(v, pltpu.HBM) for v in (rows(state), solid_wall_mask, h, coef)])
+    )(*[pltpu.with_memory_space_constraint(v, pltpu.HBM) for v in (rows(state), solid_wall_mask, h)])
     period = period_of(lax.axis_size("gx"))
     late = lambda i: i % period == period - 1
     ok = lambda flag, to: to if flag else None
     origin = lambda i, j: i == 0 and j == 0
-    beside = lambda i, j: i == 1 and j == 0
     last_z = lax.axis_size("gz") - 1
     below = send(edge, lambda i, j: ok(late(i) or (i == 0 and j == last_z), (i + 1, j + 1)))
     above = send(edge, lambda i, j: ok(late(i) or (i == 0 and j == 1), (i + 1, j - 1)))
@@ -761,7 +759,7 @@
         second_kernel, (field_shape(9), field_shape(9), FACE, FACE), 10**8, scratch_shapes=face_buf
     )(st, tg_first, *za, uz, px, ep)
     early = lambda i: not (late(i) or late(i ^ 1))
-    apart = lambda i, j: i < 2 and j == 0
+    apart = lambda i, j: i < 2 and j in (0, 1, last_z)
     xa_even = send(even_x, lambda i, j: ok(early(i) and not apart(i, j), (i ^ 1, j)))
     x_odd = send(odd_x, lambda i, j: ok(not late(i), (odd_partner(i), j)))
     zb_even = send(even_z, lambda i, j: ok(late(i), (i, j ^ 1)))
@@ -770,11 +768,11 @@
         third_kernel, (field_shape(9), field_shape(9), FACE), 10**8, scratch_shapes=face_buf
     )(st, tg_first, tg, gz, even_x, zb_even, zb_odd, uz, px, ep)
     rest = (vol, st, tg, gz, aux, x_odd, up_x, below, above, dh, dl, sw, ux, eu)
-    buffers = [block, block, pltpu.SemaphoreType.DMA((2,))]
+    buffers = [block, block, pltpu.SemaphoreType.DMA((4,))]
     outs = call(
         last_a_kernel, (whole, whole), 10**8, in_specs=[vmem] * 15, out_specs=[hbm, hbm], scratch_shapes=buffers
     )(xa_even, *rest)
-    xb_even = send(even_x, lambda i, j: ok(not early(i) or beside(i, j), (i ^ 1, j)))
+    xb_even = send(even_x, lambda i, j: ok(not early(i) or (apart(i, j) and not origin(i, j)), (i ^ 1, j)))
     state_next, reg_next = call(
         last_b_kernel,
         (whole, whole),

time: 52.4 us -> 53.4 us (1.019)
  starting transfers between devices: 31.2 us -> 32.4 us
    pallas_call x1, Pallas kernels: 0.05 us -> 2.3 us  [shards(): call(last_b_kernel, (whole, whole), 10 ** 8, in_specs=[hbm] * 3 + [vmem]...]
    pallas_call x1, Pallas kernels: 2.26 us -> 0.06 us  [shards(): call(last_a_kernel, (whole, whole), 10 ** 8, in_specs=[vmem] * 15, out_sp...]
    ppermute x11, starting transfers between devices: 31.2 us -> 32.4 us  [send(): return lax.ppermute(value, ('gx', 'gz'), pairs)]
  transfers between devices with their start and end apart: 11 -> 11, of which waited for: 1 -> 1; matrix products, arithmetic and copies ran while one was open for 0% -> 0% of each run, Pallas kernels for 12% -> 8%
where the time goes in v3:
time: 53.4 us; the launch traced here: 53.1 us
  starting transfers between devices  32.4 us (61%)
  waiting for transfers between devices  11.2 us (21%)
  Pallas kernels  8.65 us (16%)
  between operations  0.81 us (2%)
    ppermute x11, starting transfers between devices, send(): return lax.ppermute(value, ('gx', 'gz'), pairs)  32.4 us
    ppermute x11, waiting for transfers between devices, send(): return lax.ppermute(value, ('gx', 'gz'), pairs)  11.2 us
    pallas_call x1, Pallas kernels, shards(): call(volume_kernel, (field_shape(5), unpack, pack, pack, unpack, unpack),...  3.14 us
    pallas_call x1, Pallas kernels, shards(): call(first_kernel, (field_shape(5), aux_shape, table, table, table, field...  2.32 us
    pallas_call x1, Pallas kernels, shards(): call(last_b_kernel, (whole, whole), 10 ** 8, in_specs=[hbm] * 3 + [vmem]...  2.3 us
  transfers between devices with their start and end apart: 11, of which 1 were waited for; matrix products, arithmetic and copies ran while one was open for 0% of the time, Pallas kernels for 8%

profile of v3, /device:TPU:14, one launch (start us, length us, event | category | flops | bytes accessed | tf_op | source)
XLA Modules:
  0.0 53.1 jit_solution(7754322561405408617)
XLA Ops:
  0.6 2.3 %shard_map.59 = (f32[5,48,216]{2,1,0:T(8,128)S(1)}, f32[48,128]{1,0:T(8,128)S(1)}, bf16[3,216,216]{2,1,0:T(8,128)(2,1)S(1)}, bf16[3,216,216]{2,1,0:T(8,128)(2,1)...) custom-call(f32[2,5,12,2,216]{4,3,2,1,0:T(2,128)} %bitcast.9, ...), custom_call_target="tpu_custom_call" | custom-call | flops 100000000 | bytes 2000000 | tf_op jit(solution)/shard_map/pallas_call | solution.py:720
  3.0 2.4 %collective-permute-start = (f32[72,128]{1,0:T(8,128)S(1)}, f32[72,128]{1,0:T(8,128)S(1)}, u32[]{:S(2)}, u32[]{:S(2)}) collective-permute-start(f32[72,128]{1,0:T(8,128)S(1)} %get-tuple-element.34), channel_id=1, source_target_pairs={{1,2},{2,1},{3,4},{4,3},{6,7},{7,6},{9,10},{10,9},{11,12},{12,11},... | collective-permute-start | bytes 110600 | tf_op jit(solution)/shard_map/ppermute | solution.py:687
  5.3 13.2 %collective-permute-start.1 = (f32[72,128]{1,0:T(8,128)S(1)}, f32[72,128]{1,0:T(8,128)S(1)}, u32[]{:S(2)}, u32[]{:S(2)}) collective-permute-start(f32[72,128]{1,0:T(8,128)S(1)} %get-tuple-element.35), channel_id=1, source_target_pairs={{0,7},{2,3},{3,2},{4,5},{5,4},{7,0},{8,15},{10,11},{11,10},{12,13}... | collective-permute-start | bytes 110600 | tf_op jit(solution)/shard_map/ppermute | solution.py:687
  18.5 0.7 %collective-permute-start.2 = (f32[72,128]{1,0:T(8,128)S(1)}, f32[72,128]{1,0:T(8,128)S(1)}, u32[]{:S(2)}, u32[]{:S(2)}) collective-permute-start(f32[72,128]{1,0:T(8,128)S(1)} %get-tuple-element.36), channel_id=1, source_target_pairs={{0,1},{1,0},{5,6},{6,5},{8,9},{9,8},{13,14},{14,13},{16,17},{17,16... | collective-permute-start | bytes 110600 | tf_op jit(solution)/shard_map/ppermute | solution.py:687
  19.2 0.7 %collective-permute-start.4 = (f32[72,128]{1,0:T(8,128)S(1)}, f32[72,128]{1,0:T(8,128)S(1)}, u32[]{:S(2)}, u32[]{:S(2)}) collective-permute-start(f32[72,128]{1,0:T(8,128)S(1)} %get-tuple-element.48), channel_id=1, source_target_pairs={{248,249},{249,248},{250,251},{251,250},{252,253},{253,252},{254,2... | collective-permute-start | bytes 110600 | tf_op jit(solution)/shard_map/ppermute | solution.py:687
  19.9 0.7 %collective-permute-start.5 = (f32[72,128]{1,0:T(8,128)S(1)}, f32[72,128]{1,0:T(8,128)S(1)}, u32[]{:S(2)}, u32[]{:S(2)}) collective-permute-start(f32[72,128]{1,0:T(8,128)S(1)} %get-tuple-element.49), channel_id=1, source_target_pairs={{248,255},{249,250},{250,249},{251,252},{252,251},{253,254},{254,2... | collective-permute-start | bytes 110600 | tf_op jit(solution)/shard_map/ppermute | solution.py:687
  20.5 0.0 collective-permute-done.turn_1
  20.6 1.9 %collective-permute-start.8 = (f32[48,128]{1,0:T(8,128)S(1)}, f32[48,128]{1,0:T(8,128)S(1)}, u32[]{:S(2)}, u32[]{:S(2)}) collective-permute-start(f32[48,128]{1,0:T(8,128)S(1)} %get-tuple-element.54), channel_id=1, source_target_pairs={{7,8},{248,257},{249,258},{250,259},{251,260},{252,261},{253,262},... | collective-permute-start | bytes 73736 | tf_op jit(solution)/shard_map/ppermute | solution.py:687
  22.5 3.1 %shard_map.60 = (f32[5,48,216]{2,1,0:T(8,128)S(1)}, bf16[3,128,216]{2,1,0:T(8,128)(2,1)S(1)}, bf16[3,216,128]{2,1,0:T(8,128)(2,1)S(1)}, bf16[3,216,128]{2,1,0:T(...) custom-call(f32[2,5,12,2,216]{4,3,2,1,0:T(2,128)} %bitcast.5, ...), custom_call_target="tpu_custom_call" | custom-call | flops 1000000 | bytes 2000000 | tf_op jit(solution)/shard_map/pallas_call | solution.py:750
  25.6 0.0 collective-permute-done.1.turn_2
  25.6 1.3 %collective-permute-start.7 = (f32[72,128]{1,0:T(8,128)S(1)}, f32[72,128]{1,0:T(8,128)S(1)}, u32[]{:S(2)}, u32[]{:S(2)}) collective-permute-start(f32[72,128]{1,0:T(8,128)S(1)} %get-tuple-element.53), channel_id=1, source_target_pairs={{0,8},{248,256},{249,257},{250,258},{251,259},{252,260},{253,261},... | collective-permute-start | bytes 110600 | tf_op jit(solution)/shard_map/ppermute | solution.py:687
  26.9 0.0 collective-permute-done.2.turn_3
  27.0 0.7 %shard_map.61 = (f32[9,48,216]{2,1,0:T(8,128)S(1)}, f32[9,48,216]{2,1,0:T(8,128)S(1)}, f32[72,128]{1,0:T(8,128)S(1)}, f32[72,128]{1,0:T(8,128)S(1)}) custom-call(f32[5,48,216]{2,1,0:T(8,128)S(1)} %get-tuple-element.32.state_ref.refs_0_, f32[9,48,216]{2,1,0:T(8,128)S(1)} %get-tuple-element.33.tg_ref.tg_first_ref, f32[72,128]{1,0:T(8,128)S(1)} %collective-permute-done.turn_1, ...), custom_call_target="tpu_custom_call" | custom-call | flops 100000000 | bytes 2000000 | tf_op jit(solution)/shard_map/pallas_call | solution.py:758
  27.7 0.7 %collective-permute-start.3 = (f32[72,128]{1,0:T(8,128)S(1)}, f32[72,128]{1,0:T(8,128)S(1)}, u32[]{:S(2)}, u32[]{:S(2)}) collective-permute-start(f32[72,128]{1,0:T(8,128)S(1)} %get-tuple-element.44.mine_ref), channel_id=1, source_target_pairs={{2,10},{3,11},{4,12},{5,13},{6,14},{10,2},{11,3},{12,4},{13,5},{14... | collective-permute-start | bytes 110600 | tf_op jit(solution)/shard_map/ppermute | solution.py:687
  28.4 0.0 collective-permute-done.4.even_ref
  28.4 7.8 %collective-permute-start.6 = (f32[72,128]{1,0:T(8,128)S(1)}, f32[72,128]{1,0:T(8,128)S(1)}, u32[]{:S(2)}, u32[]{:S(2)}) collective-permute-start(f32[72,128]{1,0:T(8,128)S(1)} %get-tuple-element.52), channel_id=1, source_target_pairs={{0,1016},{1,1017},{2,1018},{3,1019},{4,1020},{5,1021},{6,1022},{7,... | collective-permute-start | bytes 110600 | tf_op jit(solution)/shard_map/ppermute | solution.py:687
  36.2 0.0 collective-permute-done.5.odd_ref
  36.2 0.1 shard_map.62
  36.3 1.9 %collective-permute-start.10 = (f32[72,128]{1,0:T(8,128)S(1)}, f32[72,128]{1,0:T(8,128)S(1)}, u32[]{:S(2)}, u32[]{:S(2)}) collective-permute-start(f32[72,128]{1,0:T(8,128)S(1)} %get-tuple-element.59), channel_id=1, source_target_pairs={{1,9},{7,15},{8,0},{9,1},{15,7},{240,248},{241,249},{242,250},{243... | collective-permute-start | bytes 110600 | tf_op jit(solution)/shard_map/ppermute | solution.py:687
  38.2 0.0 collective-permute-done.8.refs_6_.below_ref
  38.2 1.3 %collective-permute-start.9 = (f32[48,128]{1,0:T(8,128)S(1)}, f32[48,128]{1,0:T(8,128)S(1)}, u32[]{:S(2)}, u32[]{:S(2)}) collective-permute-start(f32[48,128]{1,0:T(8,128)S(1)} %get-tuple-element.54), channel_id=1, source_target_pairs={{1,8},{248,263},{249,256},{250,257},{251,258},{252,259},{253,260},... | collective-permute-start | bytes 73736 | tf_op jit(solution)/shard_map/ppermute | solution.py:687
  39.5 11.2 %collective-permute-done.9.refs_7_.above_ref = f32[48,128]{1,0:T(8,128)S(1)} collective-permute-done((f32[48,128]{1,0:T(8,128)S(1)}, f32[48,128]{1,0:T(8,128)S(1)}, u32[]{:S(2)}, u32[]{:S(2)}) %collective-permute-start.9) | collective-permute-done | bytes 24608 | tf_op jit(solution)/shard_map/ppermute | solution.py:687
  50.7 0.0 collective-permute-done.7.refs_5_.up_ref
  50.7 0.0 collective-permute-done.3.even_ref.even_a_ref
  50.7 0.0 collective-permute-done.6.refs_4_.odd_ref
  50.7 0.1 shard_map.63
  50.8 0.0 collective-permute-done.10.even_b_ref
  50.8 2.3 %shard_map.64 = (f32[2,5,12,2,216]{4,3,2,1,0:T(2,128)}, f32[2,5,12,2,216]{4,3,2,1,0:T(2,128)}) custom-call(f32[2,5,12,2,216]{4,3,2,1,0:T(2,128)} %get-tuple-element.57.state_in, f32[2,5,12,2,216]{4,3,2,1,0:T(2,128)} %get-tuple-element.58.reg_in, f32[2,5,12,2,216]{4,3,2,1,0:T(2,128)} %bitcast.6, ...), custom_call_target="tpu_custom_call", output_to_operand_aliasing={{0}: (0, {}), {1}: (1, {})} | custom-call | flops 100000000 | bytes 2000000 | tf_op jit(solution)/shard_map/pallas_call | solution.py:776
Async XLA Ops:
  3.0 17.6 %collective-permute-start = (f32[72,128]{1,0:T(8,128)S(1)}, f32[72,128]{1,0:T(8,128)S(1)}, u32[]{:S(2)}, u32[]{:S(2)}) collective-permute-start(f32[72,128]{1,0:T(8,128)S(1)} %get-tuple-element.34), channel_id=1, source_target_pairs={{1,2},{2,1},{3,4},{4,3},{6,7},{7,6},{9,10},{10,9},{11,12},{12,11},... | collective-permute-start | bytes 110600 | tf_op jit(solution)/shard_map/ppermute | solution.py:687
  5.3 20.3 %collective-permute-start.1 = (f32[72,128]{1,0:T(8,128)S(1)}, f32[72,128]{1,0:T(8,128)S(1)}, u32[]{:S(2)}, u32[]{:S(2)}) collective-permute-start(f32[72,128]{1,0:T(8,128)S(1)} %get-tuple-element.35), channel_id=1, source_target_pairs={{0,7},{2,3},{3,2},{4,5},{5,4},{7,0},{8,15},{10,11},{11,10},{12,13}... | collective-permute-start | bytes 110600 | tf_op jit(solution)/shard_map/ppermute | solution.py:687
  18.5 8.4 %collective-permute-start.2 = (f32[72,128]{1,0:T(8,128)S(1)}, f32[72,128]{1,0:T(8,128)S(1)}, u32[]{:S(2)}, u32[]{:S(2)}) collective-permute-start(f32[72,128]{1,0:T(8,128)S(1)} %get-tuple-element.36), channel_id=1, source_target_pairs={{0,1},{1,0},{5,6},{6,5},{8,9},{9,8},{13,14},{14,13},{16,17},{17,16... | collective-permute-start | bytes 110600 | tf_op jit(solution)/shard_map/ppermute | solution.py:687
  19.2 9.2 %collective-permute-start.4 = (f32[72,128]{1,0:T(8,128)S(1)}, f32[72,128]{1,0:T(8,128)S(1)}, u32[]{:S(2)}, u32[]{:S(2)}) collective-permute-start(f32[72,128]{1,0:T(8,128)S(1)} %get-tuple-element.48), channel_id=1, source_target_pairs={{248,249},{249,248},{250,251},{251,250},{252,253},{253,252},{254,2... | collective-permute-start | bytes 110600 | tf_op jit(solution)/shard_map/ppermute | solution.py:687
  19.9 16.3 %collective-permute-start.5 = (f32[72,128]{1,0:T(8,128)S(1)}, f32[72,128]{1,0:T(8,128)S(1)}, u32[]{:S(2)}, u32[]{:S(2)}) collective-permute-start(f32[72,128]{1,0:T(8,128)S(1)} %get-tuple-element.49), channel_id=1, source_target_pairs={{248,255},{249,250},{250,249},{251,252},{252,251},{253,254},{254,2... | collective-permute-start | bytes 110600 | tf_op jit(solution)/shard_map/ppermute | solution.py:687
  20.6 17.6 %collective-permute-start.8 = (f32[48,128]{1,0:T(8,128)S(1)}, f32[48,128]{1,0:T(8,128)S(1)}, u32[]{:S(2)}, u32[]{:S(2)}) collective-permute-start(f32[48,128]{1,0:T(8,128)S(1)} %get-tuple-element.54), channel_id=1, source_target_pairs={{7,8},{248,257},{249,258},{250,259},{251,260},{252,261},{253,262},... | collective-permute-start | bytes 73736 | tf_op jit(solution)/shard_map/ppermute | solution.py:687
  25.6 25.0 %collective-permute-start.7 = (f32[72,128]{1,0:T(8,128)S(1)}, f32[72,128]{1,0:T(8,128)S(1)}, u32[]{:S(2)}, u32[]{:S(2)}) collective-permute-start(f32[72,128]{1,0:T(8,128)S(1)} %get-tuple-element.53), channel_id=1, source_target_pairs={{0,8},{248,256},{249,257},{250,258},{251,259},{252,260},{253,261},... | collective-permute-start | bytes 110600 | tf_op jit(solution)/shard_map/ppermute | solution.py:687
  27.7 23.0 %collective-permute-start.3 = (f32[72,128]{1,0:T(8,128)S(1)}, f32[72,128]{1,0:T(8,128)S(1)}, u32[]{:S(2)}, u32[]{:S(2)}) collective-permute-start(f32[72,128]{1,0:T(8,128)S(1)} %get-tuple-element.44.mine_ref), channel_id=1, source_target_pairs={{2,10},{3,11},{4,12},{5,13},{6,14},{10,2},{11,3},{12,4},{13,5},{14... | collective-permute-start | bytes 110600 | tf_op jit(solution)/shard_map/ppermute | solution.py:687
  28.4 22.3 %collective-permute-start.6 = (f32[72,128]{1,0:T(8,128)S(1)}, f32[72,128]{1,0:T(8,128)S(1)}, u32[]{:S(2)}, u32[]{:S(2)}) collective-permute-start(f32[72,128]{1,0:T(8,128)S(1)} %get-tuple-element.52), channel_id=1, source_target_pairs={{0,1016},{1,1017},{2,1018},{3,1019},{4,1020},{5,1021},{6,1022},{7,... | collective-permute-start | bytes 110600 | tf_op jit(solution)/shard_map/ppermute | solution.py:687
  36.3 14.5 %collective-permute-start.10 = (f32[72,128]{1,0:T(8,128)S(1)}, f32[72,128]{1,0:T(8,128)S(1)}, u32[]{:S(2)}, u32[]{:S(2)}) collective-permute-start(f32[72,128]{1,0:T(8,128)S(1)} %get-tuple-element.59), channel_id=1, source_target_pairs={{1,9},{7,15},{8,0},{9,1},{15,7},{240,248},{241,249},{242,250},{243... | collective-permute-start | bytes 110600 | tf_op jit(solution)/shard_map/ppermute | solution.py:687
  38.2 12.5 %collective-permute-start.9 = (f32[48,128]{1,0:T(8,128)S(1)}, f32[48,128]{1,0:T(8,128)S(1)}, u32[]{:S(2)}, u32[]{:S(2)}) collective-permute-start(f32[48,128]{1,0:T(8,128)S(1)} %get-tuple-element.54), channel_id=1, source_target_pairs={{1,8},{248,263},{249,256},{250,257},{251,258},{252,259},{253,260},... | collective-permute-start | bytes 73736 | tf_op jit(solution)/shard_map/ppermute | solution.py:687

commit v4 on v3

--- a/solution.py
+++ b/solution.py
@@ -110,11 +110,13 @@
 
 
 def derive(pair, dh, dl):
-    return dot(pair[0], dh) + (dot(pair[1], dh) + dot(pair[0], dl))
+    return move(pair, dh) + dot(pair[0], dl)
 
 
 def move(pair, table):
-    return dot(pair[0], table) + dot(pair[1], table)
+    rows = pair[0].shape[0]
+    both = dot(jnp.concatenate(pair, axis=0), table)
+    return both[:rows] + both[rows:]
 
 
 def stack(fields):
@@ -328,7 +330,8 @@
 
 
 def first_kernel(state_hbm, mask_hbm, h_hbm, st_ref, aux_ref, dh_ref, dl_ref, sw_ref, tg_ref,
-                 even_ref, odd_ref, turn_1, turn_2, turn_3, edge_ref, upper_ref, state_buf, mask_buf, h_buf, face_buf, sems):
+                 even_ref, odd_ref, turn_1, turn_2, turn_3, edge_ref, upper_ref,
+                 uz_ref, px_ref, ep_ref, ux_ref, eu_ref, state_buf, mask_buf, h_buf, face_buf, sems):
     copies = [
         pltpu.make_async_copy(src, dst, sems.at[i])
         for i, (src, dst) in enumerate(
@@ -345,6 +348,12 @@
         high, low = halves(deriv_table(lanes, matrix, d))
         dh_ref[d] = high
         dl_ref[d] = low
+    for j in range(3):
+        uz_ref[j] = unpack_table(lanes, 2, j)
+        px_ref[j] = pack_table(0, j)
+        ep_ref[j] = edge_pack_table(j)
+        ux_ref[j] = unpack_table(lanes, 0, j)
+        eu_ref[j] = edge_unpack_table(lanes, j)
     for copy in copies:
         copy.wait()
     for i in range(5):
@@ -360,7 +369,7 @@
     )
     own = vel + [temp]
     keep = jnp.logical_and(lanes.ghost_x, lanes.ghost_z)
-    edges = edge_rows([jnp.where(keep, f, 0.0) for f in own], edge_pack_table)
+    edges = edge_rows([jnp.where(keep, f, 0.0) for f in own], lambda j: ep_ref[j])
     edge_ref[...] = stack([edges[24:48], edges[72:96]])
     pair = halves(stack(own))
     scales = (SCALE_X, sy, SCALE_Z)
@@ -384,7 +393,7 @@
         tg_ref[i] = tg[i]
     fields = [rho] + own + flux_of(tg, vel, 0)
     fields = [jnp.where(lanes.hi[0], f[24:48], 0.0) for f in fields]
-    upper_ref[...] = pack_faces(fields, lambda j: pack_table(0, j))
+    upper_ref[...] = pack_faces(fields, lambda j: px_ref[j])
     fields = [rho] + own + flux_of(tg, vel, 2)
     fields = [jnp.where(lanes.ghost_z, f, 0.0) for f in fields]
     face_buf[...] = pack_faces(fields, lambda j: pack_table(2, j))
@@ -464,16 +473,7 @@
     return jnp.logical_or(sends_late(), is_device(0, 0))
 
 
-def volume_kernel(reg_hbm, state_ref, aux_ref, dh_ref, dl_ref, sw_ref,
-                  out_ref, uz_ref, px_ref, ep_ref, ux_ref, eu_ref, reg_buf, sem):
-    lanes = Lanes()
-    for j in range(3):
-        uz_ref[j] = unpack_table(lanes, 2, j)
-        px_ref[j] = pack_table(0, j)
-        ep_ref[j] = edge_pack_table(j)
-        ux_ref[j] = unpack_table(lanes, 0, j)
-        eu_ref[j] = edge_unpack_table(lanes, j)
-
+def volume_kernel(reg_hbm, state_ref, aux_ref, dh_ref, dl_ref, sw_ref, out_ref, reg_buf, sem):
     @pl.when(jnp.logical_not(starts_late()))
     def _():
         volume(reg_hbm, state_ref, aux_ref, dh_ref, dl_ref, sw_ref, out_ref, reg_buf, sem)
@@ -717,9 +717,14 @@
     aux_shape = jax.ShapeDtypeStruct((ROWS, 128), F32)
     hbm = pl.BlockSpec(memory_space=pltpu.HBM)
     edge_shape = jax.ShapeDtypeStruct((48, 128), F32)
-    st, aux, dh, dl, sw, tg_first, even_z, odd_z, *turns_z, edge, up_x = call(
+    pack = jax.ShapeDtypeStruct((3, NODES, 128), BF16)
+    unpack = jax.ShapeDtypeStruct((3, 128, NODES), BF16)
+    st, aux, dh, dl, sw, tg_first, even_z, odd_z, *turns_z, edge, up_x, uz, px, ep, ux, eu = call(
         first_kernel,
-        (field_shape(5), aux_shape, table, table, table, field_shape(9), *[FACE] * 5, edge_shape, FACE),
+        (
+            field_shape(5), aux_shape, table, table, table, field_shape(9), *[FACE] * 5, edge_shape, FACE,
+            unpack, pack, pack, unpack, unpack,
+        ),
         10**8,
         in_specs=[hbm] * 3,
         scratch_shapes=[
@@ -743,13 +748,11 @@
         to = {j: (j + 1) % (last_z + 1) for j in turn}
         to.update({v: k for k, v in to.items()})
         za.append(send(turns_z[n], lambda i, j: ok(j in to and not late(i), (i, to.get(j)))))
-    pack = jax.ShapeDtypeStruct((3, NODES, 128), BF16)
-    unpack = jax.ShapeDtypeStruct((3, 128, NODES), BF16)
     vmem = pl.BlockSpec(memory_space=pltpu.VMEM)
     block = pltpu.VMEM((2, 5, 12, 2, NODES), F32)
-    vol, uz, px, ep, ux, eu = call(
+    vol = call(
         volume_kernel,
-        (field_shape(5), unpack, pack, pack, unpack, unpack),
+        field_shape(5),
         10**6,
         in_specs=[hbm] + [vmem] * 5,
         scratch_shapes=[block, pltpu.SemaphoreType.DMA],

time: 53.4 us -> 51 us (0.955)
  waiting for transfers between devices: 11.2 us -> 8.42 us
  starting transfers between devices: 32.4 us -> 33.5 us
  Pallas kernels: 8.65 us -> 7.93 us
    ppermute x11, waiting for transfers between devices: 11.2 us -> 8.42 us  [send(): return lax.ppermute(value, ('gx', 'gz'), pairs)]
    ppermute x11, starting transfers between devices: 32.4 us -> 33.5 us  [send(): return lax.ppermute(value, ('gx', 'gz'), pairs)]
  transfers between devices with their start and end apart: 11 -> 11, of which waited for: 1 -> 1; matrix products, arithmetic and copies ran while one was open for 0% -> 0% of each run, Pallas kernels for 8% -> 7%
where the time goes in v4:
time: 51 us; the launch traced here: 50.7 us
  starting transfers between devices  33.5 us (66%)
  waiting for transfers between devices  8.42 us (17%)
  Pallas kernels  7.93 us (16%)
  between operations  0.81 us (2%)
    ppermute x11, starting transfers between devices, send(): return lax.ppermute(value, ('gx', 'gz'), pairs)  33.5 us
    ppermute x11, waiting for transfers between devices, send(): return lax.ppermute(value, ('gx', 'gz'), pairs)  8.42 us
    pallas_call x1, Pallas kernels, shards(): call(volume_kernel, field_shape(5), 10 ** 6, in_specs=[hbm] + [vmem] * 5,...  2.8 us
    pallas_call x1, Pallas kernels, shards(): call(last_b_kernel, (whole, whole), 10 ** 8, in_specs=[hbm] * 3 + [vmem]...  2.21 us
    pallas_call x1, Pallas kernels, shards(): call(first_kernel, (field_shape(5), aux_shape, table, table, table, field...  2.17 us
  transfers between devices with their start and end apart: 11, of which 1 were waited for; matrix products, arithmetic and copies ran while one was open for 0% of the time, Pallas kernels for 7%

profile of v4, /device:TPU:14, one launch (start us, length us, event | category | flops | bytes accessed | tf_op | source)
XLA Modules:
  0.0 50.7 jit_solution(691361559704942948)
XLA Ops:
  0.6 2.2 %shard_map.59 = (f32[5,48,216]{2,1,0:T(8,128)S(1)}, f32[48,128]{1,0:T(8,128)S(1)}, bf16[3,216,216]{2,1,0:T(8,128)(2,1)S(1)}, bf16[3,216,216]{2,1,0:T(8,128)(2,1)...) custom-call(f32[2,5,12,2,216]{4,3,2,1,0:T(2,128)} %bitcast.9, ...), custom_call_target="tpu_custom_call" | custom-call | flops 100000000 | bytes 2000000 | tf_op jit(solution)/shard_map/pallas_call | solution.py:722
  2.8 2.4 %collective-permute-start = (f32[72,128]{1,0:T(8,128)S(1)}, f32[72,128]{1,0:T(8,128)S(1)}, u32[]{:S(2)}, u32[]{:S(2)}) collective-permute-start(f32[72,128]{1,0:T(8,128)S(1)} %get-tuple-element.33), channel_id=1, source_target_pairs={{1,2},{2,1},{3,4},{4,3},{6,7},{7,6},{9,10},{10,9},{11,12},{12,11},... | collective-permute-start | bytes 110600 | tf_op jit(solution)/shard_map/ppermute | solution.py:687
  5.2 13.2 %collective-permute-start.1 = (f32[72,128]{1,0:T(8,128)S(1)}, f32[72,128]{1,0:T(8,128)S(1)}, u32[]{:S(2)}, u32[]{:S(2)}) collective-permute-start(f32[72,128]{1,0:T(8,128)S(1)} %get-tuple-element.34), channel_id=1, source_target_pairs={{0,7},{2,3},{3,2},{4,5},{5,4},{7,0},{8,15},{10,11},{11,10},{12,13}... | collective-permute-start | bytes 110600 | tf_op jit(solution)/shard_map/ppermute | solution.py:687
  18.4 0.7 %collective-permute-start.2 = (f32[72,128]{1,0:T(8,128)S(1)}, f32[72,128]{1,0:T(8,128)S(1)}, u32[]{:S(2)}, u32[]{:S(2)}) collective-permute-start(f32[72,128]{1,0:T(8,128)S(1)} %get-tuple-element.35), channel_id=1, source_target_pairs={{0,1},{1,0},{5,6},{6,5},{8,9},{9,8},{13,14},{14,13},{16,17},{17,16... | collective-permute-start | bytes 110600 | tf_op jit(solution)/shard_map/ppermute | solution.py:687
  19.1 0.7 %collective-permute-start.4 = (f32[72,128]{1,0:T(8,128)S(1)}, f32[72,128]{1,0:T(8,128)S(1)}, u32[]{:S(2)}, u32[]{:S(2)}) collective-permute-start(f32[72,128]{1,0:T(8,128)S(1)} %get-tuple-element.46), channel_id=1, source_target_pairs={{248,249},{249,248},{250,251},{251,250},{252,253},{253,252},{254,2... | collective-permute-start | bytes 110600 | tf_op jit(solution)/shard_map/ppermute | solution.py:687
  19.7 0.7 %collective-permute-start.5 = (f32[72,128]{1,0:T(8,128)S(1)}, f32[72,128]{1,0:T(8,128)S(1)}, u32[]{:S(2)}, u32[]{:S(2)}) collective-permute-start(f32[72,128]{1,0:T(8,128)S(1)} %get-tuple-element.47), channel_id=1, source_target_pairs={{248,255},{249,250},{250,249},{251,252},{252,251},{253,254},{254,2... | collective-permute-start | bytes 110600 | tf_op jit(solution)/shard_map/ppermute | solution.py:687
  20.4 0.0 collective-permute-done.turn_1
  20.4 1.9 %collective-permute-start.8 = (f32[48,128]{1,0:T(8,128)S(1)}, f32[48,128]{1,0:T(8,128)S(1)}, u32[]{:S(2)}, u32[]{:S(2)}) collective-permute-start(f32[48,128]{1,0:T(8,128)S(1)} %get-tuple-element.52), channel_id=1, source_target_pairs={{7,8},{248,257},{249,258},{250,259},{251,260},{252,261},{253,262},... | collective-permute-start | bytes 73736 | tf_op jit(solution)/shard_map/ppermute | solution.py:687
  22.3 0.0 collective-permute-done.1.turn_2
  22.3 1.3 %collective-permute-start.7 = (f32[72,128]{1,0:T(8,128)S(1)}, f32[72,128]{1,0:T(8,128)S(1)}, u32[]{:S(2)}, u32[]{:S(2)}) collective-permute-start(f32[72,128]{1,0:T(8,128)S(1)} %get-tuple-element.51), channel_id=1, source_target_pairs={{0,8},{248,256},{249,257},{250,258},{251,259},{252,260},{253,261},... | collective-permute-start | bytes 110600 | tf_op jit(solution)/shard_map/ppermute | solution.py:687
  23.6 0.0 collective-permute-done.2.turn_3
  23.7 0.6 %shard_map.60 = (f32[9,48,216]{2,1,0:T(8,128)S(1)}, f32[9,48,216]{2,1,0:T(8,128)S(1)}, f32[72,128]{1,0:T(8,128)S(1)}, f32[72,128]{1,0:T(8,128)S(1)}) custom-call(f32[5,48,216]{2,1,0:T(8,128)S(1)} %get-tuple-element.31.state_ref.refs_0_, f32[9,48,216]{2,1,0:T(8,128)S(1)} %get-tuple-element.32.tg_ref.tg_first_ref, f32[72,128]{1,0:T(8,128)S(1)} %collective-permute-done.turn_1, ...), custom_call_target="tpu_custom_call" | custom-call | flops 100000000 | bytes 2000000 | tf_op jit(solution)/shard_map/pallas_call | solution.py:761
  24.3 0.7 %collective-permute-start.3 = (f32[72,128]{1,0:T(8,128)S(1)}, f32[72,128]{1,0:T(8,128)S(1)}, u32[]{:S(2)}, u32[]{:S(2)}) collective-permute-start(f32[72,128]{1,0:T(8,128)S(1)} %get-tuple-element.39.mine_ref), channel_id=1, source_target_pairs={{2,10},{3,11},{4,12},{5,13},{6,14},{10,2},{11,3},{12,4},{13,5},{14... | collective-permute-start | bytes 110600 | tf_op jit(solution)/shard_map/ppermute | solution.py:687
  24.9 0.0 collective-permute-done.4.even_ref
  24.9 8.9 %collective-permute-start.6 = (f32[72,128]{1,0:T(8,128)S(1)}, f32[72,128]{1,0:T(8,128)S(1)}, u32[]{:S(2)}, u32[]{:S(2)}) collective-permute-start(f32[72,128]{1,0:T(8,128)S(1)} %get-tuple-element.50), channel_id=1, source_target_pairs={{0,1016},{1,1017},{2,1018},{3,1019},{4,1020},{5,1021},{6,1022},{7,... | collective-permute-start | bytes 110600 | tf_op jit(solution)/shard_map/ppermute | solution.py:687
  33.8 0.0 collective-permute-done.5.odd_ref
  33.8 0.1 shard_map.62
  33.9 1.9 %collective-permute-start.10 = (f32[72,128]{1,0:T(8,128)S(1)}, f32[72,128]{1,0:T(8,128)S(1)}, u32[]{:S(2)}, u32[]{:S(2)}) collective-permute-start(f32[72,128]{1,0:T(8,128)S(1)} %get-tuple-element.57), channel_id=1, source_target_pairs={{1,9},{7,15},{8,0},{9,1},{15,7},{240,248},{241,249},{242,250},{243... | collective-permute-start | bytes 110600 | tf_op jit(solution)/shard_map/ppermute | solution.py:687
  35.9 0.0 collective-permute-done.8.refs_6_.below_ref
  35.9 1.3 %collective-permute-start.9 = (f32[48,128]{1,0:T(8,128)S(1)}, f32[48,128]{1,0:T(8,128)S(1)}, u32[]{:S(2)}, u32[]{:S(2)}) collective-permute-start(f32[48,128]{1,0:T(8,128)S(1)} %get-tuple-element.52), channel_id=1, source_target_pairs={{1,8},{248,263},{249,256},{250,257},{251,258},{252,259},{253,260},... | collective-permute-start | bytes 73736 | tf_op jit(solution)/shard_map/ppermute | solution.py:687
  37.2 2.8 %shard_map.61.vol_ref = f32[5,48,216]{2,1,0:T(8,128)S(1)} custom-call(f32[2,5,12,2,216]{4,3,2,1,0:T(2,128)} %bitcast.5, f32[5,48,216]{2,1,0:T(8,128)S(1)} %get-tuple-element.31.state_ref.refs_0_, f32[48,128]{1,0:T(8,128)S(1)} %get-tuple-element.40.aux_ref.refs_3_, bf16[3,216,216]{2,1,0:T(8,128)(2,1)S(1)} %get-tuple-element.41.dh_ref.refs_8_, ...), custom_call_target="tpu_custom_call" | custom-call | flops 1000000 | bytes 2000000 | tf_op jit(solution)/shard_map/pallas_call | solution.py:753
  40.0 8.4 %collective-permute-done.9.refs_7_.above_ref = f32[48,128]{1,0:T(8,128)S(1)} collective-permute-done((f32[48,128]{1,0:T(8,128)S(1)}, f32[48,128]{1,0:T(8,128)S(1)}, u32[]{:S(2)}, u32[]{:S(2)}) %collective-permute-start.9) | collective-permute-done | bytes 24608 | tf_op jit(solution)/shard_map/ppermute | solution.py:687
  48.4 0.0 collective-permute-done.7.refs_5_.up_ref
  48.4 0.0 collective-permute-done.3.even_ref.even_a_ref
  48.4 0.0 collective-permute-done.6.refs_4_.odd_ref
  48.4 0.1 shard_map.63
  48.5 0.0 collective-permute-done.10.even_b_ref
  48.5 2.2 %shard_map.64 = (f32[2,5,12,2,216]{4,3,2,1,0:T(2,128)}, f32[2,5,12,2,216]{4,3,2,1,0:T(2,128)}) custom-call(f32[2,5,12,2,216]{4,3,2,1,0:T(2,128)} %get-tuple-element.55.state_in, f32[2,5,12,2,216]{4,3,2,1,0:T(2,128)} %get-tuple-element.56.reg_in, f32[2,5,12,2,216]{4,3,2,1,0:T(2,128)} %bitcast.6, ...), custom_call_target="tpu_custom_call", output_to_operand_aliasing={{0}: (0, {}), {1}: (1, {})} | custom-call | flops 100000000 | bytes 2000000 | tf_op jit(solution)/shard_map/pallas_call | solution.py:779
Async XLA Ops:
  2.8 17.6 %collective-permute-start = (f32[72,128]{1,0:T(8,128)S(1)}, f32[72,128]{1,0:T(8,128)S(1)}, u32[]{:S(2)}, u32[]{:S(2)}) collective-permute-start(f32[72,128]{1,0:T(8,128)S(1)} %get-tuple-element.33), channel_id=1, source_target_pairs={{1,2},{2,1},{3,4},{4,3},{6,7},{7,6},{9,10},{10,9},{11,12},{12,11},... | collective-permute-start | bytes 110600 | tf_op jit(solution)/shard_map/ppermute | solution.py:687
  5.2 17.2 %collective-permute-start.1 = (f32[72,128]{1,0:T(8,128)S(1)}, f32[72,128]{1,0:T(8,128)S(1)}, u32[]{:S(2)}, u32[]{:S(2)}) collective-permute-start(f32[72,128]{1,0:T(8,128)S(1)} %get-tuple-element.34), channel_id=1, source_target_pairs={{0,7},{2,3},{3,2},{4,5},{5,4},{7,0},{8,15},{10,11},{11,10},{12,13}... | collective-permute-start | bytes 110600 | tf_op jit(solution)/shard_map/ppermute | solution.py:687
  18.4 5.3 %collective-permute-start.2 = (f32[72,128]{1,0:T(8,128)S(1)}, f32[72,128]{1,0:T(8,128)S(1)}, u32[]{:S(2)}, u32[]{:S(2)}) collective-permute-start(f32[72,128]{1,0:T(8,128)S(1)} %get-tuple-element.35), channel_id=1, source_target_pairs={{0,1},{1,0},{5,6},{6,5},{8,9},{9,8},{13,14},{14,13},{16,17},{17,16... | collective-permute-start | bytes 110600 | tf_op jit(solution)/shard_map/ppermute | solution.py:687
  19.1 5.9 %collective-permute-start.4 = (f32[72,128]{1,0:T(8,128)S(1)}, f32[72,128]{1,0:T(8,128)S(1)}, u32[]{:S(2)}, u32[]{:S(2)}) collective-permute-start(f32[72,128]{1,0:T(8,128)S(1)} %get-tuple-element.46), channel_id=1, source_target_pairs={{248,249},{249,248},{250,251},{251,250},{252,253},{253,252},{254,2... | collective-permute-start | bytes 110600 | tf_op jit(solution)/shard_map/ppermute | solution.py:687
  19.7 14.1 %collective-permute-start.5 = (f32[72,128]{1,0:T(8,128)S(1)}, f32[72,128]{1,0:T(8,128)S(1)}, u32[]{:S(2)}, u32[]{:S(2)}) collective-permute-start(f32[72,128]{1,0:T(8,128)S(1)} %get-tuple-element.47), channel_id=1, source_target_pairs={{248,255},{249,250},{250,249},{251,252},{252,251},{253,254},{254,2... | collective-permute-start | bytes 110600 | tf_op jit(solution)/shard_map/ppermute | solution.py:687
  20.4 15.5 %collective-permute-start.8 = (f32[48,128]{1,0:T(8,128)S(1)}, f32[48,128]{1,0:T(8,128)S(1)}, u32[]{:S(2)}, u32[]{:S(2)}) collective-permute-start(f32[48,128]{1,0:T(8,128)S(1)} %get-tuple-element.52), channel_id=1, source_target_pairs={{7,8},{248,257},{249,258},{250,259},{251,260},{252,261},{253,262},... | collective-permute-start | bytes 73736 | tf_op jit(solution)/shard_map/ppermute | solution.py:687
  22.3 26.0 %collective-permute-start.7 = (f32[72,128]{1,0:T(8,128)S(1)}, f32[72,128]{1,0:T(8,128)S(1)}, u32[]{:S(2)}, u32[]{:S(2)}) collective-permute-start(f32[72,128]{1,0:T(8,128)S(1)} %get-tuple-element.51), channel_id=1, source_target_pairs={{0,8},{248,256},{249,257},{250,258},{251,259},{252,260},{253,261},... | collective-permute-start | bytes 110600 | tf_op jit(solution)/shard_map/ppermute | solution.py:687
  24.3 24.1 %collective-permute-start.3 = (f32[72,128]{1,0:T(8,128)S(1)}, f32[72,128]{1,0:T(8,128)S(1)}, u32[]{:S(2)}, u32[]{:S(2)}) collective-permute-start(f32[72,128]{1,0:T(8,128)S(1)} %get-tuple-element.39.mine_ref), channel_id=1, source_target_pairs={{2,10},{3,11},{4,12},{5,13},{6,14},{10,2},{11,3},{12,4},{13,5},{14... | collective-permute-start | bytes 110600 | tf_op jit(solution)/shard_map/ppermute | solution.py:687
  24.9 23.5 %collective-permute-start.6 = (f32[72,128]{1,0:T(8,128)S(1)}, f32[72,128]{1,0:T(8,128)S(1)}, u32[]{:S(2)}, u32[]{:S(2)}) collective-permute-start(f32[72,128]{1,0:T(8,128)S(1)} %get-tuple-element.50), channel_id=1, source_target_pairs={{0,1016},{1,1017},{2,1018},{3,1019},{4,1020},{5,1021},{6,1022},{7,... | collective-permute-start | bytes 110600 | tf_op jit(solution)/shard_map/ppermute | solution.py:687
  33.9 14.5 %collective-permute-start.10 = (f32[72,128]{1,0:T(8,128)S(1)}, f32[72,128]{1,0:T(8,128)S(1)}, u32[]{:S(2)}, u32[]{:S(2)}) collective-permute-start(f32[72,128]{1,0:T(8,128)S(1)} %get-tuple-element.57), channel_id=1, source_target_pairs={{1,9},{7,15},{8,0},{9,1},{15,7},{240,248},{241,249},{242,250},{243... | collective-permute-start | bytes 110600 | tf_op jit(solution)/shard_map/ppermute | solution.py:687
  35.9 12.5 %collective-permute-start.9 = (f32[48,128]{1,0:T(8,128)S(1)}, f32[48,128]{1,0:T(8,128)S(1)}, u32[]{:S(2)}, u32[]{:S(2)}) collective-permute-start(f32[48,128]{1,0:T(8,128)S(1)} %get-tuple-element.52), channel_id=1, source_target_pairs={{1,8},{248,263},{249,256},{250,257},{251,258},{252,259},{253,260},... | collective-permute-start | bytes 73736 | tf_op jit(solution)/shard_map/ppermute | solution.py:687

commit v5 on v4

--- a/solution.py
+++ b/solution.py
@@ -320,8 +320,7 @@
 def ends_late():
     period = period_of(lax.axis_size("gx"))
     pair = lax.rem(lax.axis_index("gx"), period) >= period - 2
-    last = lax.axis_size("gz") - 1
-    near = [is_device(0, 0)] + [is_device(i, j) for i in (0, 1) for j in (1, last)]
+    near = [is_device(0, 0)] + [is_device(i, j) for i in (0, 1) for j in (1,)]
     return functools.reduce(jnp.logical_or, near, pair)
 
 
@@ -762,7 +761,7 @@
         second_kernel, (field_shape(9), field_shape(9), FACE, FACE), 10**8, scratch_shapes=face_buf
     )(st, tg_first, *za, uz, px, ep)
     early = lambda i: not (late(i) or late(i ^ 1))
-    apart = lambda i, j: i < 2 and j in (0, 1, last_z)
+    apart = lambda i, j: i < 2 and j in (0, 1)
     xa_even = send(even_x, lambda i, j: ok(early(i) and not apart(i, j), (i ^ 1, j)))
     x_odd = send(odd_x, lambda i, j: ok(not late(i), (odd_partner(i), j)))
     zb_even = send(even_z, lambda i, j: ok(late(i), (i, j ^ 1)))

time: 51 us -> 50.7 us (level)
  the two profiles are of different devices: /device:TPU:14 before, /device:TPU:8 now
where the time goes in v5:
time: 50.7 us; the launch traced here: 50.4 us
  starting transfers between devices  37.9 us (75%)
  Pallas kernels  7.93 us (16%)
  waiting for transfers between devices  3.75 us (7%)
  between operations  0.81 us (2%)
    ppermute x11, starting transfers between devices, send(): return lax.ppermute(value, ('gx', 'gz'), pairs)  37.9 us
    ppermute x11, waiting for transfers between devices, send(): return lax.ppermute(value, ('gx', 'gz'), pairs)  3.75 us
    pallas_call x1, Pallas kernels, shards(): call(volume_kernel, field_shape(5), 10 ** 6, in_specs=[hbm] + [vmem] * 5,...  2.8 us
    pallas_call x1, Pallas kernels, shards(): call(last_b_kernel, (whole, whole), 10 ** 8, in_specs=[hbm] * 3 + [vmem]...  2.21 us
    pallas_call x1, Pallas kernels, shards(): call(first_kernel, (field_shape(5), aux_shape, table, table, table, field...  2.17 us
  transfers between devices with their start and end apart: 11, of which 1 were waited for; matrix products, arithmetic and copies ran while one was open for 0% of the time, Pallas kernels for 7%

profile of v5, /device:TPU:8, one launch (start us, length us, event | category | flops | bytes accessed | tf_op | source)
XLA Modules:
  0.0 50.4 jit_solution(17948727677861456024)
XLA Ops:
  0.6 2.2 %shard_map.59 = (f32[5,48,216]{2,1,0:T(8,128)S(1)}, f32[48,128]{1,0:T(8,128)S(1)}, bf16[3,216,216]{2,1,0:T(8,128)(2,1)S(1)}, bf16[3,216,216]{2,1,0:T(8,128)(2,1)...) custom-call(f32[2,5,12,2,216]{4,3,2,1,0:T(2,128)} %bitcast.9, ...), custom_call_target="tpu_custom_call" | custom-call | flops 100000000 | bytes 2000000 | tf_op jit(solution)/shard_map/pallas_call | solution.py:721
  2.8 3.3 %collective-permute-start = (f32[72,128]{1,0:T(8,128)S(1)}, f32[72,128]{1,0:T(8,128)S(1)}, u32[]{:S(2)}, u32[]{:S(2)}) collective-permute-start(f32[72,128]{1,0:T(8,128)S(1)} %get-tuple-element.33), channel_id=1, source_target_pairs={{1,2},{2,1},{3,4},{4,3},{6,7},{7,6},{9,10},{10,9},{11,12},{12,11},... | collective-permute-start | bytes 110600 | tf_op jit(solution)/shard_map/ppermute | solution.py:686
  6.1 0.7 %collective-permute-start.1 = (f32[72,128]{1,0:T(8,128)S(1)}, f32[72,128]{1,0:T(8,128)S(1)}, u32[]{:S(2)}, u32[]{:S(2)}) collective-permute-start(f32[72,128]{1,0:T(8,128)S(1)} %get-tuple-element.34), channel_id=1, source_target_pairs={{0,7},{2,3},{3,2},{4,5},{5,4},{7,0},{8,15},{10,11},{11,10},{12,13}... | collective-permute-start | bytes 110600 | tf_op jit(solution)/shard_map/ppermute | solution.py:686
  6.8 13.6 %collective-permute-start.2 = (f32[72,128]{1,0:T(8,128)S(1)}, f32[72,128]{1,0:T(8,128)S(1)}, u32[]{:S(2)}, u32[]{:S(2)}) collective-permute-start(f32[72,128]{1,0:T(8,128)S(1)} %get-tuple-element.35), channel_id=1, source_target_pairs={{0,1},{1,0},{5,6},{6,5},{8,9},{9,8},{13,14},{14,13},{16,17},{17,16... | collective-permute-start | bytes 110600 | tf_op jit(solution)/shard_map/ppermute | solution.py:686
  20.4 0.7 %collective-permute-start.4 = (f32[72,128]{1,0:T(8,128)S(1)}, f32[72,128]{1,0:T(8,128)S(1)}, u32[]{:S(2)}, u32[]{:S(2)}) collective-permute-start(f32[72,128]{1,0:T(8,128)S(1)} %get-tuple-element.46), channel_id=1, source_target_pairs={{248,249},{249,248},{250,251},{251,250},{252,253},{253,252},{254,2... | collective-permute-start | bytes 110600 | tf_op jit(solution)/shard_map/ppermute | solution.py:686
  21.1 0.7 %collective-permute-start.5 = (f32[72,128]{1,0:T(8,128)S(1)}, f32[72,128]{1,0:T(8,128)S(1)}, u32[]{:S(2)}, u32[]{:S(2)}) collective-permute-start(f32[72,128]{1,0:T(8,128)S(1)} %get-tuple-element.47), channel_id=1, source_target_pairs={{248,255},{249,250},{250,249},{251,252},{252,251},{253,254},{254,2... | collective-permute-start | bytes 110600 | tf_op jit(solution)/shard_map/ppermute | solution.py:686
  21.7 0.0 collective-permute-done.turn_1
  21.7 1.3 %collective-permute-start.8 = (f32[48,128]{1,0:T(8,128)S(1)}, f32[48,128]{1,0:T(8,128)S(1)}, u32[]{:S(2)}, u32[]{:S(2)}) collective-permute-start(f32[48,128]{1,0:T(8,128)S(1)} %get-tuple-element.52), channel_id=1, source_target_pairs={{7,8},{248,257},{249,258},{250,259},{251,260},{252,261},{253,262},... | collective-permute-start | bytes 73736 | tf_op jit(solution)/shard_map/ppermute | solution.py:686
  23.0 0.0 collective-permute-done.1.turn_2
  23.1 1.3 %collective-permute-start.7 = (f32[72,128]{1,0:T(8,128)S(1)}, f32[72,128]{1,0:T(8,128)S(1)}, u32[]{:S(2)}, u32[]{:S(2)}) collective-permute-start(f32[72,128]{1,0:T(8,128)S(1)} %get-tuple-element.51), channel_id=1, source_target_pairs={{0,8},{248,256},{249,257},{250,258},{251,259},{252,260},{253,261},... | collective-permute-start | bytes 110600 | tf_op jit(solution)/shard_map/ppermute | solution.py:686
  24.4 0.0 collective-permute-done.2.turn_3
  24.4 0.6 %shard_map.60 = (f32[9,48,216]{2,1,0:T(8,128)S(1)}, f32[9,48,216]{2,1,0:T(8,128)S(1)}, f32[72,128]{1,0:T(8,128)S(1)}, f32[72,128]{1,0:T(8,128)S(1)}) custom-call(f32[5,48,216]{2,1,0:T(8,128)S(1)} %get-tuple-element.31.state_ref.refs_0_, f32[9,48,216]{2,1,0:T(8,128)S(1)} %get-tuple-element.32.tg_ref.tg_first_ref, f32[72,128]{1,0:T(8,128)S(1)} %collective-permute-done.turn_1, ...), custom_call_target="tpu_custom_call" | custom-call | flops 100000000 | bytes 2000000 | tf_op jit(solution)/shard_map/pallas_call | solution.py:760
  25.0 0.7 %collective-permute-start.3 = (f32[72,128]{1,0:T(8,128)S(1)}, f32[72,128]{1,0:T(8,128)S(1)}, u32[]{:S(2)}, u32[]{:S(2)}) collective-permute-start(f32[72,128]{1,0:T(8,128)S(1)} %get-tuple-element.39.mine_ref), channel_id=1, source_target_pairs={{2,10},{3,11},{4,12},{5,13},{6,14},{7,15},{10,2},{11,3},{12,4},{13... | collective-permute-start | bytes 110600 | tf_op jit(solution)/shard_map/ppermute | solution.py:686
  25.6 0.0 collective-permute-done.4.even_ref
  25.7 9.2 %collective-permute-start.6 = (f32[72,128]{1,0:T(8,128)S(1)}, f32[72,128]{1,0:T(8,128)S(1)}, u32[]{:S(2)}, u32[]{:S(2)}) collective-permute-start(f32[72,128]{1,0:T(8,128)S(1)} %get-tuple-element.50), channel_id=1, source_target_pairs={{0,1016},{1,1017},{2,1018},{3,1019},{4,1020},{5,1021},{6,1022},{7,... | collective-permute-start | bytes 110600 | tf_op jit(solution)/shard_map/ppermute | solution.py:686
  34.8 0.0 collective-permute-done.5.odd_ref
  34.9 0.1 shard_map.62
  34.9 1.9 %collective-permute-start.10 = (f32[72,128]{1,0:T(8,128)S(1)}, f32[72,128]{1,0:T(8,128)S(1)}, u32[]{:S(2)}, u32[]{:S(2)}) collective-permute-start(f32[72,128]{1,0:T(8,128)S(1)} %get-tuple-element.57), channel_id=1, source_target_pairs={{1,9},{8,0},{9,1},{240,248},{241,249},{242,250},{243,251},{244,252... | collective-permute-start | bytes 110600 | tf_op jit(solution)/shard_map/ppermute | solution.py:686
  36.9 0.0 collective-permute-done.8.refs_6_.below_ref
  36.9 4.6 %collective-permute-start.9 = (f32[48,128]{1,0:T(8,128)S(1)}, f32[48,128]{1,0:T(8,128)S(1)}, u32[]{:S(2)}, u32[]{:S(2)}) collective-permute-start(f32[48,128]{1,0:T(8,128)S(1)} %get-tuple-element.52), channel_id=1, source_target_pairs={{1,8},{248,263},{249,256},{250,257},{251,258},{252,259},{253,260},... | collective-permute-start | bytes 73736 | tf_op jit(solution)/shard_map/ppermute | solution.py:686
  41.5 2.8 %shard_map.61.vol_ref = f32[5,48,216]{2,1,0:T(8,128)S(1)} custom-call(f32[2,5,12,2,216]{4,3,2,1,0:T(2,128)} %bitcast.5, f32[5,48,216]{2,1,0:T(8,128)S(1)} %get-tuple-element.31.state_ref.refs_0_, f32[48,128]{1,0:T(8,128)S(1)} %get-tuple-element.40.aux_ref.refs_3_, bf16[3,216,216]{2,1,0:T(8,128)(2,1)S(1)} %get-tuple-element.41.dh_ref.refs_8_, ...), custom_call_target="tpu_custom_call" | custom-call | flops 1000000 | bytes 2000000 | tf_op jit(solution)/shard_map/pallas_call | solution.py:752
  44.3 3.7 %collective-permute-done.9.refs_7_.above_ref = f32[48,128]{1,0:T(8,128)S(1)} collective-permute-done((f32[48,128]{1,0:T(8,128)S(1)}, f32[48,128]{1,0:T(8,128)S(1)}, u32[]{:S(2)}, u32[]{:S(2)}) %collective-permute-start.9) | collective-permute-done | bytes 24608 | tf_op jit(solution)/shard_map/ppermute | solution.py:686
  48.1 0.0 collective-permute-done.7.refs_5_.up_ref
  48.1 0.0 collective-permute-done.3.even_ref.even_a_ref
  48.1 0.0 collective-permute-done.6.refs_4_.odd_ref
  48.1 0.1 shard_map.63
  48.1 0.0 collective-permute-done.10.even_b_ref
  48.1 2.2 %shard_map.64 = (f32[2,5,12,2,216]{4,3,2,1,0:T(2,128)}, f32[2,5,12,2,216]{4,3,2,1,0:T(2,128)}) custom-call(f32[2,5,12,2,216]{4,3,2,1,0:T(2,128)} %get-tuple-element.55.state_in, f32[2,5,12,2,216]{4,3,2,1,0:T(2,128)} %get-tuple-element.56.reg_in, f32[2,5,12,2,216]{4,3,2,1,0:T(2,128)} %bitcast.6, ...), custom_call_target="tpu_custom_call", output_to_operand_aliasing={{0}: (0, {}), {1}: (1, {})} | custom-call | flops 100000000 | bytes 2000000 | tf_op jit(solution)/shard_map/pallas_call | solution.py:778
Async XLA Ops:
  2.8 18.9 %collective-permute-start = (f32[72,128]{1,0:T(8,128)S(1)}, f32[72,128]{1,0:T(8,128)S(1)}, u32[]{:S(2)}, u32[]{:S(2)}) collective-permute-start(f32[72,128]{1,0:T(8,128)S(1)} %get-tuple-element.33), channel_id=1, source_target_pairs={{1,2},{2,1},{3,4},{4,3},{6,7},{7,6},{9,10},{10,9},{11,12},{12,11},... | collective-permute-start | bytes 110600 | tf_op jit(solution)/shard_map/ppermute | solution.py:686
  6.1 16.9 %collective-permute-start.1 = (f32[72,128]{1,0:T(8,128)S(1)}, f32[72,128]{1,0:T(8,128)S(1)}, u32[]{:S(2)}, u32[]{:S(2)}) collective-permute-start(f32[72,128]{1,0:T(8,128)S(1)} %get-tuple-element.34), channel_id=1, source_target_pairs={{0,7},{2,3},{3,2},{4,5},{5,4},{7,0},{8,15},{10,11},{11,10},{12,13}... | collective-permute-start | bytes 110600 | tf_op jit(solution)/shard_map/ppermute | solution.py:686
  6.8 17.6 %collective-permute-start.2 = (f32[72,128]{1,0:T(8,128)S(1)}, f32[72,128]{1,0:T(8,128)S(1)}, u32[]{:S(2)}, u32[]{:S(2)}) collective-permute-start(f32[72,128]{1,0:T(8,128)S(1)} %get-tuple-element.35), channel_id=1, source_target_pairs={{0,1},{1,0},{5,6},{6,5},{8,9},{9,8},{13,14},{14,13},{16,17},{17,16... | collective-permute-start | bytes 110600 | tf_op jit(solution)/shard_map/ppermute | solution.py:686
  20.4 5.3 %collective-permute-start.4 = (f32[72,128]{1,0:T(8,128)S(1)}, f32[72,128]{1,0:T(8,128)S(1)}, u32[]{:S(2)}, u32[]{:S(2)}) collective-permute-start(f32[72,128]{1,0:T(8,128)S(1)} %get-tuple-element.46), channel_id=1, source_target_pairs={{248,249},{249,248},{250,251},{251,250},{252,253},{253,252},{254,2... | collective-permute-start | bytes 110600 | tf_op jit(solution)/shard_map/ppermute | solution.py:686
  21.1 13.8 %collective-permute-start.5 = (f32[72,128]{1,0:T(8,128)S(1)}, f32[72,128]{1,0:T(8,128)S(1)}, u32[]{:S(2)}, u32[]{:S(2)}) collective-permute-start(f32[72,128]{1,0:T(8,128)S(1)} %get-tuple-element.47), channel_id=1, source_target_pairs={{248,255},{249,250},{250,249},{251,252},{252,251},{253,254},{254,2... | collective-permute-start | bytes 110600 | tf_op jit(solution)/shard_map/ppermute | solution.py:686
  21.7 15.1 %collective-permute-start.8 = (f32[48,128]{1,0:T(8,128)S(1)}, f32[48,128]{1,0:T(8,128)S(1)}, u32[]{:S(2)}, u32[]{:S(2)}) collective-permute-start(f32[48,128]{1,0:T(8,128)S(1)} %get-tuple-element.52), channel_id=1, source_target_pairs={{7,8},{248,257},{249,258},{250,259},{251,260},{252,261},{253,262},... | collective-permute-start | bytes 73736 | tf_op jit(solution)/shard_map/ppermute | solution.py:686
  23.1 25.0 %collective-permute-start.7 = (f32[72,128]{1,0:T(8,128)S(1)}, f32[72,128]{1,0:T(8,128)S(1)}, u32[]{:S(2)}, u32[]{:S(2)}) collective-permute-start(f32[72,128]{1,0:T(8,128)S(1)} %get-tuple-element.51), channel_id=1, source_target_pairs={{0,8},{248,256},{249,257},{250,258},{251,259},{252,260},{253,261},... | collective-permute-start | bytes 110600 | tf_op jit(solution)/shard_map/ppermute | solution.py:686
  25.0 23.1 %collective-permute-start.3 = (f32[72,128]{1,0:T(8,128)S(1)}, f32[72,128]{1,0:T(8,128)S(1)}, u32[]{:S(2)}, u32[]{:S(2)}) collective-permute-start(f32[72,128]{1,0:T(8,128)S(1)} %get-tuple-element.39.mine_ref), channel_id=1, source_target_pairs={{2,10},{3,11},{4,12},{5,13},{6,14},{7,15},{10,2},{11,3},{12,4},{13... | collective-permute-start | bytes 110600 | tf_op jit(solution)/shard_map/ppermute | solution.py:686
  25.7 22.4 %collective-permute-start.6 = (f32[72,128]{1,0:T(8,128)S(1)}, f32[72,128]{1,0:T(8,128)S(1)}, u32[]{:S(2)}, u32[]{:S(2)}) collective-permute-start(f32[72,128]{1,0:T(8,128)S(1)} %get-tuple-element.50), channel_id=1, source_target_pairs={{0,1016},{1,1017},{2,1018},{3,1019},{4,1020},{5,1021},{6,1022},{7,... | collective-permute-start | bytes 110600 | tf_op jit(solution)/shard_map/ppermute | solution.py:686
  34.9 13.2 %collective-permute-start.10 = (f32[72,128]{1,0:T(8,128)S(1)}, f32[72,128]{1,0:T(8,128)S(1)}, u32[]{:S(2)}, u32[]{:S(2)}) collective-permute-start(f32[72,128]{1,0:T(8,128)S(1)} %get-tuple-element.57), channel_id=1, source_target_pairs={{1,9},{8,0},{9,1},{240,248},{241,249},{242,250},{243,251},{244,252... | collective-permute-start | bytes 110600 | tf_op jit(solution)/shard_map/ppermute | solution.py:686
  36.9 11.2 %collective-permute-start.9 = (f32[48,128]{1,0:T(8,128)S(1)}, f32[48,128]{1,0:T(8,128)S(1)}, u32[]{:S(2)}, u32[]{:S(2)}) collective-permute-start(f32[48,128]{1,0:T(8,128)S(1)} %get-tuple-element.52), channel_id=1, source_target_pairs={{1,8},{248,263},{249,256},{250,257},{251,258},{252,259},{253,260},... | collective-permute-start | bytes 73736 | tf_op jit(solution)/shard_map/ppermute | solution.py:686
